TPU v7x, 32 devices: a whole 2x2x4 slice. The times are simulated.
32 devices in a mesh: batch: 4 (over x, core), lat: 8 (over z, y).
Axes of the slice: x: 2, y: 2, z: 4, core: 2. Of those that a mesh axis runs over, the one named last changes fastest.
Arguments:
- predicted: bfloat16 [4, 73, 192, 1440], P('batch', None, 'lat'), may hold values from -64 to 64
- target: bfloat16 [4, 73, 192, 1440], P('batch', None, 'lat'), may hold values from -128 to 128
- legendre_basis: bfloat16 [192, 96, 720], P(None, ('batch', 'lat')), may hold values from -1 to 1
Outputs:
- spectra: float32 [2, 73, 720], replicated
- channel_loss: float32 [73], replicated
All inputs are finite; a program needn't handle non-finite values.
Results may differ from a plain program's by a relative error of at most 0.0003.
Values may be sent and summed in bfloat16 or wider, within the bound.
No kernel may reach another device: no remote copies, remote signals or barrier semaphores. Data moves between devices by JAX's collectives and lax.ppermute only.
A program may use at most 128 MiB of HBM per device.

v0:
```python
import math

import jax
import jax.numpy as jnp
from jax import lax
from jax.sharding import PartitionSpec as P


def fourier_table(lon_count, order_count):
    lon_ids = jnp.arange(lon_count, dtype=jnp.int32)
    order_ids = jnp.arange(order_count, dtype=jnp.int32)
    product_ids = lon_ids[:, None] * order_ids[None, :] % lon_count
    angles = 2.0 * math.pi / lon_count * product_ids.astype(jnp.float32)
    inv_root = 1.0 / math.sqrt(lon_count)
    return jnp.stack([jnp.cos(angles) * inv_root, -jnp.sin(angles) * inv_root], axis=1).astype(
        jnp.bfloat16
    )


def band_energy(fourier, basis_block, orders):
    coefficients = jnp.einsum(
        "fpmbcn,nml->fpmbcl", fourier, basis_block, preferred_element_type=jnp.float32
    )
    squares = jnp.sum(coefficients * coefficients, axis=1)
    weights = jnp.where(orders == 0, 1.0, 2.0).astype(jnp.float32)
    return jnp.sum(squares * weights[None, :, None, None, None], axis=(1, 2))


def body(predicted, target, legendre_basis):
    groups = lax.axis_size("batch")
    band_count = lax.axis_size("lat")
    per_dev = legendre_basis.shape[1]
    order_count = per_dev * groups * band_count
    dft_table = fourier_table(predicted.shape[3], order_count)
    band_id = lax.axis_index("lat")

    def transform(field_in):
        return jnp.einsum(
            "bcnk,kpm->pmbcn", field_in, dft_table, preferred_element_type=jnp.float32
        ).astype(jnp.bfloat16)

    fourier = jnp.stack([transform(predicted), transform(target)], axis=0)
    members = fourier.shape[3]
    channels = fourier.shape[4]
    lat_rows = fourier.shape[5]
    fourier = fourier.reshape(2, 2, groups, band_count, per_dev, members, channels, lat_rows)
    arrived = lax.all_to_all(fourier, "lat", split_axis=3, concat_axis=7, tiled=True)
    arrived = arrived.reshape(
        2, 2, groups * per_dev, arrived.shape[5], arrived.shape[6], arrived.shape[7]
    )
    basis_block = lax.all_gather(legendre_basis, "batch", axis=1, tiled=True)
    taken = basis_block.shape[1]
    gathered_ids = jnp.arange(taken, dtype=jnp.int32)
    orders = (
        gathered_ids // per_dev * band_count * per_dev + band_id * per_dev + gathered_ids % per_dev
    )
    partial_value = band_energy(arrived, basis_block, orders)
    energy = lax.psum(partial_value, "lat")
    energy = lax.psum(energy, "batch")
    spectra = energy / (predicted.shape[0] * groups * order_count)
    log_spectra = jnp.log(spectra + 1e-06)
    channel_loss = jnp.mean((log_spectra[0] - log_spectra[1]) ** 2, axis=1)
    return (spectra, channel_loss)


def solution(mesh):
    placed = (
        P("batch", None, "lat", None),
        P("batch", None, "lat", None),
        P(None, ("batch", "lat"), None),
    )
    return jax.shard_map(body, mesh=mesh, in_specs=placed, out_specs=(P(), P()), check_vma=False)
```

profile of v0, /device:TPU:0, one launch (start us, length us, event | category | flops | bytes accessed | tf_op | source)
XLA Modules:
  0.0 212.2 jit_solution(11625327290755649896)
XLA Ops:
  7.2 0.0 all-gather.2.cloned.1.call-start
  7.2 0.7 all-gather.2.cloned.1.call-update
  7.9 2.6 %multiply_convert_fusion = (bf16[1440,1,96]{0,2,1:T(8,128)(2,1)S(1)}, bf16[1440,1,96]{0,2,1:T(8,128)(2,1)S(1)}) fusion(), kind=kLoop, calls=%fused_computation.17 | loop fusion | flops 1935360 | bytes 552960 | tf_op jit(solution)/shard_map/convert.1
  10.5 0.0 copy-start
  10.5 0.0 copy-start.1
  10.5 0.7 copy-done
  11.2 0.1 copy-done.1
  11.3 4.8 %fusion.8 = bf16[2,96,73,24]{1,2,3,0:T(8,128)(2,1)S(1)} fusion(bf16[73,24,1440]{2,1,0:T(8,128)(2,1)} %bitcast.33, bf16[1440,1,96]{0,2,1:T(8,128)(2,1)S(1)} %get-tuple-element.4, bf16[1440,1,96]{0,2,1:T(8,128)(2,1)S(1)} %get-tuple-element.5), kind=kOutput, calls=%fused_computation.11 | convolution fusion | flops 970228224 | bytes 6271488 | tf_op jit(solution)/shard_map/bcnk,kpm->pmbcn/dot_general | solution.py:38
  16.1 0.9 copy.29
  17.0 5.5 %fusion.11 = bf16[2,96,73,24]{1,2,3,0:T(8,128)(2,1)S(1)} fusion(bf16[73,24,1440]{2,1,0:T(8,128)(2,1)} %bitcast.34, bf16[1440,1,96]{0,2,1:T(8,128)(2,1)} %copy-done, bf16[1440,1,96]{0,2,1:T(8,128)(2,1)} %copy-done.1), kind=kOutput, calls=%fused_computation.12 | convolution fusion | flops 970228224 | bytes 6271488 | tf_op jit(solution)/shard_map/bcnk,kpm->pmbcn/dot_general | solution.py:38
  22.5 0.9 copy.31
  23.3 0.5 pad_maximum_fusion
  23.9 2.0 copy.32
  25.9 7.5 %all-to-all-start = ((bf16[2,2,4,8,3,1,73,24]{6,7,4,2,1,5,0,3:T(8,128)(2,1)}), bf16[2,2,4,8,3,1,73,24]{6,7,4,2,1,5,0,3:T(8,128)(2,1)S(1)}, u32[]{:S(2)}, u32[]{:S(2)}) async-start(bf16[2,2,4,8,3,1,73,24]{6,7,4,2,1,5,0,3:T(8,128)(2,1)} %copy.32), calls=%async_computation | async-start | bytes 4718592 | tf_op jit(solution)/shard_map/all_to_all | solution.py:47
  33.5 0.0 all-reduce.3.cloned.1.call-start
  33.5 53.6 %all-to-all-done = bf16[2,2,4,8,3,1,73,24]{6,7,4,2,1,5,0,3:T(8,128)(2,1)S(1)} async-done(((bf16[2,2,4,8,3,1,73,24]{6,7,4,2,1,5,0,3:T(8,128)(2,1)}), bf16[2,2,4,8,3,1,73,24]{6,7,4,2,1,5,0,3:T(8,128)(2,1)S(1)}, u32[]{:S(2)}, u32[]{:S(2)}) %all-to-all-start) | async-done | bytes 1345568 | tf_op jit(solution)/shard_map/all_to_all | solution.py:47
  87.1 2.1 copy.33
  89.2 0.0 all-gather.2.cloned.1.call-done
  89.2 5.1 %multiply_reduce_fusion = f32[12,2,73,720]{3,2,1,0:T(8,128)S(1)} fusion(bf16[192,12,720]{2,0,1:T(8,128)(2,1)} %all-gather.2.cloned.1.call-done, bf16[2,2,12,73,192]{3,4,2,1,0:T(8,128)(2,1)} %bitcast.30), kind=kOutput, calls=%fused_computation | convolution fusion | flops 972570240 | bytes 9709056 | tf_op jit(solution)/shard_map/fpmbcn,nml->fpmbcl/dot_general | solution.py:21
  94.3 0.6 multiply_reduce_fusion.1
  94.9 1.1 copy.40
  96.0 0.0 all-reduce.3.cloned.1.call-update
  96.1 0.0 all-reduce.5.cloned.1.call-start
  96.1 71.4 %all-reduce.3.cloned.1.call-done = f32[2,73,720]{2,0,1:T(2,128)} async-done(((f32[2,73,720]{2,0,1:T(2,128)}), f32[2,73,720]{2,0,1:T(2,128)}) %all-reduce.3.cloned.1.call-update) | async-done | bytes 420496 | tf_op jit(solution)/shard_map/psum | solution.py:58
  167.5 0.0 all-reduce.5.cloned.1.call-update
  167.6 34.7 %all-reduce.5.cloned.1.call-done = f32[2,73,720]{2,0,1:T(2,128)} async-done(((f32[2,73,720]{2,0,1:T(2,128)}), f32[2,73,720]{2,0,1:T(2,128)}) %all-reduce.5.cloned.1.call-update) | async-done | bytes 420496 | tf_op jit(solution)/shard_map/psum | solution.py:59
  202.2 2.2 %add_log_fusion = (f32[2,73,720]{2,0,1:T(2,128)S(1)}, f32[2,73,720]{2,0,1:T(2,128)}) fusion(f32[2,73,720]{2,0,1:T(2,128)} %all-reduce.5.cloned.1.call-done), kind=kLoop, calls=%fused_computation.23 | loop fusion | flops 210240 | bytes 1261440 | tf_op jit(solution)/shard_map/log | solution.py:61
  204.5 0.6 fusion.20
  205.1 0.5 broadcast_multiply_fusion.1
  (1 shorter events, 0.0 us)
Async XLA Ops:
  7.2 82.1 %all-gather.2.cloned.1.call-start = ((), (), s32[]{:S(2)}) async-start(), calls=%async_computation.1 | async-start | bytes 4423680 | tf_op jit(solution)/shard_map/all_gather | solution.py:51
  10.5 0.7 copy-start
  10.5 0.8 copy-start.1
  25.9 61.2 %all-to-all-start = ((bf16[2,2,4,8,3,1,73,24]{6,7,4,2,1,5,0,3:T(8,128)(2,1)}), bf16[2,2,4,8,3,1,73,24]{6,7,4,2,1,5,0,3:T(8,128)(2,1)S(1)}, u32[]{:S(2)}, u32[]{:S(2)}) async-start(bf16[2,2,4,8,3,1,73,24]{6,7,4,2,1,5,0,3:T(8,128)(2,1)} %copy.32), calls=%async_computation | async-start | bytes 4718592 | tf_op jit(solution)/shard_map/all_to_all | solution.py:47
  33.5 134.1 %all-reduce.3.cloned.1.call-start = ((), (), s32[]{:S(2)}) async-start(), calls=%async_computation.2 | async-start | bytes 897024 | tf_op jit(solution)/shard_map/psum | solution.py:58
  96.1 106.2 %all-reduce.5.cloned.1.call-start = ((), (), s32[]{:S(2)}) async-start(), calls=%async_computation.3 | async-start | bytes 897024 | tf_op jit(solution)/shard_map/psum | solution.py:59
Sparse Core Ops, SparseCore 0:
  9.5 33.4 all-gather.1
  96.2 71.2 all-reduce.2
  169.9 32.2 all-reduce.4
where the time goes:
time: 212 us
  waiting for transfers between devices  160 us (75%)
  matrix products  15.4 us (7%)
  between operations  13.8 us (7%)
  local copies, waits for them, and re-layouts  7.77 us (4%)
  starting transfers between devices  7.66 us (4%)
  other arithmetic  7.07 us (3%)
    psum x1, waiting for transfers between devices, body(): energy = lax.psum(partial_value, 'lat')  71.4 us
    all_to_all x1, waiting for transfers between devices, body(): lax.all_to_all(fourier, 'lat', split_axis=3, concat_axis=7, tiled=True)  53.6 us
    psum x1, waiting for transfers between devices, body(): energy = lax.psum(energy, 'batch')  34.7 us
    dot_general x2, matrix products, transform(): jnp.einsum('bcnk,kpm->pmbcn', field_in, dft_table, preferred_element_type...  10.3 us
    all_to_all x1, starting transfers between devices, body(): lax.all_to_all(fourier, 'lat', split_axis=3, concat_axis=7, tiled=True)  7.55 us
    dot_general x1, matrix products, band_energy(): jnp.einsum('fpmbcn,nml->fpmbcl', fourier, basis_block, preferred_element_...  5.1 us
  transfers between devices with their start and end apart: 4, of which 3 were waited for; matrix products, arithmetic and copies ran while one was open for 9% of the time, Pallas kernels for 0%

commit v1 on v0

v1 whole, which is shorter than its diff:
```python
import functools
import math

import jax
import jax.numpy as jnp
import numpy as np
from jax import lax
from jax.experimental import pallas as pl
from jax.experimental.pallas import tpu as pltpu
from jax.sharding import PartitionSpec as P

LANES = 128
VMEM_LIMIT = 60 * 1024 * 1024


def round_up(value, step):
    return -(-value // step) * step


def fourier_table(lon_count, groups, bands, per_dev):
    orders = np.arange(groups * bands * per_dev).reshape(groups, bands, per_dev)
    orders = orders.transpose(1, 0, 2).reshape(-1)
    product_ids = np.arange(lon_count)[:, None] * orders[None, :] % lon_count
    angles = np.float32(2.0 * math.pi / lon_count) * product_ids.astype(np.float32)
    inv_root = np.float32(1.0 / math.sqrt(lon_count))
    both = np.stack([np.cos(angles) * inv_root, -np.sin(angles) * inv_root], axis=2)
    flat = both.reshape(lon_count, -1).astype(jnp.bfloat16)
    padded = round_up(flat.shape[1], LANES)
    return np.pad(flat, ((0, 0), (0, padded - flat.shape[1])))


def peers(count, step):
    if count & (count - 1) == 0:
        return [(i, i ^ step) for i in range(count)]
    return [(i, (i + step) % count) for i in range(count)]


def target_of(index, count, step):
    if count & (count - 1) == 0:
        return jnp.bitwise_xor(index, step)
    return lax.rem(index + step, count)


def source_of(index, count, step):
    if count & (count - 1) == 0:
        return jnp.bitwise_xor(index, step)
    return lax.rem(index + count - step, count)


def dft_kernel(bands, per, chans, lats, chunks, place, p_hbm, t_hbm, table, *rest):
    outs = rest[:bands]
    xbuf, dscr, turned, packed, sems = rest[bands:]
    copies = []
    for f, field in enumerate((p_hbm, t_hbm)):
        row = 0
        for i, rows in enumerate(chunks):
            cp = pltpu.make_async_copy(
                field.at[pl.ds(row, rows), :], xbuf.at[f, pl.ds(row, rows), :], sems.at[f, i]
            )
            cp.start()
            copies.append((f, row, rows, cp))
            row += rows
    band = place[0]
    tiles = dscr.shape[0]
    for f in range(2):
        for owner, row, rows, cp in copies:
            if owner != f:
                continue
            cp.wait()
            res = jnp.dot(
                xbuf[f, pl.ds(row, rows), :], table[...], preferred_element_type=jnp.float32
            )
            for q in range(tiles):
                dscr[q, pl.ds(row, rows), :] = res[:, q * LANES : (q + 1) * LANES]

        def turn(q, carry):
            for n in range(lats):
                block = dscr.at[q][pl.ds(n, LANES, stride=lats), :]
                turned.at[q][pl.ds(n, LANES, stride=lats), :] = block.T
            return carry

        lax.fori_loop(0, tiles, turn, 0)

        def pack(s, carry):
            base = target_of(band, bands, s) * per
            for g in range(per):
                column = base + g
                start = pl.multiple_of(lax.rem(column, LANES) * lats, 8)
                packed[s, :, pl.ds(g * chans, chans)] = turned[
                    column // LANES, pl.ds(start, lats), pl.ds(0, chans)
                ]
            return carry

        lax.fori_loop(0, bands, pack, 0)
        for s in range(bands):
            outs[s][f] = packed[s].astype(jnp.bfloat16)


def dft_blocks(place, predicted, target, table, bands, per, chans, lats):
    rows_all, lon_count = predicted.shape
    width = round_up(per * chans, LANES)
    step = -(-chans // 4) * lats
    chunks = []
    left = rows_all
    while left > 0:
        chunks.append(min(step, left))
        left -= step
    columns = table.shape[1]
    anywhere = pl.BlockSpec(memory_space=pl.ANY)
    vmem = pl.BlockSpec(memory_space=pltpu.VMEM)
    return pl.pallas_call(
        functools.partial(dft_kernel, bands, per, chans, lats, tuple(chunks)),
        out_shape=[jax.ShapeDtypeStruct((2, lats, width), jnp.bfloat16)] * bands,
        in_specs=[pl.BlockSpec(memory_space=pltpu.SMEM), anywhere, anywhere, vmem],
        out_specs=[vmem] * bands,
        scratch_shapes=[
            pltpu.VMEM((2, rows_all, lon_count), jnp.bfloat16),
            pltpu.VMEM((columns // LANES, LANES * lats, LANES), jnp.float32),
            pltpu.VMEM((columns // LANES, LANES * lats, LANES), jnp.float32),
            pltpu.VMEM((bands, lats, width), jnp.float32),
            pltpu.SemaphoreType.DMA((2, len(chunks))),
        ],
        compiler_params=pltpu.CompilerParams(vmem_limit_bytes=VMEM_LIMIT),
        name="dft",
    )(place, predicted, target, table)


def turn_kernel(basis, out):
    for o in range(basis.shape[0]):
        out[o] = basis[o].T


def turned_basis(basis):
    per_dev, lat_count, degrees = basis.shape
    return pl.pallas_call(
        turn_kernel,
        out_shape=jax.ShapeDtypeStruct((per_dev, degrees, lat_count), basis.dtype),
        compiler_params=pltpu.CompilerParams(vmem_limit_bytes=VMEM_LIMIT),
        name="turn",
    )(basis)


def legendre_kernel(bands, groups, per_dev, chans, lats, place, *rest):
    blocks = rest[:bands]
    bases = rest[bands : bands + groups]
    out = rest[bands + groups]
    basis, fourier, columns, total, sems = rest[bands + groups + 1 :]
    band, group = place[0], place[1]
    copies = []
    for q in range(groups):
        start = source_of(group, groups, q) * per_dev
        cp = pltpu.make_async_copy(bases[q], basis.at[pl.ds(start, per_dev)], sems.at[q])
        cp.start()
        copies.append(cp)
    degrees = basis.shape[1]
    width = 2 * chans
    first = jnp.where(band == 0, 1.0, 2.0).astype(jnp.float32)
    for f in range(2):
        for s in range(bands):
            row = pl.multiple_of(source_of(band, bands, s) * lats, 8)
            fourier[pl.ds(row, lats), :] = blocks[s][f].astype(jnp.float32)
        if f == 0:
            for cp in copies:
                cp.wait()
        for i in range(groups * per_dev):
            columns[i] = fourier[:, pl.ds(i * width, width)].astype(jnp.bfloat16)
        coef = jnp.dot(basis[0], columns[0], preferred_element_type=jnp.float32)
        total[:, pl.ds(0, width)] = coef * coef * first

        def one_order(i, carry):
            coef = jnp.dot(basis[i], columns[i], preferred_element_type=jnp.float32)
            total[:, pl.ds(0, width)] += coef * coef * 2.0
            return carry

        lax.fori_loop(1, groups * per_dev, one_order, 0)
        sums = total[...]
        energy = sums[:, :chans] + sums[:, chans:width]
        flat = jnp.pad(
            energy, ((0, round_up(degrees, LANES) - degrees), (0, round_up(chans, 8) - chans))
        )
        lane_tiles = round_up(degrees, LANES) // LANES
        row_tiles = round_up(chans, 8) // 8
        for k in range(lane_tiles):
            piece = flat[k * LANES : (k + 1) * LANES, :].T
            for r in range(row_tiles):
                out[(f * row_tiles + r) * lane_tiles + k] = piece[r * 8 : (r + 1) * 8, :]


def legendre_energy(place, blocks, bases, chans, lats):
    bands, groups = len(blocks), len(bases)
    per_dev, degrees, lat_count = bases[0].shape
    vmem = pl.BlockSpec(memory_space=pltpu.VMEM)
    anywhere = pl.BlockSpec(memory_space=pl.ANY)
    row_tiles = round_up(chans, 8) // 8
    lane_tiles = round_up(degrees, LANES) // LANES
    return pl.pallas_call(
        functools.partial(legendre_kernel, bands, groups, per_dev, chans, lats),
        out_shape=jax.ShapeDtypeStruct((2 * row_tiles * lane_tiles, 8, LANES), jnp.float32),
        in_specs=[pl.BlockSpec(memory_space=pltpu.SMEM)] + [vmem] * bands + [anywhere] * groups,
        out_specs=vmem,
        scratch_shapes=[
            pltpu.VMEM((groups * per_dev, degrees, lat_count), jnp.bfloat16),
            pltpu.VMEM((lat_count, blocks[0].shape[2]), jnp.float32),
            pltpu.VMEM((groups * per_dev, lat_count, 2 * chans), jnp.bfloat16),
            pltpu.VMEM((degrees, round_up(2 * chans, LANES)), jnp.float32),
            pltpu.SemaphoreType.DMA((groups,)),
        ],
        compiler_params=pltpu.CompilerParams(vmem_limit_bytes=VMEM_LIMIT),
        name="legendre",
    )(place, *blocks, *bases)


def loss_kernel(chans, degrees, count, blocks, spectra, loss):
    lane_tiles = round_up(degrees, LANES) // LANES
    row_tiles = round_up(chans, 8) // 8
    scale = 1.0 / count
    for r in range(row_tiles):
        rows = min(8, chans - r * 8)
        acc = jnp.zeros((8, LANES), jnp.float32)
        for k in range(lane_tiles):
            lanes = min(LANES, degrees - k * LANES)
            first = blocks[r * lane_tiles + k] * scale
            second = blocks[(row_tiles + r) * lane_tiles + k] * scale
            spectra[0, pl.ds(r * 8, rows), pl.ds(k * LANES, lanes)] = first[:rows, :lanes]
            spectra[1, pl.ds(r * 8, rows), pl.ds(k * LANES, lanes)] = second[:rows, :lanes]
            gap = jnp.log(first + 1e-06) - jnp.log(second + 1e-06)
            gap = gap * gap
            if lanes < LANES:
                lane_ids = lax.broadcasted_iota(jnp.int32, gap.shape, 1)
                gap = jnp.where(lane_ids < lanes, gap, 0.0)
            acc = acc + gap
        loss[pl.ds(r * 8, 8), :] = jnp.sum(acc, axis=1, keepdims=True) * (1.0 / degrees)


def loss_call(blocks, chans, degrees, count):
    return pl.pallas_call(
        functools.partial(loss_kernel, chans, degrees, count),
        out_shape=(
            jax.ShapeDtypeStruct((2, chans, degrees), jnp.float32),
            jax.ShapeDtypeStruct((round_up(chans, 8), 1), jnp.float32),
        ),
        compiler_params=pltpu.CompilerParams(vmem_limit_bytes=VMEM_LIMIT),
        name="loss",
    )(blocks)


def exchange(value, axis, step):
    return lax.ppermute(value, axis, peers(lax.axis_size(axis), step))


def reduce_all(value):
    halved = []
    for axis in ("batch", "lat"):
        index = lax.axis_index(axis)
        step = 1
        while step < lax.axis_size(axis):
            if value.shape[0] % 2 == 0:
                half = value.shape[0] // 2
                high = (index // step) % 2 == 1
                lower, upper = value[:half], value[half:]
                kept = jnp.where(high, upper, lower)
                sent = jnp.where(high, lower, upper)
                value = kept + exchange(sent, axis, step)
                halved.append((axis, step, high))
            else:
                value = value + exchange(value, axis, step)
            step *= 2
    for axis, step, high in reversed(halved):
        other = exchange(value, axis, step)
        value = jnp.where(
            high, jnp.concatenate([other, value]), jnp.concatenate([value, other])
        )
    return value


def body(predicted, target, legendre_basis):
    groups = lax.axis_size("batch")
    bands = lax.axis_size("lat")
    per_dev = legendre_basis.shape[1]
    members, chans, lats, lon_count = predicted.shape
    degrees = legendre_basis.shape[2]
    place = jnp.stack([lax.axis_index("lat"), lax.axis_index("batch")]).astype(jnp.int32)
    table = jnp.asarray(fourier_table(lon_count, groups, bands, per_dev))
    rows = members * chans * lats
    blocks = dft_blocks(
        place,
        predicted.reshape(rows, lon_count),
        target.reshape(rows, lon_count),
        table,
        bands,
        groups * per_dev * 2,
        chans,
        lats,
    )
    mine = turned_basis(jnp.transpose(legendre_basis, (1, 0, 2)))
    bases = [mine] + [exchange(mine, "batch", q) for q in range(1, groups)]
    arrived = [blocks[0]] + [exchange(blocks[s], "lat", s) for s in range(1, bands)]
    energy = legendre_energy(place, arrived, bases, chans, lats)
    energy = reduce_all(energy)
    spectra, loss = loss_call(energy, chans, degrees, members * groups * groups * bands * per_dev)
    return (spectra, loss[:chans, 0])


def solution(mesh):
    placed = (
        P("batch", None, "lat", None),
        P("batch", None, "lat", None),
        P(None, ("batch", "lat"), None),
    )
    return jax.shard_map(body, mesh=mesh, in_specs=placed, out_specs=(P(), P()), check_vma=False)
```

time: 212 us -> 118 us (0.56)
  waiting for transfers between devices: 160 us -> 38.8 us
  Pallas kernels: 0 us -> 31.8 us
  starting transfers between devices: 7.66 us -> 33.3 us
  matrix products: 15.4 us -> 0 us
  between operations: 13.8 us -> 0.79 us
  other arithmetic: 7.07 us -> 2.76 us
  local copies, waits for them, and re-layouts: 7.77 us -> 10.1 us
    psum x2 -> x0, waiting for transfers between devices: 106 us -> none  [the longest x1 71.4 us: body(): energy = lax.psum(partial_value, 'lat')]
    all_to_all x1 -> x0, waiting for transfers between devices: 53.6 us -> none  [body(): lax.all_to_all(fourier, 'lat', split_axis=3, concat_axis=7, tiled=True)]
    ppermute x0 -> x18, waiting for transfers between devices: none -> 38.8 us  [exchange(): return lax.ppermute(value, axis, peers(lax.axis_size(axis), step))]
    ppermute x0 -> x18, starting transfers between devices: none -> 33.3 us  [exchange(): return lax.ppermute(value, axis, peers(lax.axis_size(axis), step))]
    pallas_call x0 -> x4, Pallas kernels: none -> 31.8 us  [the longest x1 15.6 us: dft_blocks(): pl.pallas_call(functools.partial(dft_kernel, bands, per, chans, lats, tup...]
    dot_general x3 -> x0, matrix products: 15.4 us -> none  [the longest x2 10.3 us: transform(): jnp.einsum('bcnk,kpm->pmbcn', field_in, dft_table, preferred_element_type...]
    all_to_all x1 -> x0, starting transfers between devices: 7.55 us -> none  [body(): lax.all_to_all(fourier, 'lat', split_axis=3, concat_axis=7, tiled=True)]
    ppermute x0 -> x3, local copies, waits for them, and re-layouts: none -> 4.28 us  [exchange(): return lax.ppermute(value, axis, peers(lax.axis_size(axis), step))]
  transfers between devices with their start and end apart: 4 -> 18, of which waited for: 3 -> 11; matrix products, arithmetic and copies ran while one was open for 9% -> 4% of each run, Pallas kernels for 0% -> 13%
where the time goes in v1:
time: 118 us
  waiting for transfers between devices  38.8 us (33%)
  starting transfers between devices  33.3 us (28%)
  Pallas kernels  31.8 us (27%)
  local copies, waits for them, and re-layouts  10.1 us (9%)
  other arithmetic  2.76 us (2%)
    ppermute x18, waiting for transfers between devices, exchange(): return lax.ppermute(value, axis, peers(lax.axis_size(axis), step))  38.8 us
    ppermute x18, starting transfers between devices, exchange(): return lax.ppermute(value, axis, peers(lax.axis_size(axis), step))  33.3 us
    pallas_call x1, Pallas kernels, dft_blocks(): pl.pallas_call(functools.partial(dft_kernel, bands, per, chans, lats, tup...  15.6 us
    pallas_call x1, Pallas kernels, legendre_energy(): pl.pallas_call(functools.partial(legendre_kernel, bands, groups, per_dev,...  11.7 us
    ppermute x3, local copies, waits for them, and re-layouts, exchange(): return lax.ppermute(value, axis, peers(lax.axis_size(axis), step))  4.28 us
    unnamed x9, local copies, waits for them, and re-layouts  2.82 us
    pallas_call x1, Pallas kernels, turned_basis(): pl.pallas_call(turn_kernel, out_shape=jax.ShapeDtypeStruct((per_dev, degr...  2.56 us
  transfers between devices with their start and end apart: 18, of which 11 were waited for; matrix products, arithmetic and copies ran while one was open for 4% of the time, Pallas kernels for 13%

profile of v1, /device:TPU:0, one launch (start us, length us, event | category | flops | bytes accessed | tf_op | source)
XLA Modules:
  0.0 117.5 jit_solution(10806970446322260167)
XLA Ops:
  0.6 2.6 %turn.1.rest_8_ = bf16[3,720,192]{2,1,0:T(8,128)(2,1)} custom-call(bf16[3,192,720]{2,1,0:T(8,128)(2,1)} %bitcast.7), custom_call_target="tpu_custom_call" | custom-call | tf_op jit(solution)/shard_map/turn/pallas_call | solution.py:135
  3.2 1.6 %copy.8 = bf16[3,720,192]{1,2,0:T(8,128)(2,1)S(1)} copy(bf16[3,720,192]{2,1,0:T(8,128)(2,1)} %turn.1.rest_8_) | data formatting | bytes 1658880 | tf_op jit(solution)/shard_map/turn/pallas_call | solution.py:135
  4.8 2.5 %collective-permute-start.9 = (bf16[3,720,192]{1,2,0:T(8,128)(2,1)S(1)}, bf16[3,720,192]{1,2,0:T(8,128)(2,1)S(1)}, u32[]{:S(2)}, u32[]{:S(2)}) collective-permute-start(bf16[3,720,192]{1,2,0:T(8,128)(2,1)S(1)} %copy.8), channel_id=1, source_target_pairs={{0,24},{8,16},{16,8},{24,0},{1,25},{9,17},{17,9},{25,1},{2,26},{10... | collective-permute-start | bytes 2488328 | tf_op jit(solution)/shard_map/ppermute | solution.py:248
  8.6 15.6 %dft.1 = (bf16[2,24,1792]{2,1,0:T(8,128)(2,1)}, bf16[2,24,1792]{2,1,0:T(8,128)(2,1)}, bf16[2,24,1792]{2,1,0:T(8,128)(2,1)}, bf16[2,24,1792]{2,1,0:T(8,128)(2,1)}...) custom-call(s32[2]{0:T(128)} %pad_add_fusion.place, ...), custom_call_target="tpu_custom_call" | custom-call | tf_op jit(solution)/shard_map/dft/pallas_call | solution.py:111
  24.2 1.8 %collective-permute-start = (bf16[2,24,1792]{2,1,0:T(8,128)(2,1)}, bf16[2,24,1792]{2,1,0:T(8,128)(2,1)S(1)}, u32[]{:S(2)}, u32[]{:S(2)}) collective-permute-start(bf16[2,24,1792]{2,1,0:T(8,128)(2,1)} %get-tuple-element.13), channel_id=1, source_target_pairs={{0,1},{1,0},{2,3},{3,2},{4,5},{5,4},{6,7},{7,6},{8,9},{9,8},{10,11... | collective-permute-start | bytes 516104 | tf_op jit(solution)/shard_map/ppermute | solution.py:248
  26.1 1.6 %collective-permute-start.1 = (bf16[2,24,1792]{2,1,0:T(8,128)(2,1)}, bf16[2,24,1792]{2,1,0:T(8,128)(2,1)S(1)}, u32[]{:S(2)}, u32[]{:S(2)}) collective-permute-start(bf16[2,24,1792]{2,1,0:T(8,128)(2,1)} %get-tuple-element.14), channel_id=1, source_target_pairs={{0,2},{1,3},{2,0},{3,1},{4,6},{5,7},{6,4},{7,5},{8,10},{9,11},{10,... | collective-permute-start | bytes 516104 | tf_op jit(solution)/shard_map/ppermute | solution.py:248
  27.7 3.6 %collective-permute-done.rest_1_ = bf16[2,24,1792]{2,1,0:T(8,128)(2,1)S(1)} collective-permute-done((bf16[2,24,1792]{2,1,0:T(8,128)(2,1)}, bf16[2,24,1792]{2,1,0:T(8,128)(2,1)S(1)}, u32[]{:S(2)}, u32[]{:S(2)}) %collective-permute-start) | collective-permute-done | bytes 172064 | tf_op jit(solution)/shard_map/ppermute | solution.py:248
  31.3 2.5 %collective-permute-start.2 = (bf16[2,24,1792]{2,1,0:T(8,128)(2,1)}, bf16[2,24,1792]{2,1,0:T(8,128)(2,1)}, u32[]{:S(2)}, u32[]{:S(2)}) collective-permute-start(bf16[2,24,1792]{2,1,0:T(8,128)(2,1)} %get-tuple-element.15), channel_id=1, source_target_pairs={{0,3},{1,2},{2,1},{3,0},{4,7},{5,6},{6,5},{7,4},{8,11},{9,10},{10,... | collective-permute-start | bytes 516104 | tf_op jit(solution)/shard_map/ppermute | solution.py:248
  33.8 2.6 %collective-permute-start.3 = (bf16[2,24,1792]{2,1,0:T(8,128)(2,1)}, bf16[2,24,1792]{2,1,0:T(8,128)(2,1)}, u32[]{:S(2)}, u32[]{:S(2)}) collective-permute-start(bf16[2,24,1792]{2,1,0:T(8,128)(2,1)} %get-tuple-element.16), channel_id=1, source_target_pairs={{0,4},{1,5},{2,6},{3,7},{4,0},{5,1},{6,2},{7,3},{8,12},{9,13},{10,... | collective-permute-start | bytes 516104 | tf_op jit(solution)/shard_map/ppermute | solution.py:248
  36.7 9.8 %collective-permute-done.8 = bf16[3,720,192]{1,2,0:T(8,128)(2,1)S(1)} collective-permute-done((bf16[3,720,192]{1,2,0:T(8,128)(2,1)S(1)}, bf16[3,720,192]{1,2,0:T(8,128)(2,1)S(1)}, u32[]{:S(2)}, u32[]{:S(2)}) %collective-permute-start.8) | collective-permute-done | bytes 829472 | tf_op jit(solution)/shard_map/ppermute | solution.py:248
  46.5 4.4 %collective-permute-start.5 = (bf16[2,24,1792]{2,1,0:T(8,128)(2,1)}, bf16[2,24,1792]{2,1,0:T(8,128)(2,1)}, u32[]{:S(2)}, u32[]{:S(2)}) collective-permute-start(bf16[2,24,1792]{2,1,0:T(8,128)(2,1)} %get-tuple-element.18), channel_id=1, source_target_pairs={{0,6},{1,7},{2,4},{3,5},{4,2},{5,3},{6,0},{7,1},{8,14},{9,15},{10,... | collective-permute-start | bytes 516104 | tf_op jit(solution)/shard_map/ppermute | solution.py:248
  50.9 1.2 %collective-permute-start.6 = (bf16[2,24,1792]{2,1,0:T(8,128)(2,1)}, bf16[2,24,1792]{2,1,0:T(8,128)(2,1)S(1)}, u32[]{:S(2)}, u32[]{:S(2)}) collective-permute-start(bf16[2,24,1792]{2,1,0:T(8,128)(2,1)} %get-tuple-element.19), channel_id=1, source_target_pairs={{0,7},{1,6},{2,5},{3,4},{4,3},{5,2},{6,1},{7,0},{8,15},{9,14},{10,... | collective-permute-start | bytes 516104 | tf_op jit(solution)/shard_map/ppermute | solution.py:248
  52.1 1.4 %copy.13.rest_11_ = bf16[3,720,192]{2,1,0:T(8,128)(2,1)} copy(bf16[3,720,192]{1,2,0:T(8,128)(2,1)S(1)} %collective-permute-done.9) | data formatting | bytes 1658880 | tf_op jit(solution)/shard_map/ppermute | solution.py:248
  53.6 1.4 %copy.12.rest_10_ = bf16[3,720,192]{2,1,0:T(8,128)(2,1)} copy(bf16[3,720,192]{1,2,0:T(8,128)(2,1)S(1)} %collective-permute-done.8) | data formatting | bytes 1658880 | tf_op jit(solution)/shard_map/ppermute | solution.py:248
  55.0 1.4 %copy.11.rest_9_ = bf16[3,720,192]{2,1,0:T(8,128)(2,1)} copy(bf16[3,720,192]{1,2,0:T(8,128)(2,1)S(1)} %collective-permute-done.7) | data formatting | bytes 1658880 | tf_op jit(solution)/shard_map/ppermute | solution.py:248
  56.4 4.0 %collective-permute-done.6.rest_7_ = bf16[2,24,1792]{2,1,0:T(8,128)(2,1)S(1)} collective-permute-done((bf16[2,24,1792]{2,1,0:T(8,128)(2,1)}, bf16[2,24,1792]{2,1,0:T(8,128)(2,1)S(1)}, u32[]{:S(2)}, u32[]{:S(2)}) %collective-permute-start.6) | collective-permute-done | bytes 172064 | tf_op jit(solution)/shard_map/ppermute | solution.py:248
  61.2 11.7 %legendre.1 = f32[120,8,128]{2,1,0:T(8,128)} custom-call(s32[2]{0:T(128)} %pad_add_fusion.place, bf16[2,24,1792]{2,1,0:T(8,128)(2,1)} %get-tuple-element.12.rest_0_, bf16[2,24,1792]{2,1,0:T(8,128)(2,1)} %copy-done.1, bf16[2,24,1792]{2,1,0:T(8,128)(2,1)} %copy-done.2, bf16[2,24,1792]{2,1,0:T(8,128)(2,1)} %collective-permute-done.2.rest_3_, ...), custom_call_target="tpu_custom_call" | custom-call | tf_op jit(solution)/shard_map/legendre/pallas_call | solution.py:196
  74.1 1.5 %collective-permute-done.10 = f32[60,8,128]{2,1,0:T(8,128)S(1)} collective-permute-done((f32[60,8,128]{2,1,0:T(8,128)S(1)}, f32[60,8,128]{2,1,0:T(8,128)S(1)}, u32[]{:S(2)}, u32[]{:S(2)}) %collective-permute-start.10) | collective-permute-done | bytes 245792 | tf_op jit(solution)/shard_map/ppermute | solution.py:248
  75.6 1.6 %collective-permute-start.11 = (f32[30,8,128]{2,1,0:T(8,128)S(1)}, f32[30,8,128]{2,1,0:T(8,128)S(1)}, u32[]{:S(2)}, u32[]{:S(2)}) collective-permute-start(f32[30,8,128]{2,1,0:T(8,128)S(1)} %slice_select_fusion.1), channel_id=1, source_target_pairs={{0,16},{8,24},{16,0},{24,8},{1,17},{9,25},{17,1},{25,9},{2,18},{10... | collective-permute-start | bytes 368648 | tf_op jit(solution)/shard_map/ppermute | solution.py:248
  77.2 3.8 %collective-permute-done.11 = f32[30,8,128]{2,1,0:T(8,128)S(1)} collective-permute-done((f32[30,8,128]{2,1,0:T(8,128)S(1)}, f32[30,8,128]{2,1,0:T(8,128)S(1)}, u32[]{:S(2)}, u32[]{:S(2)}) %collective-permute-start.11) | collective-permute-done | bytes 122912 | tf_op jit(solution)/shard_map/ppermute | solution.py:248
  82.1 3.2 %collective-permute-done.12 = f32[15,8,128]{2,1,0:T(8,128)S(1)} collective-permute-done((f32[15,8,128]{2,1,0:T(8,128)S(1)}, f32[15,8,128]{2,1,0:T(8,128)S(1)}, u32[]{:S(2)}, u32[]{:S(2)}) %collective-permute-start.12) | collective-permute-done | bytes 61472 | tf_op jit(solution)/shard_map/ppermute | solution.py:248
  85.4 7.0 %collective-permute-start.13 = (f32[15,8,128]{2,1,0:T(8,128)S(1)}, f32[15,8,128]{2,1,0:T(8,128)S(1)}, u32[]{:S(2)}, u32[]{:S(2)}) collective-permute-start(f32[15,8,128]{2,1,0:T(8,128)S(1)} %select_add_fusion.2), channel_id=1, source_target_pairs={{0,2},{1,3},{2,0},{3,1},{4,6},{5,7},{6,4},{7,5},{8,10},{9,11},{10,... | collective-permute-start | bytes 184328 | tf_op jit(solution)/shard_map/ppermute | solution.py:248
  92.4 2.2 %collective-permute-done.13 = f32[15,8,128]{2,1,0:T(8,128)S(1)} collective-permute-done((f32[15,8,128]{2,1,0:T(8,128)S(1)}, f32[15,8,128]{2,1,0:T(8,128)S(1)}, u32[]{:S(2)}, u32[]{:S(2)}) %collective-permute-start.13) | collective-permute-done | bytes 61472 | tf_op jit(solution)/shard_map/ppermute | solution.py:248
  94.6 3.6 %collective-permute-start.14 = (f32[15,8,128]{2,1,0:T(8,128)S(1)}, f32[15,8,128]{2,1,0:T(8,128)S(1)}, u32[]{:S(2)}, u32[]{:S(2)}) collective-permute-start(f32[15,8,128]{2,1,0:T(8,128)S(1)} %add.34), channel_id=1, source_target_pairs={{0,4},{1,5},{2,6},{3,7},{4,0},{5,1},{6,2},{7,3},{8,12},{9,13},{10,... | collective-permute-start | bytes 184328 | tf_op jit(solution)/shard_map/ppermute | solution.py:248
  98.2 2.2 %collective-permute-done.14 = f32[15,8,128]{2,1,0:T(8,128)S(1)} collective-permute-done((f32[15,8,128]{2,1,0:T(8,128)S(1)}, f32[15,8,128]{2,1,0:T(8,128)S(1)}, u32[]{:S(2)}, u32[]{:S(2)}) %collective-permute-start.14) | collective-permute-done | bytes 61472 | tf_op jit(solution)/shard_map/ppermute | solution.py:248
  101.2 3.5 %collective-permute-done.15 = f32[15,8,128]{2,1,0:T(8,128)S(1)} collective-permute-done((f32[15,8,128]{2,1,0:T(8,128)S(1)}, f32[15,8,128]{2,1,0:T(8,128)S(1)}, u32[]{:S(2)}, u32[]{:S(2)}) %collective-permute-start.15) | collective-permute-done | bytes 61472 | tf_op jit(solution)/shard_map/ppermute | solution.py:248
  104.7 1.6 %collective-permute-start.16 = (f32[30,8,128]{2,1,0:T(8,128)S(1)}, f32[30,8,128]{2,1,0:T(8,128)S(1)}, u32[]{:S(2)}, u32[]{:S(2)}) collective-permute-start(f32[30,8,128]{2,1,0:T(8,128)S(1)} %maximum_select_fusion.2), channel_id=1, source_target_pairs={{0,16},{8,24},{16,0},{24,8},{1,17},{9,25},{17,1},{25,9},{2,18},{10... | collective-permute-start | bytes 368648 | tf_op jit(solution)/shard_map/ppermute | solution.py:248
  106.3 3.4 %collective-permute-done.16 = f32[30,8,128]{2,1,0:T(8,128)S(1)} collective-permute-done((f32[30,8,128]{2,1,0:T(8,128)S(1)}, f32[30,8,128]{2,1,0:T(8,128)S(1)}, u32[]{:S(2)}, u32[]{:S(2)}) %collective-permute-start.16) | collective-permute-done | bytes 122912 | tf_op jit(solution)/shard_map/ppermute | solution.py:248
  109.7 1.5 %collective-permute-done.17 = f32[60,8,128]{2,1,0:T(8,128)S(1)} collective-permute-done((f32[60,8,128]{2,1,0:T(8,128)S(1)}, f32[60,8,128]{2,1,0:T(8,128)S(1)}, u32[]{:S(2)}, u32[]{:S(2)}) %collective-permute-start.17) | collective-permute-done | bytes 245792 | tf_op jit(solution)/shard_map/ppermute | solution.py:248
  112.1 1.9 %loss.1 = (f32[2,73,720]{2,1,0:T(8,128)}, f32[80,1]{1,0:T(8,128)}) custom-call(f32[120,8,128]{2,1,0:T(8,128)} %maximum_select_fusion.blocks), custom_call_target="tpu_custom_call" | custom-call | tf_op jit(solution)/shard_map/loss/pallas_call | solution.py:236
  114.0 2.1 %copy.14 = f32[2,73,720]{2,0,1:T(2,128)} copy(f32[2,73,720]{2,1,0:T(8,128)} %get-tuple-element.26) | data formatting | bytes 840960
  116.1 1.4 %slice_reduce_fusion = f32[73]{0:T(128)} fusion(f32[80,1]{1,0:T(8,128)} %get-tuple-element.21), kind=kLoop, calls=%fused_computation.9 | loop fusion | bytes 584 | tf_op jit(solution)/shard_map/slice | solution.py:301
  (34 shorter events, 6.4 us)
Async XLA Ops:
  4.8 31.6 %collective-permute-start.9 = (bf16[3,720,192]{1,2,0:T(8,128)(2,1)S(1)}, bf16[3,720,192]{1,2,0:T(8,128)(2,1)S(1)}, u32[]{:S(2)}, u32[]{:S(2)}) collective-permute-start(bf16[3,720,192]{1,2,0:T(8,128)(2,1)S(1)} %copy.8), channel_id=1, source_target_pairs={{0,24},{8,16},{16,8},{24,0},{1,25},{9,17},{17,9},{25,1},{2,26},{10... | collective-permute-start | bytes 2488328 | tf_op jit(solution)/shard_map/ppermute | solution.py:248
  7.3 39.2 %collective-permute-start.8 = (bf16[3,720,192]{1,2,0:T(8,128)(2,1)S(1)}, bf16[3,720,192]{1,2,0:T(8,128)(2,1)S(1)}, u32[]{:S(2)}, u32[]{:S(2)}) collective-permute-start(bf16[3,720,192]{1,2,0:T(8,128)(2,1)S(1)} %copy.8), channel_id=1, source_target_pairs={{0,16},{8,24},{16,0},{24,8},{1,17},{9,25},{17,1},{25,9},{2,18},{10... | collective-permute-start | bytes 2488328 | tf_op jit(solution)/shard_map/ppermute | solution.py:248
  7.9 42.9 %collective-permute-start.7 = (bf16[3,720,192]{1,2,0:T(8,128)(2,1)S(1)}, bf16[3,720,192]{1,2,0:T(8,128)(2,1)S(1)}, u32[]{:S(2)}, u32[]{:S(2)}) collective-permute-start(bf16[3,720,192]{1,2,0:T(8,128)(2,1)S(1)} %copy.8), channel_id=1, source_target_pairs={{0,8},{8,0},{16,24},{24,16},{1,9},{9,1},{17,25},{25,17},{2,10},{10... | collective-permute-start | bytes 2488328 | tf_op jit(solution)/shard_map/ppermute | solution.py:248
  24.2 7.0 %collective-permute-start = (bf16[2,24,1792]{2,1,0:T(8,128)(2,1)}, bf16[2,24,1792]{2,1,0:T(8,128)(2,1)S(1)}, u32[]{:S(2)}, u32[]{:S(2)}) collective-permute-start(bf16[2,24,1792]{2,1,0:T(8,128)(2,1)} %get-tuple-element.13), channel_id=1, source_target_pairs={{0,1},{1,0},{2,3},{3,2},{4,5},{5,4},{6,7},{7,6},{8,9},{9,8},{10,11... | collective-permute-start | bytes 516104 | tf_op jit(solution)/shard_map/ppermute | solution.py:248
  26.1 7.7 %collective-permute-start.1 = (bf16[2,24,1792]{2,1,0:T(8,128)(2,1)}, bf16[2,24,1792]{2,1,0:T(8,128)(2,1)S(1)}, u32[]{:S(2)}, u32[]{:S(2)}) collective-permute-start(bf16[2,24,1792]{2,1,0:T(8,128)(2,1)} %get-tuple-element.14), channel_id=1, source_target_pairs={{0,2},{1,3},{2,0},{3,1},{4,6},{5,7},{6,4},{7,5},{8,10},{9,11},{10,... | collective-permute-start | bytes 516104 | tf_op jit(solution)/shard_map/ppermute | solution.py:248
  31.3 19.6 %copy-start.1 = (bf16[2,24,1792]{2,1,0:T(8,128)(2,1)}, bf16[2,24,1792]{2,1,0:T(8,128)(2,1)S(1)}, u32[]{:S(2)}) copy-start(bf16[2,24,1792]{2,1,0:T(8,128)(2,1)S(1)} %collective-permute-done.rest_1_) | copy-start | bytes 516100
  31.3 25.1 %collective-permute-start.2 = (bf16[2,24,1792]{2,1,0:T(8,128)(2,1)}, bf16[2,24,1792]{2,1,0:T(8,128)(2,1)}, u32[]{:S(2)}, u32[]{:S(2)}) collective-permute-start(bf16[2,24,1792]{2,1,0:T(8,128)(2,1)} %get-tuple-element.15), channel_id=1, source_target_pairs={{0,3},{1,2},{2,1},{3,0},{4,7},{5,6},{6,5},{7,4},{8,11},{9,10},{10,... | collective-permute-start | bytes 516104 | tf_op jit(solution)/shard_map/ppermute | solution.py:248
  33.8 17.1 %copy-start.2 = (bf16[2,24,1792]{2,1,0:T(8,128)(2,1)}, bf16[2,24,1792]{2,1,0:T(8,128)(2,1)S(1)}, u32[]{:S(2)}) copy-start(bf16[2,24,1792]{2,1,0:T(8,128)(2,1)S(1)} %collective-permute-done.1.rest_2_) | copy-start | bytes 516100
  33.8 22.6 %collective-permute-start.3 = (bf16[2,24,1792]{2,1,0:T(8,128)(2,1)}, bf16[2,24,1792]{2,1,0:T(8,128)(2,1)}, u32[]{:S(2)}, u32[]{:S(2)}) collective-permute-start(bf16[2,24,1792]{2,1,0:T(8,128)(2,1)} %get-tuple-element.16), channel_id=1, source_target_pairs={{0,4},{1,5},{2,6},{3,7},{4,0},{5,1},{6,2},{7,3},{8,12},{9,13},{10,... | collective-permute-start | bytes 516104 | tf_op jit(solution)/shard_map/ppermute | solution.py:248
  36.4 20.0 %collective-permute-start.4 = (bf16[2,24,1792]{2,1,0:T(8,128)(2,1)}, bf16[2,24,1792]{2,1,0:T(8,128)(2,1)}, u32[]{:S(2)}, u32[]{:S(2)}) collective-permute-start(bf16[2,24,1792]{2,1,0:T(8,128)(2,1)} %get-tuple-element.17), channel_id=1, source_target_pairs={{0,5},{1,4},{2,7},{3,6},{4,1},{5,0},{6,3},{7,2},{8,13},{9,12},{10,... | collective-permute-start | bytes 516104 | tf_op jit(solution)/shard_map/ppermute | solution.py:248
  46.5 10.0 %collective-permute-start.5 = (bf16[2,24,1792]{2,1,0:T(8,128)(2,1)}, bf16[2,24,1792]{2,1,0:T(8,128)(2,1)}, u32[]{:S(2)}, u32[]{:S(2)}) collective-permute-start(bf16[2,24,1792]{2,1,0:T(8,128)(2,1)} %get-tuple-element.18), channel_id=1, source_target_pairs={{0,6},{1,7},{2,4},{3,5},{4,2},{5,3},{6,0},{7,1},{8,14},{9,15},{10,... | collective-permute-start | bytes 516104 | tf_op jit(solution)/shard_map/ppermute | solution.py:248
  50.9 9.6 %collective-permute-start.6 = (bf16[2,24,1792]{2,1,0:T(8,128)(2,1)}, bf16[2,24,1792]{2,1,0:T(8,128)(2,1)S(1)}, u32[]{:S(2)}, u32[]{:S(2)}) collective-permute-start(bf16[2,24,1792]{2,1,0:T(8,128)(2,1)} %get-tuple-element.19), channel_id=1, source_target_pairs={{0,7},{1,6},{2,5},{3,4},{4,3},{5,2},{6,1},{7,0},{8,15},{9,14},{10,... | collective-permute-start | bytes 516104 | tf_op jit(solution)/shard_map/ppermute | solution.py:248
  60.5 0.7 copy-start.3
  72.8 2.7 %copy-start = (f32[120,8,128]{2,1,0:T(8,128)S(1)}, f32[120,8,128]{2,1,0:T(8,128)}, u32[]{:S(2)}) copy-start(f32[120,8,128]{2,1,0:T(8,128)} %legendre.1) | copy-start | bytes 1474564
  74.0 1.6 %collective-permute-start.10 = (f32[60,8,128]{2,1,0:T(8,128)S(1)}, f32[60,8,128]{2,1,0:T(8,128)S(1)}, u32[]{:S(2)}, u32[]{:S(2)}) collective-permute-start(f32[60,8,128]{2,1,0:T(8,128)S(1)} %slice_select_fusion), channel_id=1, source_target_pairs={{0,8},{8,0},{16,24},{24,16},{1,9},{9,1},{17,25},{25,17},{2,10},{10... | collective-permute-start | bytes 737288 | tf_op jit(solution)/shard_map/ppermute | solution.py:248
  75.6 5.4 %collective-permute-start.11 = (f32[30,8,128]{2,1,0:T(8,128)S(1)}, f32[30,8,128]{2,1,0:T(8,128)S(1)}, u32[]{:S(2)}, u32[]{:S(2)}) collective-permute-start(f32[30,8,128]{2,1,0:T(8,128)S(1)} %slice_select_fusion.1), channel_id=1, source_target_pairs={{0,16},{8,24},{16,0},{24,8},{1,17},{9,25},{17,1},{25,9},{2,18},{10... | collective-permute-start | bytes 368648 | tf_op jit(solution)/shard_map/ppermute | solution.py:248
  81.1 4.3 %collective-permute-start.12 = (f32[15,8,128]{2,1,0:T(8,128)S(1)}, f32[15,8,128]{2,1,0:T(8,128)S(1)}, u32[]{:S(2)}, u32[]{:S(2)}) collective-permute-start(f32[15,8,128]{2,1,0:T(8,128)S(1)} %slice_select_fusion.2), channel_id=1, source_target_pairs={{0,1},{1,0},{2,3},{3,2},{4,5},{5,4},{6,7},{7,6},{8,9},{9,8},{10,11... | collective-permute-start | bytes 184328 | tf_op jit(solution)/shard_map/ppermute | solution.py:248
  85.4 9.2 %collective-permute-start.13 = (f32[15,8,128]{2,1,0:T(8,128)S(1)}, f32[15,8,128]{2,1,0:T(8,128)S(1)}, u32[]{:S(2)}, u32[]{:S(2)}) collective-permute-start(f32[15,8,128]{2,1,0:T(8,128)S(1)} %select_add_fusion.2), channel_id=1, source_target_pairs={{0,2},{1,3},{2,0},{3,1},{4,6},{5,7},{6,4},{7,5},{8,10},{9,11},{10,... | collective-permute-start | bytes 184328 | tf_op jit(solution)/shard_map/ppermute | solution.py:248
  94.6 5.8 %collective-permute-start.14 = (f32[15,8,128]{2,1,0:T(8,128)S(1)}, f32[15,8,128]{2,1,0:T(8,128)S(1)}, u32[]{:S(2)}, u32[]{:S(2)}) collective-permute-start(f32[15,8,128]{2,1,0:T(8,128)S(1)} %add.34), channel_id=1, source_target_pairs={{0,4},{1,5},{2,6},{3,7},{4,0},{5,1},{6,2},{7,3},{8,12},{9,13},{10,... | collective-permute-start | bytes 184328 | tf_op jit(solution)/shard_map/ppermute | solution.py:248
  100.4 4.3 %collective-permute-start.15 = (f32[15,8,128]{2,1,0:T(8,128)S(1)}, f32[15,8,128]{2,1,0:T(8,128)S(1)}, u32[]{:S(2)}, u32[]{:S(2)}) collective-permute-start(f32[15,8,128]{2,1,0:T(8,128)S(1)} %add.35), channel_id=1, source_target_pairs={{0,1},{1,0},{2,3},{3,2},{4,5},{5,4},{6,7},{7,6},{8,9},{9,8},{10,11... | collective-permute-start | bytes 184328 | tf_op jit(solution)/shard_map/ppermute | solution.py:248
  104.7 4.9 %collective-permute-start.16 = (f32[30,8,128]{2,1,0:T(8,128)S(1)}, f32[30,8,128]{2,1,0:T(8,128)S(1)}, u32[]{:S(2)}, u32[]{:S(2)}) collective-permute-start(f32[30,8,128]{2,1,0:T(8,128)S(1)} %maximum_select_fusion.2), channel_id=1, source_target_pairs={{0,16},{8,24},{16,0},{24,8},{1,17},{9,25},{17,1},{25,9},{2,18},{10... | collective-permute-start | bytes 368648 | tf_op jit(solution)/shard_map/ppermute | solution.py:248
  109.7 1.6 %collective-permute-start.17 = (f32[60,8,128]{2,1,0:T(8,128)S(1)}, f32[60,8,128]{2,1,0:T(8,128)S(1)}, u32[]{:S(2)}, u32[]{:S(2)}) collective-permute-start(f32[60,8,128]{2,1,0:T(8,128)S(1)} %maximum_select_fusion.1), channel_id=1, source_target_pairs={{0,8},{8,0},{16,24},{24,16},{1,9},{9,1},{17,25},{25,17},{2,10},{10... | collective-permute-start | bytes 737288 | tf_op jit(solution)/shard_map/ppermute | solution.py:248

commit v2 on v1

v2 whole, which is shorter than its diff:
```python
import functools
import math

import jax
import jax.numpy as jnp
import numpy as np
from jax import lax
from jax.experimental import pallas as pl
from jax.experimental.pallas import tpu as pltpu
from jax.sharding import PartitionSpec as P


LANES = 128
VMEM_LIMIT = 24 * 1024 * 1024
STAGED_LIMIT = 59 * 1024 * 1024
SPARE_VMEM = 16 * 1024 * 1024


def round_up(value, step):
    return -(-value // step) * step


def fourier_table(lon_count, groups, bands, per_dev):
    orders = np.arange(groups * bands * per_dev).reshape(groups, bands, per_dev)
    orders = orders.transpose(1, 0, 2).reshape(-1)
    product_ids = np.arange(lon_count)[:, None] * orders[None, :] % lon_count
    angles = np.float32(2.0 * math.pi / lon_count) * product_ids.astype(np.float32)
    inv_root = np.float32(1.0 / math.sqrt(lon_count))
    both = np.stack([np.cos(angles) * inv_root, -np.sin(angles) * inv_root], axis=2)
    flat = both.reshape(lon_count, -1).astype(jnp.bfloat16)
    padded = round_up(flat.shape[1], LANES)
    return np.pad(flat, ((0, 0), (0, padded - flat.shape[1])))


def peers(count, step):
    if count & (count - 1) == 0:
        return [(i, i ^ step) for i in range(count)]
    return [(i, (i + step) % count) for i in range(count)]


def target_of(index, count, step):
    if count & (count - 1) == 0:
        return jnp.bitwise_xor(index, step)
    return lax.rem(index + step, count)


def source_of(index, count, step):
    if count & (count - 1) == 0:
        return jnp.bitwise_xor(index, step)
    return lax.rem(index + count - step, count)


def dft_kernel(bands, per, chans, lats, chunks, staged, place, field, table, *rest):
    outs = rest[:bands]
    dscr, turned, packed = rest[bands : bands + 3]
    copies = []
    row = 0
    xbuf = rest[bands + 3] if staged else field
    for i, rows in enumerate(chunks):
        cp = None
        if staged:
            cp = pltpu.make_async_copy(
                field.at[pl.ds(row, rows), :], xbuf.at[pl.ds(row, rows), :], rest[-1].at[i]
            )
            cp.start()
        copies.append((row, rows, cp))
        row += rows
    band = place[0]
    tiles = dscr.shape[0]
    for row, rows, cp in copies:
        if staged:
            cp.wait()
        res = jnp.dot(xbuf[pl.ds(row, rows), :], table[...], preferred_element_type=jnp.float32)
        for q in range(tiles):
            dscr[q, pl.ds(row, rows), :] = res[:, q * LANES : (q + 1) * LANES]

    def turn(q, carry):
        for n in range(lats):
            block = dscr.at[q][pl.ds(n, LANES, stride=lats), :]
            turned.at[q][pl.ds(n, LANES, stride=lats), :] = block.T
        return carry

    lax.fori_loop(0, tiles, turn, 0)

    def pack(s, carry):
        base = target_of(band, bands, s) * per
        for g in range(per):
            column = base + g
            start = pl.multiple_of(lax.rem(column, LANES) * lats, 8)
            packed[s, :, pl.ds(g * chans, chans)] = turned[
                column // LANES, pl.ds(start, lats), pl.ds(0, chans)
            ]
        return carry

    lax.fori_loop(0, bands, pack, 0)
    for s in range(bands):
        outs[s][...] = packed[s].astype(jnp.bfloat16)


def dft_blocks(place, field, table, bands, per, chans, lats, staged):
    rows_all, lon_count = field.shape
    width = round_up(per * chans, LANES)
    step = -(-chans // 4) * lats
    chunks = []
    left = rows_all
    while left > 0:
        chunks.append(min(step, left))
        left -= step
    columns = table.shape[1]
    held = 4 * lats * (2 * columns * LANES + bands * width)
    anywhere = pl.BlockSpec(memory_space=pl.ANY)
    vmem = pl.BlockSpec(memory_space=pltpu.VMEM)
    return pl.pallas_call(
        functools.partial(dft_kernel, bands, per, chans, lats, tuple(chunks), staged),
        out_shape=[jax.ShapeDtypeStruct((lats, width), jnp.bfloat16)] * bands,
        in_specs=[pl.BlockSpec(memory_space=pltpu.SMEM), anywhere if staged else vmem, vmem],
        out_specs=[vmem] * bands,
        scratch_shapes=[
            pltpu.VMEM((columns // LANES, LANES * lats, LANES), jnp.float32),
            pltpu.VMEM((columns // LANES, LANES * lats, LANES), jnp.float32),
            pltpu.VMEM((bands, lats, width), jnp.float32),
        ]
        + (
            [
                pltpu.VMEM((rows_all, lon_count), jnp.bfloat16),
                pltpu.SemaphoreType.DMA((len(chunks),)),
            ]
            if staged
            else []
        ),
        compiler_params=pltpu.CompilerParams(
            vmem_limit_bytes=STAGED_LIMIT if staged else SPARE_VMEM + held
        ),
        name="dft",
    )(place, field, table)


def turn_kernel(basis, out):
    for o in range(basis.shape[0]):
        out[o, :, : basis.shape[1]] = basis[o].T


def turned_basis(basis):
    per_dev, lat_count, degrees = basis.shape
    return pl.pallas_call(
        turn_kernel,
        out_shape=jax.ShapeDtypeStruct((per_dev, degrees, round_up(lat_count, LANES)), basis.dtype),
        compiler_params=pltpu.CompilerParams(vmem_limit_bytes=VMEM_LIMIT),
        name="turn",
    )(basis)


def legendre_kernel(bands, groups, per_dev, chans, lats, slots, place, *rest):
    blocks = rest[:bands]
    bases = rest[bands : bands + groups]
    out = rest[bands + groups]
    fourier, columns, total = rest[bands + groups + 1 :]
    band, group = place[0], place[1]
    degrees = bases[0].shape[1]
    depth = bands * lats
    width = 2 * chans
    for s in range(bands):
        row = pl.multiple_of(source_of(band, bands, s) * lats, 8)
        fourier[pl.ds(row, lats), :] = blocks[s][...].astype(jnp.float32)
    for i in range(groups * per_dev):
        columns[i] = fourier[:, pl.ds(i * width, width)].astype(jnp.bfloat16)
    for q in range(groups):
        owner = jnp.bitwise_xor(group, slots[q])
        first = jnp.where(jnp.logical_and(band == 0, owner == 0), 1.0, 2.0)
        squares = None
        for o in range(per_dev):
            coef = jnp.dot(
                bases[q][o, :, :depth],
                columns[owner * per_dev + o],
                preferred_element_type=jnp.float32,
            )
            term = coef * coef * (first if o == 0 else 2.0)
            squares = term if squares is None else squares + term
        if q == 0:
            total[:, pl.ds(0, width)] = squares
        else:
            total[:, pl.ds(0, width)] += squares
    sums = total[...]
    energy = sums[:, :chans] + sums[:, chans:width]
    flat = jnp.pad(
        energy, ((0, round_up(degrees, LANES) - degrees), (0, round_up(chans, 8) - chans))
    )
    lane_tiles = round_up(degrees, LANES) // LANES
    row_tiles = round_up(chans, 8) // 8
    for k in range(lane_tiles):
        piece = flat[k * LANES : (k + 1) * LANES, :].T
        for r in range(row_tiles):
            out[r * lane_tiles + k] = piece[r * 8 : (r + 1) * 8, :]


def legendre_energy(place, blocks, bases, slots, chans, lats):
    bands, groups = len(blocks), len(bases)
    per_dev, degrees, _ = bases[0].shape
    vmem = pl.BlockSpec(memory_space=pltpu.VMEM)
    row_tiles = round_up(chans, 8) // 8
    lane_tiles = round_up(degrees, LANES) // LANES
    return pl.pallas_call(
        functools.partial(legendre_kernel, bands, groups, per_dev, chans, lats, slots),
        out_shape=jax.ShapeDtypeStruct((row_tiles * lane_tiles, 8, LANES), jnp.float32),
        in_specs=[pl.BlockSpec(memory_space=pltpu.SMEM)] + [vmem] * (bands + groups),
        out_specs=vmem,
        scratch_shapes=[
            pltpu.VMEM((bands * lats, blocks[0].shape[1]), jnp.float32),
            pltpu.VMEM((groups * per_dev, bands * lats, 2 * chans), jnp.bfloat16),
            pltpu.VMEM((degrees, round_up(2 * chans, LANES)), jnp.float32),
        ],
        compiler_params=pltpu.CompilerParams(vmem_limit_bytes=VMEM_LIMIT),
        name="legendre",
    )(place, *blocks, *bases)


def loss_kernel(chans, degrees, count, blocks, spectra, loss, sums):
    lane_tiles = round_up(degrees, LANES) // LANES
    row_tiles = round_up(chans, 8) // 8
    scale = 1.0 / count
    for r in range(row_tiles):
        rows = min(8, chans - r * 8)
        acc = jnp.zeros((8, LANES), jnp.float32)
        for k in range(lane_tiles):
            lanes = min(LANES, degrees - k * LANES)
            first = blocks[r * lane_tiles + k] * scale
            second = blocks[(row_tiles + r) * lane_tiles + k] * scale
            spectra[0, pl.ds(r * 8, rows), pl.ds(k * LANES, lanes)] = first[:rows, :lanes]
            spectra[1, pl.ds(r * 8, rows), pl.ds(k * LANES, lanes)] = second[:rows, :lanes]
            gap = jnp.log(first + 1e-06) - jnp.log(second + 1e-06)
            gap = gap * gap
            if lanes < LANES:
                lane_ids = lax.broadcasted_iota(jnp.int32, gap.shape, 1)
                gap = jnp.where(lane_ids < lanes, gap, 0.0)
            acc = acc + gap
        sums[pl.ds(r * 8, 8), :] = acc
    turned = sums[...].T
    loss[...] = (jnp.sum(turned, axis=0, keepdims=True) * (1.0 / degrees))[:, :chans]


def loss_call(blocks, chans, degrees, count):
    return pl.pallas_call(
        functools.partial(loss_kernel, chans, degrees, count),
        out_shape=(
            jax.ShapeDtypeStruct((2, chans, degrees), jnp.float32),
            jax.ShapeDtypeStruct((1, chans), jnp.float32),
        ),
        scratch_shapes=[pltpu.VMEM((round_up(chans, 8), LANES), jnp.float32)],
        compiler_params=pltpu.CompilerParams(vmem_limit_bytes=VMEM_LIMIT),
        name="loss",
    )(blocks)


def exchange(value, axis, step):
    return lax.ppermute(value, axis, peers(lax.axis_size(axis), step))


def reduce_all(value):
    halved = []
    index = lax.axis_index("batch")
    step = 1
    while step < lax.axis_size("batch"):
        if value.shape[0] % 2 == 0:
            half = value.shape[0] // 2
            high = (index // step) % 2 == 1
            lower, upper = value[:half], value[half:]
            kept = jnp.where(high, upper, lower)
            sent = jnp.where(high, lower, upper)
            value = kept + exchange(sent, "batch", step)
            halved.append((step, high))
        else:
            value = value + exchange(value, "batch", step)
        step *= 2
    bands = lax.axis_size("lat")
    step = 1
    radix = 2 if bands.bit_length() % 2 == 0 else 4
    while step < bands:
        parts = [exchange(value, "lat", k * step) for k in range(radix - 1, 0, -1)]
        value = value + sum(parts[1:], parts[0])
        step *= radix
        radix = 4
    for step, high in reversed(halved):
        other = exchange(value, "batch", step)
        value = jnp.where(
            high, jnp.concatenate([other, value]), jnp.concatenate([value, other])
        )
    return value


def spectrum_loss(predicted, target, legendre_basis):
    groups = lax.axis_size("batch")
    bands = lax.axis_size("lat")
    per_dev = legendre_basis.shape[1]
    members, chans, lats, lon_count = predicted.shape
    degrees = legendre_basis.shape[2]
    place = jnp.stack([lax.axis_index("lat"), lax.axis_index("batch")]).astype(jnp.int32)
    table = jnp.asarray(fourier_table(lon_count, groups, bands, per_dev))
    rows = members * chans * lats
    fields = (predicted, target)
    steps = list(range(bands - 1, 0, -1))

    sent = []
    for f, field in enumerate(fields):
        flat = field.reshape(rows, lon_count)
        sent.append(
            dft_blocks(
                place, flat, table, bands, groups * per_dev * 2, chans, lats, f == 0
            )
        )
    arrived = []
    for f in range(2):
        got = {0: sent[f][0]}
        for s in steps:
            got[s] = exchange(sent[f][s], "lat", s)
        arrived.append([got[s] for s in range(bands)])
    bases = [turned_basis(jnp.transpose(legendre_basis, (1, 0, 2)))]
    slots = [0]
    step = groups // 2
    while step:
        bases = bases + [exchange(block, "batch", step) for block in bases]
        slots = slots + [slot ^ step for slot in slots]
        step //= 2
    energies = []
    for f in range(2):
        energies.append(legendre_energy(place, arrived[f], bases, slots, chans, lats))
    energy = reduce_all(jnp.concatenate(energies))
    spectra, loss = loss_call(energy, chans, degrees, members * groups * groups * bands * per_dev)
    return (spectra, loss.reshape(chans))


def solution(mesh):
    placed = (
        P("batch", None, "lat", None),
        P("batch", None, "lat", None),
        P(None, ("batch", "lat"), None),
    )
    return jax.shard_map(spectrum_loss, mesh=mesh, in_specs=placed, out_specs=(P(), P()), check_vma=False)
```

time: 118 us -> 126 us (1.068)
  waiting for transfers between devices: 38.8 us -> 52.5 us
  Pallas kernels: 31.8 us -> 22.1 us
  local copies, waits for them, and re-layouts: 10.1 us -> 16.9 us
  other arithmetic: 2.76 us -> 1.24 us
  starting transfers between devices: 33.3 us -> 32 us
    unnamed x9 -> x49, local copies, waits for them, and re-layouts: 2.82 us -> 16.9 us
    ppermute x18 -> x25, waiting for transfers between devices: 38.8 us -> 52.5 us  [exchange(): return lax.ppermute(value, axis, peers(lax.axis_size(axis), step))]
    pallas_call x1 -> x2, Pallas kernels: 11.7 us -> 7.12 us  [legendre_energy(): pl.pallas_call(functools.partial(legendre_kernel, bands, groups, per_dev,...]
    ppermute x3 -> x0, local copies, waits for them, and re-layouts: 4.28 us -> none  [exchange(): return lax.ppermute(value, axis, peers(lax.axis_size(axis), step))]
    pallas_call x1, Pallas kernels: 2.56 us -> 0.35 us  [turned_basis(): pl.pallas_call(turn_kernel, out_shape=jax.ShapeDtypeStruct((per_dev, degr...]
    pallas_call x1 -> x2, Pallas kernels: 15.6 us -> 14 us  [dft_blocks(): pl.pallas_call(functools.partial(dft_kernel, bands, per, chans, lats, tup...]
    pallas_call x1 -> x0, local copies, waits for them, and re-layouts: 1.63 us -> none  [turned_basis(): pl.pallas_call(turn_kernel, out_shape=jax.ShapeDtypeStruct((per_dev, degr...]
    slice x1 -> x0, local copies, waits for them, and re-layouts: 1.4 us -> none  [body(): return (spectra, loss[:chans, 0])]
  transfers between devices with their start and end apart: 18 -> 25, of which waited for: 11 -> 10; matrix products, arithmetic and copies ran while one was open for 4% -> 0% of each run, Pallas kernels for 13% -> 14%
where the time goes in v2:
time: 126 us
  waiting for transfers between devices  52.5 us (42%)
  starting transfers between devices  32 us (25%)
  Pallas kernels  22.1 us (18%)
  local copies, waits for them, and re-layouts  16.9 us (13%)
    ppermute x25, waiting for transfers between devices, exchange(): return lax.ppermute(value, axis, peers(lax.axis_size(axis), step))  52.5 us
    ppermute x25, starting transfers between devices, exchange(): return lax.ppermute(value, axis, peers(lax.axis_size(axis), step))  32 us
    unnamed x49, local copies, waits for them, and re-layouts  16.9 us
    pallas_call x2, Pallas kernels, dft_blocks(): pl.pallas_call(functools.partial(dft_kernel, bands, per, chans, lats, tup...  14 us
    pallas_call x2, Pallas kernels, legendre_energy(): pl.pallas_call(functools.partial(legendre_kernel, bands, groups, per_dev,...  7.12 us
  transfers between devices with their start and end apart: 25, of which 10 were waited for; matrix products, arithmetic and copies ran while one was open for 0% of the time, Pallas kernels for 14%

profile of v2, /device:TPU:0, one launch (start us, length us, event | category | flops | bytes accessed | tf_op | source)
XLA Modules:
  0.0 125.7 jit_solution(6359305743058244124)
XLA Ops:
  0.6 1.2 copy-done.4
  2.2 3.0 %collective-permute-start.7 = (bf16[3,720,256]{2,1,0:T(8,128)(2,1)S(1)}, bf16[3,720,256]{2,1,0:T(8,128)(2,1)S(1)}, u32[]{:S(2)}, u32[]{:S(2)}) collective-permute-start(bf16[3,720,256]{2,1,0:T(8,128)(2,1)S(1)} %turn.1.rest_8_), channel_id=1, source_target_pairs={{0,16},{8,24},{16,0},{24,8},{1,17},{9,25},{17,1},{25,9},{2,18},{10... | collective-permute-start | bytes 3317768 | tf_op jit(solution)/shard_map/ppermute | solution.py:255
  5.2 24.4 %collective-permute-done.7.rest_9_ = bf16[3,720,256]{2,1,0:T(8,128)(2,1)S(1)} collective-permute-done((bf16[3,720,256]{2,1,0:T(8,128)(2,1)S(1)}, bf16[3,720,256]{2,1,0:T(8,128)(2,1)S(1)}, u32[]{:S(2)}, u32[]{:S(2)}) %collective-permute-start.7) | collective-permute-done | bytes 1105952 | tf_op jit(solution)/shard_map/ppermute | solution.py:255
  29.7 2.5 %copy-done = bf16[1,73,24,1440]{3,2,1,0:T(8,128)(2,1)S(1)} copy-done((bf16[1,73,24,1440]{3,2,1,0:T(8,128)(2,1)S(1)}, bf16[1,73,24,1440]{3,2,1,0:T(8,128)(2,1)}, u32[]{:S(2)}) %copy-start) | copy-done | bytes 5045784
  32.2 1.1 copy-done.1
  33.3 4.7 %dft.2 = (bf16[24,1792]{1,0:T(8,128)(2,1)S(1)}, bf16[24,1792]{1,0:T(8,128)(2,1)S(1)}, bf16[24,1792]{1,0:T(8,128)(2,1)S(1)}, bf16[24,1792]{1,0:T(8,128)(2,1)S(1)}...) custom-call(s32[2]{0:T(128)S(1)} %pad_add_fusion.place, ...), custom_call_target="tpu_custom_call" | custom-call | tf_op jit(solution)/shard_map/dft/pallas_call | solution.py:113
  38.0 1.8 %collective-permute-start = (bf16[24,1792]{1,0:T(8,128)(2,1)S(1)}, bf16[24,1792]{1,0:T(8,128)(2,1)S(1)}, u32[]{:S(2)}, u32[]{:S(2)}) collective-permute-start(bf16[24,1792]{1,0:T(8,128)(2,1)S(1)} %get-tuple-element.21), channel_id=1, source_target_pairs={{0,1},{1,0},{2,3},{3,2},{4,5},{5,4},{6,7},{7,6},{8,9},{9,8},{10,11... | collective-permute-start | bytes 258056 | tf_op jit(solution)/shard_map/ppermute | solution.py:255
  39.9 1.6 %collective-permute-start.1 = (bf16[24,1792]{1,0:T(8,128)(2,1)S(1)}, bf16[24,1792]{1,0:T(8,128)(2,1)S(1)}, u32[]{:S(2)}, u32[]{:S(2)}) collective-permute-start(bf16[24,1792]{1,0:T(8,128)(2,1)S(1)} %get-tuple-element.22), channel_id=1, source_target_pairs={{0,2},{1,3},{2,0},{3,1},{4,6},{5,7},{6,4},{7,5},{8,10},{9,11},{10,... | collective-permute-start | bytes 258056 | tf_op jit(solution)/shard_map/ppermute | solution.py:255
  41.6 1.5 %collective-permute-done.rest_1_ = bf16[24,1792]{1,0:T(8,128)(2,1)S(1)} collective-permute-done((bf16[24,1792]{1,0:T(8,128)(2,1)S(1)}, bf16[24,1792]{1,0:T(8,128)(2,1)S(1)}, u32[]{:S(2)}, u32[]{:S(2)}) %collective-permute-start) | collective-permute-done | bytes 86048 | tf_op jit(solution)/shard_map/ppermute | solution.py:255
  43.1 2.8 %collective-permute-start.3 = (bf16[24,1792]{1,0:T(8,128)(2,1)S(1)}, bf16[24,1792]{1,0:T(8,128)(2,1)S(1)}, u32[]{:S(2)}, u32[]{:S(2)}) collective-permute-start(bf16[24,1792]{1,0:T(8,128)(2,1)S(1)} %get-tuple-element.24), channel_id=1, source_target_pairs={{0,4},{1,5},{2,6},{3,7},{4,0},{5,1},{6,2},{7,3},{8,12},{9,13},{10,... | collective-permute-start | bytes 258056 | tf_op jit(solution)/shard_map/ppermute | solution.py:255
  46.5 1.3 %collective-permute-start.4 = (bf16[24,1792]{1,0:T(8,128)(2,1)S(1)}, bf16[24,1792]{1,0:T(8,128)(2,1)S(1)}, u32[]{:S(2)}, u32[]{:S(2)}) collective-permute-start(bf16[24,1792]{1,0:T(8,128)(2,1)S(1)} %get-tuple-element.25), channel_id=1, source_target_pairs={{0,5},{1,4},{2,7},{3,6},{4,1},{5,0},{6,3},{7,2},{8,13},{9,12},{10,... | collective-permute-start | bytes 258056 | tf_op jit(solution)/shard_map/ppermute | solution.py:255
  48.4 3.6 %collective-permute-start.5 = (bf16[24,1792]{1,0:T(8,128)(2,1)S(1)}, bf16[24,1792]{1,0:T(8,128)(2,1)S(1)}, u32[]{:S(2)}, u32[]{:S(2)}) collective-permute-start(bf16[24,1792]{1,0:T(8,128)(2,1)S(1)} %get-tuple-element.26), channel_id=1, source_target_pairs={{0,6},{1,7},{2,4},{3,5},{4,2},{5,3},{6,0},{7,1},{8,14},{9,15},{10,... | collective-permute-start | bytes 258056 | tf_op jit(solution)/shard_map/ppermute | solution.py:255
  52.0 9.2 %dft.3 = (bf16[24,1792]{1,0:T(8,128)(2,1)}, bf16[24,1792]{1,0:T(8,128)(2,1)}, bf16[24,1792]{1,0:T(8,128)(2,1)}, bf16[24,1792]{1,0:T(8,128)(2,1)}, bf16[24,1792]{...) custom-call(s32[2]{0:T(128)} %copy-done.22, ...), custom_call_target="tpu_custom_call" | custom-call | tf_op jit(solution)/shard_map/dft/pallas_call | solution.py:113
  61.9 1.7 %collective-permute-start.6 = (bf16[24,1792]{1,0:T(8,128)(2,1)S(1)}, bf16[24,1792]{1,0:T(8,128)(2,1)S(1)}, u32[]{:S(2)}, u32[]{:S(2)}) collective-permute-start(bf16[24,1792]{1,0:T(8,128)(2,1)S(1)} %get-tuple-element.27), channel_id=1, source_target_pairs={{0,7},{1,6},{2,5},{3,4},{4,3},{5,2},{6,1},{7,0},{8,15},{9,14},{10,... | collective-permute-start | bytes 258056 | tf_op jit(solution)/shard_map/ppermute | solution.py:255
  65.3 4.4 %collective-permute-done.6.rest_7_ = bf16[24,1792]{1,0:T(8,128)(2,1)S(1)} collective-permute-done((bf16[24,1792]{1,0:T(8,128)(2,1)S(1)}, bf16[24,1792]{1,0:T(8,128)(2,1)S(1)}, u32[]{:S(2)}, u32[]{:S(2)}) %collective-permute-start.6) | collective-permute-done | bytes 86048 | tf_op jit(solution)/shard_map/ppermute | solution.py:255
  71.0 1.7 %collective-permute-start.13 = (bf16[24,1792]{1,0:T(8,128)(2,1)}, bf16[24,1792]{1,0:T(8,128)(2,1)}, u32[]{:S(2)}, u32[]{:S(2)}) collective-permute-start(bf16[24,1792]{1,0:T(8,128)(2,1)} %get-tuple-element.32), channel_id=1, source_target_pairs={{0,4},{1,5},{2,6},{3,7},{4,0},{5,1},{6,2},{7,3},{8,12},{9,13},{10,... | collective-permute-start | bytes 258056 | tf_op jit(solution)/shard_map/ppermute | solution.py:255
  74.3 2.6 %collective-permute-start.15 = (bf16[24,1792]{1,0:T(8,128)(2,1)}, bf16[24,1792]{1,0:T(8,128)(2,1)}, u32[]{:S(2)}, u32[]{:S(2)}) collective-permute-start(bf16[24,1792]{1,0:T(8,128)(2,1)} %get-tuple-element.34), channel_id=1, source_target_pairs={{0,6},{1,7},{2,4},{3,5},{4,2},{5,3},{6,0},{7,1},{8,14},{9,15},{10,... | collective-permute-start | bytes 258056 | tf_op jit(solution)/shard_map/ppermute | solution.py:255
  76.9 2.4 %collective-permute-start.16 = (bf16[24,1792]{1,0:T(8,128)(2,1)}, bf16[24,1792]{1,0:T(8,128)(2,1)}, u32[]{:S(2)}, u32[]{:S(2)}) collective-permute-start(bf16[24,1792]{1,0:T(8,128)(2,1)} %get-tuple-element.35), channel_id=1, source_target_pairs={{0,7},{1,6},{2,5},{3,4},{4,3},{5,2},{6,1},{7,0},{8,15},{9,14},{10,... | collective-permute-start | bytes 258056 | tf_op jit(solution)/shard_map/ppermute | solution.py:255
  84.6 3.5 %legendre.2 = f32[60,8,128]{2,1,0:T(8,128)S(1)} custom-call(s32[2]{0:T(128)S(1)} %copy-done.23, bf16[24,1792]{1,0:T(8,128)(2,1)S(1)} %get-tuple-element.20.rest_0_, bf16[24,1792]{1,0:T(8,128)(2,1)S(1)} %collective-permute-done.rest_1_, bf16[24,1792]{1,0:T(8,128)(2,1)S(1)} %copy-done.6, bf16[24,1792]{1,0:T(8,128)(2,1)S(1)} %copy-done.8, ...), custom_call_target="tpu_custom_call" | custom-call | tf_op jit(solution)/shard_map/legendre/pallas_call | solution.py:202
  88.2 3.7 %legendre.3 = f32[60,8,128]{2,1,0:T(8,128)S(1)} custom-call(s32[2]{0:T(128)S(1)} %copy-done.23, bf16[24,1792]{1,0:T(8,128)(2,1)S(1)} %copy-done.9, bf16[24,1792]{1,0:T(8,128)(2,1)S(1)} %copy-done.15, bf16[24,1792]{1,0:T(8,128)(2,1)S(1)} %copy-done.19, bf16[24,1792]{1,0:T(8,128)(2,1)} %collective-permute-done.12.rest_3_, ...), custom_call_target="tpu_custom_call" | custom-call | tf_op jit(solution)/shard_map/legendre/pallas_call | solution.py:202
  92.5 1.5 %collective-permute-done.17 = f32[60,8,128]{2,1,0:T(8,128)S(1)} collective-permute-done((f32[60,8,128]{2,1,0:T(8,128)S(1)}, f32[60,8,128]{2,1,0:T(8,128)S(1)}, u32[]{:S(2)}, u32[]{:S(2)}) %collective-permute-start.17) | collective-permute-done | bytes 245792 | tf_op jit(solution)/shard_map/ppermute | solution.py:255
  95.0 1.6 %collective-permute-start.18 = (f32[30,8,128]{2,1,0:T(8,128)S(1)}, f32[30,8,128]{2,1,0:T(8,128)S(1)}, u32[]{:S(2)}, u32[]{:S(2)}) collective-permute-start(f32[30,8,128]{2,1,0:T(8,128)S(1)} %slice_select_fusion), channel_id=1, source_target_pairs={{0,16},{8,24},{16,0},{24,8},{1,17},{9,25},{17,1},{25,9},{2,18},{10... | collective-permute-start | bytes 368648 | tf_op jit(solution)/shard_map/ppermute | solution.py:255
  96.6 3.9 %collective-permute-done.18 = f32[30,8,128]{2,1,0:T(8,128)S(1)} collective-permute-done((f32[30,8,128]{2,1,0:T(8,128)S(1)}, f32[30,8,128]{2,1,0:T(8,128)S(1)}, u32[]{:S(2)}, u32[]{:S(2)}) %collective-permute-start.18) | collective-permute-done | bytes 122912 | tf_op jit(solution)/shard_map/ppermute | solution.py:255
  100.9 4.6 %collective-permute-done.19 = f32[30,8,128]{2,1,0:T(8,128)S(1)} collective-permute-done((f32[30,8,128]{2,1,0:T(8,128)S(1)}, f32[30,8,128]{2,1,0:T(8,128)S(1)}, u32[]{:S(2)}, u32[]{:S(2)}) %collective-permute-start.19) | collective-permute-done | bytes 122912 | tf_op jit(solution)/shard_map/ppermute | solution.py:255
  105.5 1.5 %collective-permute-start.20 = (f32[30,8,128]{2,1,0:T(8,128)S(1)}, f32[30,8,128]{2,1,0:T(8,128)S(1)}, u32[]{:S(2)}, u32[]{:S(2)}) collective-permute-start(f32[30,8,128]{2,1,0:T(8,128)S(1)} %add.31), channel_id=1, source_target_pairs={{0,6},{1,7},{2,4},{3,5},{4,2},{5,3},{6,0},{7,1},{8,14},{9,15},{10,... | collective-permute-start | bytes 368648 | tf_op jit(solution)/shard_map/ppermute | solution.py:255
  107.5 2.4 %collective-permute-start.22 = (f32[30,8,128]{2,1,0:T(8,128)S(1)}, f32[30,8,128]{2,1,0:T(8,128)S(1)}, u32[]{:S(2)}, u32[]{:S(2)}) collective-permute-start(f32[30,8,128]{2,1,0:T(8,128)S(1)} %add.31), channel_id=1, source_target_pairs={{0,2},{1,3},{2,0},{3,1},{4,6},{5,7},{6,4},{7,5},{8,10},{9,11},{10,... | collective-permute-start | bytes 368648 | tf_op jit(solution)/shard_map/ppermute | solution.py:255
  109.9 3.4 %collective-permute-done.20 = f32[30,8,128]{2,1,0:T(8,128)S(1)} collective-permute-done((f32[30,8,128]{2,1,0:T(8,128)S(1)}, f32[30,8,128]{2,1,0:T(8,128)S(1)}, u32[]{:S(2)}, u32[]{:S(2)}) %collective-permute-start.20) | collective-permute-done | bytes 122912 | tf_op jit(solution)/shard_map/ppermute | solution.py:255
  113.4 3.9 %collective-permute-done.21 = f32[30,8,128]{2,1,0:T(8,128)S(1)} collective-permute-done((f32[30,8,128]{2,1,0:T(8,128)S(1)}, f32[30,8,128]{2,1,0:T(8,128)S(1)}, u32[]{:S(2)}, u32[]{:S(2)}) %collective-permute-start.21) | collective-permute-done | bytes 122912 | tf_op jit(solution)/shard_map/ppermute | solution.py:255
  117.3 1.6 %collective-permute-start.23 = (f32[30,8,128]{2,1,0:T(8,128)S(1)}, f32[30,8,128]{2,1,0:T(8,128)S(1)}, u32[]{:S(2)}, u32[]{:S(2)}) collective-permute-start(f32[30,8,128]{2,1,0:T(8,128)S(1)} %add_add_fusion), channel_id=1, source_target_pairs={{0,16},{8,24},{16,0},{24,8},{1,17},{9,25},{17,1},{25,9},{2,18},{10... | collective-permute-start | bytes 368648 | tf_op jit(solution)/shard_map/ppermute | solution.py:255
  118.9 3.4 %collective-permute-done.23 = f32[30,8,128]{2,1,0:T(8,128)S(1)} collective-permute-done((f32[30,8,128]{2,1,0:T(8,128)S(1)}, f32[30,8,128]{2,1,0:T(8,128)S(1)}, u32[]{:S(2)}, u32[]{:S(2)}) %collective-permute-start.23) | collective-permute-done | bytes 122912 | tf_op jit(solution)/shard_map/ppermute | solution.py:255
  122.3 1.5 %collective-permute-done.24 = f32[60,8,128]{2,1,0:T(8,128)S(1)} collective-permute-done((f32[60,8,128]{2,1,0:T(8,128)S(1)}, f32[60,8,128]{2,1,0:T(8,128)S(1)}, u32[]{:S(2)}, u32[]{:S(2)}) %collective-permute-start.24) | collective-permute-done | bytes 245792 | tf_op jit(solution)/shard_map/ppermute | solution.py:255
  124.6 1.1 copy.6
  (82 shorter events, 15.8 us)
Async XLA Ops:
  2.2 27.4 %collective-permute-start.7 = (bf16[3,720,256]{2,1,0:T(8,128)(2,1)S(1)}, bf16[3,720,256]{2,1,0:T(8,128)(2,1)S(1)}, u32[]{:S(2)}, u32[]{:S(2)}) collective-permute-start(bf16[3,720,256]{2,1,0:T(8,128)(2,1)S(1)} %turn.1.rest_8_), channel_id=1, source_target_pairs={{0,16},{8,24},{16,0},{24,8},{1,17},{9,25},{17,1},{25,9},{2,18},{10... | collective-permute-start | bytes 3317768 | tf_op jit(solution)/shard_map/ppermute | solution.py:255
  5.2 69.1 %collective-permute-start.8 = (bf16[3,720,256]{2,1,0:T(8,128)(2,1)S(1)}, bf16[3,720,256]{2,1,0:T(8,128)(2,1)S(1)}, u32[]{:S(2)}, u32[]{:S(2)}) collective-permute-start(bf16[3,720,256]{2,1,0:T(8,128)(2,1)S(1)} %turn.1.rest_8_), channel_id=1, source_target_pairs={{0,8},{8,0},{16,24},{24,16},{1,9},{9,1},{17,25},{25,17},{2,10},{10... | collective-permute-start | bytes 3317768 | tf_op jit(solution)/shard_map/ppermute | solution.py:255
  29.6 47.3 %collective-permute-start.9 = (bf16[3,720,256]{2,1,0:T(8,128)(2,1)S(1)}, bf16[3,720,256]{2,1,0:T(8,128)(2,1)}, u32[]{:S(2)}, u32[]{:S(2)}) collective-permute-start(bf16[3,720,256]{2,1,0:T(8,128)(2,1)S(1)} %collective-permute-done.7.rest_9_), channel_id=1, source_target_pairs={{0,8},{8,0},{16,24},{24,16},{1,9},{9,1},{17,25},{25,17},{2,10},{10... | collective-permute-start | bytes 3317768 | tf_op jit(solution)/shard_map/ppermute | solution.py:255
  29.7 8.4 %copy-start.22 = (s32[2]{0:T(128)}, s32[2]{0:T(128)S(1)}, u32[]{:S(2)}) copy-start(s32[2]{0:T(128)S(1)} %pad_add_fusion.place) | copy-start | bytes 28
  29.7 2.5 %copy-start = (bf16[1,73,24,1440]{3,2,1,0:T(8,128)(2,1)S(1)}, bf16[1,73,24,1440]{3,2,1,0:T(8,128)(2,1)}, u32[]{:S(2)}) copy-start(bf16[1,73,24,1440]{3,2,1,0:T(8,128)(2,1)} %param.5) | copy-start | bytes 15137284
  38.0 5.0 %collective-permute-start = (bf16[24,1792]{1,0:T(8,128)(2,1)S(1)}, bf16[24,1792]{1,0:T(8,128)(2,1)S(1)}, u32[]{:S(2)}, u32[]{:S(2)}) collective-permute-start(bf16[24,1792]{1,0:T(8,128)(2,1)S(1)} %get-tuple-element.21), channel_id=1, source_target_pairs={{0,1},{1,0},{2,3},{3,2},{4,5},{5,4},{6,7},{7,6},{8,9},{9,8},{10,11... | collective-permute-start | bytes 258056 | tf_op jit(solution)/shard_map/ppermute | solution.py:255
  39.9 6.0 %collective-permute-start.1 = (bf16[24,1792]{1,0:T(8,128)(2,1)S(1)}, bf16[24,1792]{1,0:T(8,128)(2,1)S(1)}, u32[]{:S(2)}, u32[]{:S(2)}) collective-permute-start(bf16[24,1792]{1,0:T(8,128)(2,1)S(1)} %get-tuple-element.22), channel_id=1, source_target_pairs={{0,2},{1,3},{2,0},{3,1},{4,6},{5,7},{6,4},{7,5},{8,10},{9,11},{10,... | collective-permute-start | bytes 258056 | tf_op jit(solution)/shard_map/ppermute | solution.py:255
  41.4 6.4 %collective-permute-start.2 = (bf16[24,1792]{1,0:T(8,128)(2,1)S(1)}, bf16[24,1792]{1,0:T(8,128)(2,1)S(1)}, u32[]{:S(2)}, u32[]{:S(2)}) collective-permute-start(bf16[24,1792]{1,0:T(8,128)(2,1)S(1)} %get-tuple-element.23), channel_id=1, source_target_pairs={{0,3},{1,2},{2,1},{3,0},{4,7},{5,6},{6,5},{7,4},{8,11},{9,10},{10,... | collective-permute-start | bytes 258056 | tf_op jit(solution)/shard_map/ppermute | solution.py:255
  43.1 18.2 %collective-permute-start.3 = (bf16[24,1792]{1,0:T(8,128)(2,1)S(1)}, bf16[24,1792]{1,0:T(8,128)(2,1)S(1)}, u32[]{:S(2)}, u32[]{:S(2)}) collective-permute-start(bf16[24,1792]{1,0:T(8,128)(2,1)S(1)} %get-tuple-element.24), channel_id=1, source_target_pairs={{0,4},{1,5},{2,6},{3,7},{4,0},{5,1},{6,2},{7,3},{8,12},{9,13},{10,... | collective-permute-start | bytes 258056 | tf_op jit(solution)/shard_map/ppermute | solution.py:255
  46.5 17.1 %collective-permute-start.4 = (bf16[24,1792]{1,0:T(8,128)(2,1)S(1)}, bf16[24,1792]{1,0:T(8,128)(2,1)S(1)}, u32[]{:S(2)}, u32[]{:S(2)}) collective-permute-start(bf16[24,1792]{1,0:T(8,128)(2,1)S(1)} %get-tuple-element.25), channel_id=1, source_target_pairs={{0,5},{1,4},{2,7},{3,6},{4,1},{5,0},{6,3},{7,2},{8,13},{9,12},{10,... | collective-permute-start | bytes 258056 | tf_op jit(solution)/shard_map/ppermute | solution.py:255
  48.4 15.8 %collective-permute-start.5 = (bf16[24,1792]{1,0:T(8,128)(2,1)S(1)}, bf16[24,1792]{1,0:T(8,128)(2,1)S(1)}, u32[]{:S(2)}, u32[]{:S(2)}) collective-permute-start(bf16[24,1792]{1,0:T(8,128)(2,1)S(1)} %get-tuple-element.26), channel_id=1, source_target_pairs={{0,6},{1,7},{2,4},{3,5},{4,2},{5,3},{6,0},{7,1},{8,14},{9,15},{10,... | collective-permute-start | bytes 258056 | tf_op jit(solution)/shard_map/ppermute | solution.py:255
  52.0 27.2 %copy-start.23 = (s32[2]{0:T(128)S(1)}, s32[2]{0:T(128)}, u32[]{:S(2)}) copy-start(s32[2]{0:T(128)} %copy-done.22) | copy-start | bytes 28
  61.9 7.8 %collective-permute-start.6 = (bf16[24,1792]{1,0:T(8,128)(2,1)S(1)}, bf16[24,1792]{1,0:T(8,128)(2,1)S(1)}, u32[]{:S(2)}, u32[]{:S(2)}) collective-permute-start(bf16[24,1792]{1,0:T(8,128)(2,1)S(1)} %get-tuple-element.27), channel_id=1, source_target_pairs={{0,7},{1,6},{2,5},{3,4},{4,3},{5,2},{6,1},{7,0},{8,15},{9,14},{10,... | collective-permute-start | bytes 258056 | tf_op jit(solution)/shard_map/ppermute | solution.py:255
  64.2 6.1 %collective-permute-start.10 = (bf16[24,1792]{1,0:T(8,128)(2,1)}, bf16[24,1792]{1,0:T(8,128)(2,1)S(1)}, u32[]{:S(2)}, u32[]{:S(2)}) collective-permute-start(bf16[24,1792]{1,0:T(8,128)(2,1)} %get-tuple-element.29), channel_id=1, source_target_pairs={{0,1},{1,0},{2,3},{3,2},{4,5},{5,4},{6,7},{7,6},{8,9},{9,8},{10,11... | collective-permute-start | bytes 258056 | tf_op jit(solution)/shard_map/ppermute | solution.py:255
  64.9 7.8 %collective-permute-start.11 = (bf16[24,1792]{1,0:T(8,128)(2,1)}, bf16[24,1792]{1,0:T(8,128)(2,1)S(1)}, u32[]{:S(2)}, u32[]{:S(2)}) collective-permute-start(bf16[24,1792]{1,0:T(8,128)(2,1)} %get-tuple-element.30), channel_id=1, source_target_pairs={{0,2},{1,3},{2,0},{3,1},{4,6},{5,7},{6,4},{7,5},{8,10},{9,11},{10,... | collective-permute-start | bytes 258056 | tf_op jit(solution)/shard_map/ppermute | solution.py:255
  70.3 17.8 %collective-permute-start.12 = (bf16[24,1792]{1,0:T(8,128)(2,1)}, bf16[24,1792]{1,0:T(8,128)(2,1)}, u32[]{:S(2)}, u32[]{:S(2)}) collective-permute-start(bf16[24,1792]{1,0:T(8,128)(2,1)} %get-tuple-element.31), channel_id=1, source_target_pairs={{0,3},{1,2},{2,1},{3,0},{4,7},{5,6},{6,5},{7,4},{8,11},{9,10},{10,... | collective-permute-start | bytes 258056 | tf_op jit(solution)/shard_map/ppermute | solution.py:255
  71.0 17.1 %collective-permute-start.13 = (bf16[24,1792]{1,0:T(8,128)(2,1)}, bf16[24,1792]{1,0:T(8,128)(2,1)}, u32[]{:S(2)}, u32[]{:S(2)}) collective-permute-start(bf16[24,1792]{1,0:T(8,128)(2,1)} %get-tuple-element.32), channel_id=1, source_target_pairs={{0,4},{1,5},{2,6},{3,7},{4,0},{5,1},{6,2},{7,3},{8,12},{9,13},{10,... | collective-permute-start | bytes 258056 | tf_op jit(solution)/shard_map/ppermute | solution.py:255
  73.3 14.8 %collective-permute-start.14 = (bf16[24,1792]{1,0:T(8,128)(2,1)}, bf16[24,1792]{1,0:T(8,128)(2,1)}, u32[]{:S(2)}, u32[]{:S(2)}) collective-permute-start(bf16[24,1792]{1,0:T(8,128)(2,1)} %get-tuple-element.33), channel_id=1, source_target_pairs={{0,5},{1,4},{2,7},{3,6},{4,1},{5,0},{6,3},{7,2},{8,13},{9,12},{10,... | collective-permute-start | bytes 258056 | tf_op jit(solution)/shard_map/ppermute | solution.py:255
  74.3 13.8 %collective-permute-start.15 = (bf16[24,1792]{1,0:T(8,128)(2,1)}, bf16[24,1792]{1,0:T(8,128)(2,1)}, u32[]{:S(2)}, u32[]{:S(2)}) collective-permute-start(bf16[24,1792]{1,0:T(8,128)(2,1)} %get-tuple-element.34), channel_id=1, source_target_pairs={{0,6},{1,7},{2,4},{3,5},{4,2},{5,3},{6,0},{7,1},{8,14},{9,15},{10,... | collective-permute-start | bytes 258056 | tf_op jit(solution)/shard_map/ppermute | solution.py:255
  76.9 11.2 %collective-permute-start.16 = (bf16[24,1792]{1,0:T(8,128)(2,1)}, bf16[24,1792]{1,0:T(8,128)(2,1)}, u32[]{:S(2)}, u32[]{:S(2)}) collective-permute-start(bf16[24,1792]{1,0:T(8,128)(2,1)} %get-tuple-element.35), channel_id=1, source_target_pairs={{0,7},{1,6},{2,5},{3,4},{4,3},{5,2},{6,1},{7,0},{8,15},{9,14},{10,... | collective-permute-start | bytes 258056 | tf_op jit(solution)/shard_map/ppermute | solution.py:255
  84.6 3.5 %copy-start.9 = (bf16[24,1792]{1,0:T(8,128)(2,1)S(1)}, bf16[24,1792]{1,0:T(8,128)(2,1)}, u32[]{:S(2)}) copy-start(bf16[24,1792]{1,0:T(8,128)(2,1)} %get-tuple-element.28.rest_0_) | copy-start | bytes 258052
  84.6 3.5 %copy-start.15 = (bf16[24,1792]{1,0:T(8,128)(2,1)S(1)}, bf16[24,1792]{1,0:T(8,128)(2,1)}, u32[]{:S(2)}) copy-start(bf16[24,1792]{1,0:T(8,128)(2,1)} %copy-done.14) | copy-start | bytes 258052
  84.6 3.6 %copy-start.19 = (bf16[24,1792]{1,0:T(8,128)(2,1)S(1)}, bf16[24,1792]{1,0:T(8,128)(2,1)}, u32[]{:S(2)}) copy-start(bf16[24,1792]{1,0:T(8,128)(2,1)} %copy-done.18) | copy-start | bytes 258052
  88.1 3.8 %copy-start.2 = (f32[60,8,128]{2,1,0:T(8,128)}, f32[60,8,128]{2,1,0:T(8,128)S(1)}, u32[]{:S(2)}) copy-start(f32[60,8,128]{2,1,0:T(8,128)S(1)} %legendre.2) | copy-start | bytes 737284
  92.5 1.5 %collective-permute-start.17 = (f32[60,8,128]{2,1,0:T(8,128)S(1)}, f32[60,8,128]{2,1,0:T(8,128)S(1)}, u32[]{:S(2)}, u32[]{:S(2)}) collective-permute-start(f32[60,8,128]{2,1,0:T(8,128)S(1)} %broadcast_select_fusion), channel_id=1, source_target_pairs={{0,8},{8,0},{16,24},{24,16},{1,9},{9,1},{17,25},{25,17},{2,10},{10... | collective-permute-start | bytes 737288 | tf_op jit(solution)/shard_map/ppermute | solution.py:255
  95.0 5.4 %collective-permute-start.18 = (f32[30,8,128]{2,1,0:T(8,128)S(1)}, f32[30,8,128]{2,1,0:T(8,128)S(1)}, u32[]{:S(2)}, u32[]{:S(2)}) collective-permute-start(f32[30,8,128]{2,1,0:T(8,128)S(1)} %slice_select_fusion), channel_id=1, source_target_pairs={{0,16},{8,24},{16,0},{24,8},{1,17},{9,25},{17,1},{25,9},{2,18},{10... | collective-permute-start | bytes 368648 | tf_op jit(solution)/shard_map/ppermute | solution.py:255
  100.5 4.9 %collective-permute-start.19 = (f32[30,8,128]{2,1,0:T(8,128)S(1)}, f32[30,8,128]{2,1,0:T(8,128)S(1)}, u32[]{:S(2)}, u32[]{:S(2)}) collective-permute-start(f32[30,8,128]{2,1,0:T(8,128)S(1)} %select_add_fusion.1), channel_id=1, source_target_pairs={{0,1},{1,0},{2,3},{3,2},{4,5},{5,4},{6,7},{7,6},{8,9},{9,8},{10,11... | collective-permute-start | bytes 368648 | tf_op jit(solution)/shard_map/ppermute | solution.py:255
  105.5 7.9 %collective-permute-start.20 = (f32[30,8,128]{2,1,0:T(8,128)S(1)}, f32[30,8,128]{2,1,0:T(8,128)S(1)}, u32[]{:S(2)}, u32[]{:S(2)}) collective-permute-start(f32[30,8,128]{2,1,0:T(8,128)S(1)} %add.31), channel_id=1, source_target_pairs={{0,6},{1,7},{2,4},{3,5},{4,2},{5,3},{6,0},{7,1},{8,14},{9,15},{10,... | collective-permute-start | bytes 368648 | tf_op jit(solution)/shard_map/ppermute | solution.py:255
  107.0 10.3 %collective-permute-start.21 = (f32[30,8,128]{2,1,0:T(8,128)S(1)}, f32[30,8,128]{2,1,0:T(8,128)S(1)}, u32[]{:S(2)}, u32[]{:S(2)}) collective-permute-start(f32[30,8,128]{2,1,0:T(8,128)S(1)} %add.31), channel_id=1, source_target_pairs={{0,4},{1,5},{2,6},{3,7},{4,0},{5,1},{6,2},{7,3},{8,12},{9,13},{10,... | collective-permute-start | bytes 368648 | tf_op jit(solution)/shard_map/ppermute | solution.py:255
  107.5 9.8 %collective-permute-start.22 = (f32[30,8,128]{2,1,0:T(8,128)S(1)}, f32[30,8,128]{2,1,0:T(8,128)S(1)}, u32[]{:S(2)}, u32[]{:S(2)}) collective-permute-start(f32[30,8,128]{2,1,0:T(8,128)S(1)} %add.31), channel_id=1, source_target_pairs={{0,2},{1,3},{2,0},{3,1},{4,6},{5,7},{6,4},{7,5},{8,10},{9,11},{10,... | collective-permute-start | bytes 368648 | tf_op jit(solution)/shard_map/ppermute | solution.py:255
  117.3 4.9 %collective-permute-start.23 = (f32[30,8,128]{2,1,0:T(8,128)S(1)}, f32[30,8,128]{2,1,0:T(8,128)S(1)}, u32[]{:S(2)}, u32[]{:S(2)}) collective-permute-start(f32[30,8,128]{2,1,0:T(8,128)S(1)} %add_add_fusion), channel_id=1, source_target_pairs={{0,16},{8,24},{16,0},{24,8},{1,17},{9,25},{17,1},{25,9},{2,18},{10... | collective-permute-start | bytes 368648 | tf_op jit(solution)/shard_map/ppermute | solution.py:255
  122.3 1.6 %collective-permute-start.24 = (f32[60,8,128]{2,1,0:T(8,128)S(1)}, f32[60,8,128]{2,1,0:T(8,128)S(1)}, u32[]{:S(2)}, u32[]{:S(2)}) collective-permute-start(f32[60,8,128]{2,1,0:T(8,128)S(1)} %maximum_select_fusion.1), channel_id=1, source_target_pairs={{0,8},{8,0},{16,24},{24,16},{1,9},{9,1},{17,25},{25,17},{2,10},{10... | collective-permute-start | bytes 737288 | tf_op jit(solution)/shard_map/ppermute | solution.py:255
  (17 other events, 13.4 us)

commit v3 on v2

--- a/solution.py
+++ b/solution.py
@@ -13,7 +13,6 @@
 LANES = 128
 VMEM_LIMIT = 24 * 1024 * 1024
 STAGED_LIMIT = 59 * 1024 * 1024
-SPARE_VMEM = 16 * 1024 * 1024
 
 
 def round_up(value, step):
@@ -50,26 +49,27 @@
     return lax.rem(index + count - step, count)
 
 
-def dft_kernel(bands, per, chans, lats, chunks, staged, place, field, table, *rest):
+def dft_kernel(bands, per, chans, lats, chunks, joined, field, table_hbm, *rest):
+    near = bands // 2 - 1 if joined else 0
+    before, rest = rest[:near], rest[near:]
     outs = rest[:bands]
-    dscr, turned, packed = rest[bands : bands + 3]
+    dscr, turned, packed, xbuf, table, sems = rest[bands:]
+    load = pltpu.make_async_copy(table_hbm, table, sems.at[len(chunks)])
+    load.start()
     copies = []
     row = 0
-    xbuf = rest[bands + 3] if staged else field
     for i, rows in enumerate(chunks):
-        cp = None
-        if staged:
-            cp = pltpu.make_async_copy(
-                field.at[pl.ds(row, rows), :], xbuf.at[pl.ds(row, rows), :], rest[-1].at[i]
-            )
-            cp.start()
+        cp = pltpu.make_async_copy(
+            field.at[pl.ds(row, rows), :], xbuf.at[pl.ds(row, rows), :], sems.at[i]
+        )
+        cp.start()
         copies.append((row, rows, cp))
         row += rows
-    band = place[0]
+    band = lax.axis_index("lat")
     tiles = dscr.shape[0]
+    load.wait()
     for row, rows, cp in copies:
-        if staged:
-            cp.wait()
+        cp.wait()
         res = jnp.dot(xbuf[pl.ds(row, rows), :], table[...], preferred_element_type=jnp.float32)
         for q in range(tiles):
             dscr[q, pl.ds(row, rows), :] = res[:, q * LANES : (q + 1) * LANES]
@@ -92,76 +92,85 @@
             ]
         return carry
 
-    lax.fori_loop(0, bands, pack, 0)
+    lax.fori_loop(0, bands, pack, 0, unroll=min(bands, 8))
     for s in range(bands):
-        outs[s][...] = packed[s].astype(jnp.bfloat16)
-
-
-def dft_blocks(place, field, table, bands, per, chans, lats, staged):
+        if 0 < s <= near:
+            outs[s][0] = before[s - 1][...]
+            outs[s][1] = packed[s].astype(jnp.bfloat16)
+        else:
+            outs[s][...] = packed[s].astype(jnp.bfloat16)
+
+
+def dft_blocks(field, table, before, bands, per, chans, lats):
     rows_all, lon_count = field.shape
     width = round_up(per * chans, LANES)
-    step = -(-chans // 4) * lats
+    step = -(-chans // 3) * lats
     chunks = []
     left = rows_all
     while left > 0:
         chunks.append(min(step, left))
         left -= step
     columns = table.shape[1]
-    held = 4 * lats * (2 * columns * LANES + bands * width)
     anywhere = pl.BlockSpec(memory_space=pl.ANY)
     vmem = pl.BlockSpec(memory_space=pltpu.VMEM)
+    one, two = ((2,) * k + (lats, width) for k in (0, 1))
+    out_shape = [
+        jax.ShapeDtypeStruct(two if 0 < s <= len(before) else one, jnp.bfloat16)
+        for s in range(bands)
+    ]
+    args = [field, table, *before]
     return pl.pallas_call(
-        functools.partial(dft_kernel, bands, per, chans, lats, tuple(chunks), staged),
-        out_shape=[jax.ShapeDtypeStruct((lats, width), jnp.bfloat16)] * bands,
-        in_specs=[pl.BlockSpec(memory_space=pltpu.SMEM), anywhere if staged else vmem, vmem],
-        out_specs=[vmem] * bands,
+        functools.partial(dft_kernel, bands, per, chans, lats, tuple(chunks), bool(before)),
+        out_shape=out_shape,
+        in_specs=[anywhere, anywhere] + [vmem] * (len(args) - 2),
+        out_specs=[vmem] * len(out_shape),
         scratch_shapes=[
             pltpu.VMEM((columns // LANES, LANES * lats, LANES), jnp.float32),
             pltpu.VMEM((columns // LANES, LANES * lats, LANES), jnp.float32),
             pltpu.VMEM((bands, lats, width), jnp.float32),
-        ]
-        + (
-            [
-                pltpu.VMEM((rows_all, lon_count), jnp.bfloat16),
-                pltpu.SemaphoreType.DMA((len(chunks),)),
-            ]
-            if staged
-            else []
-        ),
-        compiler_params=pltpu.CompilerParams(
-            vmem_limit_bytes=STAGED_LIMIT if staged else SPARE_VMEM + held
-        ),
+            pltpu.VMEM((rows_all, lon_count), jnp.bfloat16),
+            pltpu.VMEM(table.shape, jnp.bfloat16),
+            pltpu.SemaphoreType.DMA((len(chunks) + 1,)),
+        ],
+        compiler_params=pltpu.CompilerParams(vmem_limit_bytes=STAGED_LIMIT),
         name="dft",
-    )(place, field, table)
-
-
-def turn_kernel(basis, out):
-    for o in range(basis.shape[0]):
-        out[o, :, : basis.shape[1]] = basis[o].T
-
-
-def turned_basis(basis):
-    per_dev, lat_count, degrees = basis.shape
+    )(*args)
+
+
+def turn_kernel(count, *refs):
+    for basis, out in zip(refs[:count], refs[count:]):
+        for o in range(basis.shape[0]):
+            out[o, :, : basis.shape[1]] = basis[o].T
+
+
+def turned_bases(bases):
+    per_dev, lat_count, degrees = bases[0].shape
+    shape = (per_dev, degrees, round_up(lat_count, LANES))
     return pl.pallas_call(
-        turn_kernel,
-        out_shape=jax.ShapeDtypeStruct((per_dev, degrees, round_up(lat_count, LANES)), basis.dtype),
+        functools.partial(turn_kernel, len(bases)),
+        out_shape=[jax.ShapeDtypeStruct(shape, bases[0].dtype)] * len(bases),
         compiler_params=pltpu.CompilerParams(vmem_limit_bytes=VMEM_LIMIT),
         name="turn",
-    )(basis)
-
-
-def legendre_kernel(bands, groups, per_dev, chans, lats, slots, place, *rest):
+    )(*bases)
+
+
+def legendre_kernel(bands, groups, per_dev, chans, lats, slots, field, *rest):
     blocks = rest[:bands]
     bases = rest[bands : bands + groups]
-    out = rest[bands + groups]
-    fourier, columns, total = rest[bands + groups + 1 :]
-    band, group = place[0], place[1]
+    rest = rest[bands + groups :]
+    fourier, columns, total = rest[-3:]
+    if field == 0:
+        out = rest[0]
+    else:
+        energy_before, kept, sent, out = rest[0], rest[1], rest[2], rest[3]
+    band, group = lax.axis_index("lat"), lax.axis_index("batch")
     degrees = bases[0].shape[1]
     depth = bands * lats
     width = 2 * chans
     for s in range(bands):
         row = pl.multiple_of(source_of(band, bands, s) * lats, 8)
-        fourier[pl.ds(row, lats), :] = blocks[s][...].astype(jnp.float32)
+        block = blocks[s][...] if len(blocks[s].shape) == 2 else blocks[s][field]
+        fourier[pl.ds(row, lats), :] = block.astype(jnp.float32)
     for i in range(groups * per_dev):
         columns[i] = fourier[:, pl.ds(i * width, width)].astype(jnp.bfloat16)
     for q in range(groups):
@@ -191,27 +200,33 @@
         piece = flat[k * LANES : (k + 1) * LANES, :].T
         for r in range(row_tiles):
             out[r * lane_tiles + k] = piece[r * 8 : (r + 1) * 8, :]
-
-
-def legendre_energy(place, blocks, bases, slots, chans, lats):
+    if field == 1:
+        high = lax.rem(group, 2) == 1
+        first, second = energy_before[...], out[...]
+        kept[...] = jnp.where(high, second, first)
+        sent[...] = jnp.where(high, first, second)
+
+
+def legendre_energy(blocks, bases, slots, chans, lats, before):
     bands, groups = len(blocks), len(bases)
     per_dev, degrees, _ = bases[0].shape
-    vmem = pl.BlockSpec(memory_space=pltpu.VMEM)
     row_tiles = round_up(chans, 8) // 8
     lane_tiles = round_up(degrees, LANES) // LANES
+    tiles = (row_tiles * lane_tiles, 8, LANES)
+    field = len(before)
+    out = jax.ShapeDtypeStruct(tiles, jnp.float32)
     return pl.pallas_call(
-        functools.partial(legendre_kernel, bands, groups, per_dev, chans, lats, slots),
-        out_shape=jax.ShapeDtypeStruct((row_tiles * lane_tiles, 8, LANES), jnp.float32),
-        in_specs=[pl.BlockSpec(memory_space=pltpu.SMEM)] + [vmem] * (bands + groups),
-        out_specs=vmem,
-        scratch_shapes=[
-            pltpu.VMEM((bands * lats, blocks[0].shape[1]), jnp.float32),
+        functools.partial(legendre_kernel, bands, groups, per_dev, chans, lats, slots, field),
+        out_shape=[out, out] if field else [out],
+        scratch_shapes=([pltpu.VMEM(tiles, jnp.float32)] if field else [])
+        + [
+            pltpu.VMEM((bands * lats, blocks[0].shape[-1]), jnp.float32),
             pltpu.VMEM((groups * per_dev, bands * lats, 2 * chans), jnp.bfloat16),
             pltpu.VMEM((degrees, round_up(2 * chans, LANES)), jnp.float32),
         ],
         compiler_params=pltpu.CompilerParams(vmem_limit_bytes=VMEM_LIMIT),
         name="legendre",
-    )(place, *blocks, *bases)
+    )(*blocks, *bases, *before)
 
 
 def loss_kernel(chans, degrees, count, blocks, spectra, loss, sums):
@@ -255,11 +270,13 @@
     return lax.ppermute(value, axis, peers(lax.axis_size(axis), step))
 
 
-def reduce_all(value):
-    halved = []
+def reduce_all(kept, sent):
     index = lax.axis_index("batch")
-    step = 1
-    while step < lax.axis_size("batch"):
+    groups = lax.axis_size("batch")
+    value = kept + exchange(sent, "batch", 1)
+    halved = [(1, index % 2 == 1)]
+    step = 2
+    while step < groups:
         if value.shape[0] % 2 == 0:
             half = value.shape[0] // 2
             high = (index // step) % 2 == 1
@@ -293,39 +310,44 @@
     per_dev = legendre_basis.shape[1]
     members, chans, lats, lon_count = predicted.shape
     degrees = legendre_basis.shape[2]
-    place = jnp.stack([lax.axis_index("lat"), lax.axis_index("batch")]).astype(jnp.int32)
     table = jnp.asarray(fourier_table(lon_count, groups, bands, per_dev))
     rows = members * chans * lats
-    fields = (predicted, target)
-    steps = list(range(bands - 1, 0, -1))
-
-    sent = []
-    for f, field in enumerate(fields):
-        flat = field.reshape(rows, lon_count)
-        sent.append(
-            dft_blocks(
-                place, flat, table, bands, groups * per_dev * 2, chans, lats, f == 0
-            )
-        )
-    arrived = []
-    for f in range(2):
-        got = {0: sent[f][0]}
-        for s in steps:
-            got[s] = exchange(sent[f][s], "lat", s)
-        arrived.append([got[s] for s in range(bands)])
-    bases = [turned_basis(jnp.transpose(legendre_basis, (1, 0, 2)))]
-    slots = [0]
+    far, near = reach(bands)
+    basis = jnp.transpose(legendre_basis, (1, 0, 2))
+    bases, slots = [basis], [0]
     step = groups // 2
     while step:
         bases = bases + [exchange(block, "batch", step) for block in bases]
         slots = slots + [slot ^ step for slot in slots]
         step //= 2
-    energies = []
-    for f in range(2):
-        energies.append(legendre_energy(place, arrived[f], bases, slots, chans, lats))
-    energy = reduce_all(jnp.concatenate(energies))
-    spectra, loss = loss_call(energy, chans, degrees, members * groups * groups * bands * per_dev)
+
+    def transform(field, before):
+        flat = field.reshape(rows, lon_count)
+        return dft_blocks(flat, table, before, bands, groups * per_dev * 2, chans, lats)
+
+    first = transform(predicted, [])
+    second = transform(target, [first[s] for s in sorted(near)])
+    got0, got1 = {0: first[0]}, {0: second[0]}
+    for s in far:
+        got0[s] = exchange(first[s], "lat", s)
+        got1[s] = exchange(second[s], "lat", s)
+    for s in near:
+        got0[s] = got1[s] = exchange(second[s], "lat", s)
+    bases = turned_bases(bases)
+    blocks = [got0[s] for s in range(bands)]
+    before = legendre_energy(blocks, bases, slots, chans, lats, [])
+    blocks = [got1[s] for s in range(bands)]
+    kept, sent = legendre_energy(blocks, bases, slots, chans, lats, before)
+    energy = reduce_all(kept, sent)
+    spectra, loss = loss_call(
+        energy, chans, degrees, members * groups * groups * bands * per_dev
+    )
     return (spectra, loss.reshape(chans))
+
+
+def reach(bands):
+    steps = range(bands - 1, 0, -1)
+    return [s for s in steps if s >= bands // 2], [s for s in steps if s < bands // 2]
 
 
 def solution(mesh):

time: 126 us -> 109 us (0.87)
  local copies, waits for them, and re-layouts: 16.9 us -> 1.13 us
  waiting for transfers between devices: 52.5 us -> 57.5 us
  starting transfers between devices: 32 us -> 27.1 us
    unnamed x49 -> x9, local copies, waits for them, and re-layouts: 16.9 us -> 1.13 us
    ppermute x25 -> x22, waiting for transfers between devices: 52.5 us -> 57.5 us  [exchange(): return lax.ppermute(value, axis, peers(lax.axis_size(axis), step))]
    ppermute x25 -> x22, starting transfers between devices: 32 us -> 27.1 us  [exchange(): return lax.ppermute(value, axis, peers(lax.axis_size(axis), step))]
    pallas_call x2, Pallas kernels: 7.12 us -> 4.2 us  [legendre_energy(): pl.pallas_call(functools.partial(legendre_kernel, bands, groups, per_dev,...]
    pallas_call x2, Pallas kernels: 14 us -> 16.3 us  [dft_blocks(): pl.pallas_call(functools.partial(dft_kernel, bands, per, chans, lats, tup...]
  transfers between devices with their start and end apart: 25 -> 22, of which waited for: 10 -> 13; matrix products, arithmetic and copies ran while one was open for 0% -> 0% of each run, Pallas kernels for 14% -> 18%
where the time goes in v3:
time: 109 us
  waiting for transfers between devices  57.5 us (53%)
  starting transfers between devices  27.1 us (25%)
  Pallas kernels  22.4 us (21%)
  local copies, waits for them, and re-layouts  1.13 us (1%)
    ppermute x22, waiting for transfers between devices, exchange(): return lax.ppermute(value, axis, peers(lax.axis_size(axis), step))  57.5 us
    ppermute x22, starting transfers between devices, exchange(): return lax.ppermute(value, axis, peers(lax.axis_size(axis), step))  27.1 us
    pallas_call x2, Pallas kernels, dft_blocks(): pl.pallas_call(functools.partial(dft_kernel, bands, per, chans, lats, tup...  16.3 us
    pallas_call x2, Pallas kernels, legendre_energy(): pl.pallas_call(functools.partial(legendre_kernel, bands, groups, per_dev,...  4.2 us
  transfers between devices with their start and end apart: 22, of which 13 were waited for; matrix products, arithmetic and copies ran while one was open for 0% of the time, Pallas kernels for 18%

profile of v3, /device:TPU:0, one launch (start us, length us, event | category | flops | bytes accessed | tf_op | source)
XLA Modules:
  0.0 109.2 jit_solution(13197959790038849686)
XLA Ops:
  0.6 3.0 %collective-permute-start.7 = (bf16[3,192,720]{2,1,0:T(8,128)(2,1)}, bf16[3,192,720]{2,1,0:T(8,128)(2,1)S(1)}, u32[]{:S(2)}, u32[]{:S(2)}) collective-permute-start(bf16[3,192,720]{2,1,0:T(8,128)(2,1)} %bitcast.4), channel_id=1, source_target_pairs={{0,16},{8,24},{16,0},{24,8},{1,17},{9,25},{17,1},{25,9},{2,18},{10... | collective-permute-start | bytes 2488328 | tf_op jit(solution)/shard_map/ppermute | solution.py:270
  3.7 19.9 %collective-permute-done.7.refs_1_ = bf16[3,192,720]{2,1,0:T(8,128)(2,1)S(1)} collective-permute-done((bf16[3,192,720]{2,1,0:T(8,128)(2,1)}, bf16[3,192,720]{2,1,0:T(8,128)(2,1)S(1)}, u32[]{:S(2)}, u32[]{:S(2)}) %collective-permute-start.7) | collective-permute-done | bytes 829472 | tf_op jit(solution)/shard_map/ppermute | solution.py:270
  23.5 7.6 %dft.2 = (bf16[24,1792]{1,0:T(8,128)(2,1)}, bf16[24,1792]{1,0:T(8,128)(2,1)}, bf16[24,1792]{1,0:T(8,128)(2,1)}, bf16[24,1792]{1,0:T(8,128)(2,1)}, bf16[24,1792]{...) custom-call(bf16[1752,1440]{1,0:T(8,128)(2,1)} %bitcast.7, ...), custom_call_target="tpu_custom_call" | custom-call | tf_op jit(solution)/shard_map/dft/pallas_call | solution.py:122
  31.1 2.9 %collective-permute-start.10 = (bf16[24,1792]{1,0:T(8,128)(2,1)}, bf16[24,1792]{1,0:T(8,128)(2,1)S(1)}, u32[]{:S(2)}, u32[]{:S(2)}) collective-permute-start(bf16[24,1792]{1,0:T(8,128)(2,1)} %get-tuple-element.42), channel_id=1, source_target_pairs={{0,4},{1,5},{2,6},{3,7},{4,0},{5,1},{6,2},{7,3},{8,12},{9,13},{10,... | collective-permute-start | bytes 258056 | tf_op jit(solution)/shard_map/ppermute | solution.py:270
  34.0 1.3 %collective-permute-start.11 = (bf16[24,1792]{1,0:T(8,128)(2,1)}, bf16[24,1792]{1,0:T(8,128)(2,1)S(1)}, u32[]{:S(2)}, u32[]{:S(2)}) collective-permute-start(bf16[24,1792]{1,0:T(8,128)(2,1)} %get-tuple-element.43), channel_id=1, source_target_pairs={{0,5},{1,4},{2,7},{3,6},{4,1},{5,0},{6,3},{7,2},{8,13},{9,12},{10,... | collective-permute-start | bytes 258056 | tf_op jit(solution)/shard_map/ppermute | solution.py:270
  35.3 3.6 %collective-permute-start.12 = (bf16[24,1792]{1,0:T(8,128)(2,1)}, bf16[24,1792]{1,0:T(8,128)(2,1)S(1)}, u32[]{:S(2)}, u32[]{:S(2)}) collective-permute-start(bf16[24,1792]{1,0:T(8,128)(2,1)} %get-tuple-element.44), channel_id=1, source_target_pairs={{0,6},{1,7},{2,4},{3,5},{4,2},{5,3},{6,0},{7,1},{8,14},{9,15},{10,... | collective-permute-start | bytes 258056 | tf_op jit(solution)/shard_map/ppermute | solution.py:270
  38.9 8.7 %dft.3 = (bf16[24,1792]{1,0:T(8,128)(2,1)}, bf16[2,24,1792]{2,1,0:T(8,128)(2,1)}, bf16[2,24,1792]{2,1,0:T(8,128)(2,1)}, bf16[2,24,1792]{2,1,0:T(8,128)(2,1)}, bf...) custom-call(bf16[1752,1440]{1,0:T(8,128)(2,1)} %bitcast.8, ...), custom_call_target="tpu_custom_call" | custom-call | tf_op jit(solution)/shard_map/dft/pallas_call | solution.py:122
  47.7 1.7 %collective-permute-start = (bf16[2,24,1792]{2,1,0:T(8,128)(2,1)}, bf16[2,24,1792]{2,1,0:T(8,128)(2,1)S(1)}, u32[]{:S(2)}, u32[]{:S(2)}) collective-permute-start(bf16[2,24,1792]{2,1,0:T(8,128)(2,1)} %get-tuple-element.30), channel_id=1, source_target_pairs={{0,1},{1,0},{2,3},{3,2},{4,5},{5,4},{6,7},{7,6},{8,9},{9,8},{10,11... | collective-permute-start | bytes 516104 | tf_op jit(solution)/shard_map/ppermute | solution.py:270
  49.4 6.4 %collective-permute-done.13.rest_7_ = bf16[24,1792]{1,0:T(8,128)(2,1)S(1)} collective-permute-done((bf16[24,1792]{1,0:T(8,128)(2,1)S(1)}, bf16[24,1792]{1,0:T(8,128)(2,1)S(1)}, u32[]{:S(2)}, u32[]{:S(2)}) %collective-permute-start.13) | collective-permute-done | bytes 86048 | tf_op jit(solution)/shard_map/ppermute | solution.py:270
  56.0 2.5 %collective-permute-done.1.rest_2_ = bf16[2,24,1792]{2,1,0:T(8,128)(2,1)S(1)} collective-permute-done((bf16[2,24,1792]{2,1,0:T(8,128)(2,1)}, bf16[2,24,1792]{2,1,0:T(8,128)(2,1)S(1)}, u32[]{:S(2)}, u32[]{:S(2)}) %collective-permute-start.1) | collective-permute-done | bytes 172064 | tf_op jit(solution)/shard_map/ppermute | solution.py:270
  58.5 1.6 %collective-permute-start.4 = (bf16[24,1792]{1,0:T(8,128)(2,1)}, bf16[24,1792]{1,0:T(8,128)(2,1)S(1)}, u32[]{:S(2)}, u32[]{:S(2)}) collective-permute-start(bf16[24,1792]{1,0:T(8,128)(2,1)} %get-tuple-element.34), channel_id=1, source_target_pairs={{0,5},{1,4},{2,7},{3,6},{4,1},{5,0},{6,3},{7,2},{8,13},{9,12},{10,... | collective-permute-start | bytes 258056 | tf_op jit(solution)/shard_map/ppermute | solution.py:270
  60.1 2.7 %collective-permute-start.5 = (bf16[24,1792]{1,0:T(8,128)(2,1)}, bf16[24,1792]{1,0:T(8,128)(2,1)S(1)}, u32[]{:S(2)}, u32[]{:S(2)}) collective-permute-start(bf16[24,1792]{1,0:T(8,128)(2,1)} %get-tuple-element.35), channel_id=1, source_target_pairs={{0,6},{1,7},{2,4},{3,5},{4,2},{5,3},{6,0},{7,1},{8,14},{9,15},{10,... | collective-permute-start | bytes 258056 | tf_op jit(solution)/shard_map/ppermute | solution.py:270
  62.7 1.0 collective-permute-start.6
  63.7 1.2 %turn.1 = (bf16[3,720,256]{2,1,0:T(8,128)(2,1)S(1)}, bf16[3,720,256]{2,1,0:T(8,128)(2,1)S(1)}, bf16[3,720,256]{2,1,0:T(8,128)(2,1)S(1)}, bf16[3,720,256]{2,1,0:T(8,128)(2,1)S(1)}) custom-call(bf16[3,192,720]{2,1,0:T(8,128)(2,1)S(1)} %bitcast.6, bf16[3,192,720]{2,1,0:T(8,128)(2,1)S(1)} %collective-permute-done.7.refs_1_, ...), custom_call_target="tpu_custom_call" | custom-call | tf_op jit(solution)/shard_map/turn/pallas_call | solution.py:149
  65.0 2.1 %legendre.2.rest_12_ = f32[60,8,128]{2,1,0:T(8,128)S(1)} custom-call(bf16[24,1792]{1,0:T(8,128)(2,1)S(1)} %copy-done.2, bf16[2,24,1792]{2,1,0:T(8,128)(2,1)S(1)} %collective-permute-done.rest_1_, bf16[2,24,1792]{2,1,0:T(8,128)(2,1)S(1)} %collective-permute-done.1.rest_2_, bf16[2,24,1792]{2,1,0:T(8,128)(2,1)S(1)} %collective-permute-done.2.rest_3_, ...), custom_call_target="tpu_custom_call" | custom-call | tf_op jit(solution)/shard_map/legendre/pallas_call | solution.py:218
  67.1 1.5 %collective-permute-done.3.rest_4_ = bf16[24,1792]{1,0:T(8,128)(2,1)S(1)} collective-permute-done((bf16[24,1792]{1,0:T(8,128)(2,1)}, bf16[24,1792]{1,0:T(8,128)(2,1)S(1)}, u32[]{:S(2)}, u32[]{:S(2)}) %collective-permute-start.3) | collective-permute-done | bytes 86048 | tf_op jit(solution)/shard_map/ppermute | solution.py:270
  68.7 3.3 %collective-permute-done.4.rest_5_ = bf16[24,1792]{1,0:T(8,128)(2,1)S(1)} collective-permute-done((bf16[24,1792]{1,0:T(8,128)(2,1)}, bf16[24,1792]{1,0:T(8,128)(2,1)S(1)}, u32[]{:S(2)}, u32[]{:S(2)}) %collective-permute-start.4) | collective-permute-done | bytes 86048 | tf_op jit(solution)/shard_map/ppermute | solution.py:270
  72.0 2.1 %legendre.3 = (f32[60,8,128]{2,1,0:T(8,128)S(1)}, f32[60,8,128]{2,1,0:T(8,128)S(1)}) custom-call(bf16[24,1792]{1,0:T(8,128)(2,1)S(1)} %copy-done.1, bf16[2,24,1792]{2,1,0:T(8,128)(2,1)S(1)} %collective-permute-done.rest_1_, bf16[2,24,1792]{2,1,0:T(8,128)(2,1)S(1)} %collective-permute-done.1.rest_2_, bf16[2,24,1792]{2,1,0:T(8,128)(2,1)S(1)} %collective-permute-done.2.rest_3_, ...), custom_call_target="tpu_custom_call" | custom-call | tf_op jit(solution)/shard_map/legendre/pallas_call | solution.py:218
  74.2 1.5 %collective-permute-done.14 = f32[60,8,128]{2,1,0:T(8,128)S(1)} collective-permute-done((f32[60,8,128]{2,1,0:T(8,128)S(1)}, f32[60,8,128]{2,1,0:T(8,128)S(1)}, u32[]{:S(2)}, u32[]{:S(2)}) %collective-permute-start.14) | collective-permute-done | bytes 245792 | tf_op jit(solution)/shard_map/ppermute | solution.py:270
  75.8 1.6 %collective-permute-start.15 = (f32[30,8,128]{2,1,0:T(8,128)S(1)}, f32[30,8,128]{2,1,0:T(8,128)S(1)}, u32[]{:S(2)}, u32[]{:S(2)}) collective-permute-start(f32[30,8,128]{2,1,0:T(8,128)S(1)} %slice_select_fusion), channel_id=1, source_target_pairs={{0,16},{8,24},{16,0},{24,8},{1,17},{9,25},{17,1},{25,9},{2,18},{10... | collective-permute-start | bytes 368648 | tf_op jit(solution)/shard_map/ppermute | solution.py:270
  77.3 3.9 %collective-permute-done.15 = f32[30,8,128]{2,1,0:T(8,128)S(1)} collective-permute-done((f32[30,8,128]{2,1,0:T(8,128)S(1)}, f32[30,8,128]{2,1,0:T(8,128)S(1)}, u32[]{:S(2)}, u32[]{:S(2)}) %collective-permute-start.15) | collective-permute-done | bytes 122912 | tf_op jit(solution)/shard_map/ppermute | solution.py:270
  81.2 0.9 collective-permute-start.16
  82.2 4.0 %collective-permute-done.16 = f32[30,8,128]{2,1,0:T(8,128)S(1)} collective-permute-done((f32[30,8,128]{2,1,0:T(8,128)S(1)}, f32[30,8,128]{2,1,0:T(8,128)S(1)}, u32[]{:S(2)}, u32[]{:S(2)}) %collective-permute-start.16) | collective-permute-done | bytes 122912 | tf_op jit(solution)/shard_map/ppermute | solution.py:270
  86.2 3.2 %collective-permute-start.19 = (f32[30,8,128]{2,1,0:T(8,128)S(1)}, f32[30,8,128]{2,1,0:T(8,128)S(1)}, u32[]{:S(2)}, u32[]{:S(2)}) collective-permute-start(f32[30,8,128]{2,1,0:T(8,128)S(1)} %add.30), channel_id=1, source_target_pairs={{0,2},{1,3},{2,0},{3,1},{4,6},{5,7},{6,4},{7,5},{8,10},{9,11},{10,... | collective-permute-start | bytes 368648 | tf_op jit(solution)/shard_map/ppermute | solution.py:270
  89.4 1.0 collective-permute-start.17
  90.9 3.6 %collective-permute-done.19 = f32[30,8,128]{2,1,0:T(8,128)S(1)} collective-permute-done((f32[30,8,128]{2,1,0:T(8,128)S(1)}, f32[30,8,128]{2,1,0:T(8,128)S(1)}, u32[]{:S(2)}, u32[]{:S(2)}) %collective-permute-start.19) | collective-permute-done | bytes 122912 | tf_op jit(solution)/shard_map/ppermute | solution.py:270
  94.5 2.4 %collective-permute-done.17 = f32[30,8,128]{2,1,0:T(8,128)S(1)} collective-permute-done((f32[30,8,128]{2,1,0:T(8,128)S(1)}, f32[30,8,128]{2,1,0:T(8,128)S(1)}, u32[]{:S(2)}, u32[]{:S(2)}) %collective-permute-start.17) | collective-permute-done | bytes 122912 | tf_op jit(solution)/shard_map/ppermute | solution.py:270
  96.9 3.8 %collective-permute-done.18 = f32[30,8,128]{2,1,0:T(8,128)S(1)} collective-permute-done((f32[30,8,128]{2,1,0:T(8,128)S(1)}, f32[30,8,128]{2,1,0:T(8,128)S(1)}, u32[]{:S(2)}, u32[]{:S(2)}) %collective-permute-start.18) | collective-permute-done | bytes 122912 | tf_op jit(solution)/shard_map/ppermute | solution.py:270
  100.7 1.7 %collective-permute-start.20 = (f32[30,8,128]{2,1,0:T(8,128)S(1)}, f32[30,8,128]{2,1,0:T(8,128)S(1)}, u32[]{:S(2)}, u32[]{:S(2)}) collective-permute-start(f32[30,8,128]{2,1,0:T(8,128)S(1)} %add_add_fusion), channel_id=1, source_target_pairs={{0,16},{8,24},{16,0},{24,8},{1,17},{9,25},{17,1},{25,9},{2,18},{10... | collective-permute-start | bytes 368648 | tf_op jit(solution)/shard_map/ppermute | solution.py:270
  102.4 3.3 %collective-permute-done.20 = f32[30,8,128]{2,1,0:T(8,128)S(1)} collective-permute-done((f32[30,8,128]{2,1,0:T(8,128)S(1)}, f32[30,8,128]{2,1,0:T(8,128)S(1)}, u32[]{:S(2)}, u32[]{:S(2)}) %collective-permute-start.20) | collective-permute-done | bytes 122912 | tf_op jit(solution)/shard_map/ppermute | solution.py:270
  105.8 1.5 %collective-permute-done.21 = f32[60,8,128]{2,1,0:T(8,128)S(1)} collective-permute-done((f32[60,8,128]{2,1,0:T(8,128)S(1)}, f32[60,8,128]{2,1,0:T(8,128)S(1)}, u32[]{:S(2)}, u32[]{:S(2)}) %collective-permute-start.21) | collective-permute-done | bytes 245792 | tf_op jit(solution)/shard_map/ppermute | solution.py:270
  108.0 1.1 %copy.6 = f32[2,73,720]{2,0,1:T(2,128)} copy(f32[2,73,720]{2,1,0:T(8,128)S(1)} %get-tuple-element.50) | data formatting | bytes 840960
  (34 shorter events, 1.9 us)
Async XLA Ops:
  0.6 22.9 %collective-permute-start.7 = (bf16[3,192,720]{2,1,0:T(8,128)(2,1)}, bf16[3,192,720]{2,1,0:T(8,128)(2,1)S(1)}, u32[]{:S(2)}, u32[]{:S(2)}) collective-permute-start(bf16[3,192,720]{2,1,0:T(8,128)(2,1)} %bitcast.4), channel_id=1, source_target_pairs={{0,16},{8,24},{16,0},{24,8},{1,17},{9,25},{17,1},{25,9},{2,18},{10... | collective-permute-start | bytes 2488328 | tf_op jit(solution)/shard_map/ppermute | solution.py:270
  3.7 56.4 %collective-permute-start.8 = (bf16[3,192,720]{2,1,0:T(8,128)(2,1)}, bf16[3,192,720]{2,1,0:T(8,128)(2,1)S(1)}, u32[]{:S(2)}, u32[]{:S(2)}) collective-permute-start(bf16[3,192,720]{2,1,0:T(8,128)(2,1)} %bitcast.5), channel_id=1, source_target_pairs={{0,8},{8,0},{16,24},{24,16},{1,9},{9,1},{17,25},{25,17},{2,10},{10... | collective-permute-start | bytes 2488328 | tf_op jit(solution)/shard_map/ppermute | solution.py:270
  23.5 39.2 %collective-permute-start.9 = (bf16[3,192,720]{2,1,0:T(8,128)(2,1)S(1)}, bf16[3,192,720]{2,1,0:T(8,128)(2,1)S(1)}, u32[]{:S(2)}, u32[]{:S(2)}) collective-permute-start(bf16[3,192,720]{2,1,0:T(8,128)(2,1)S(1)} %collective-permute-done.7.refs_1_), channel_id=1, source_target_pairs={{0,8},{8,0},{16,24},{24,16},{1,9},{9,1},{17,25},{25,17},{2,10},{10... | collective-permute-start | bytes 2488328 | tf_op jit(solution)/shard_map/ppermute | solution.py:270
  31.1 16.5 %collective-permute-start.10 = (bf16[24,1792]{1,0:T(8,128)(2,1)}, bf16[24,1792]{1,0:T(8,128)(2,1)S(1)}, u32[]{:S(2)}, u32[]{:S(2)}) collective-permute-start(bf16[24,1792]{1,0:T(8,128)(2,1)} %get-tuple-element.42), channel_id=1, source_target_pairs={{0,4},{1,5},{2,6},{3,7},{4,0},{5,1},{6,2},{7,3},{8,12},{9,13},{10,... | collective-permute-start | bytes 258056 | tf_op jit(solution)/shard_map/ppermute | solution.py:270
  34.0 13.7 %collective-permute-start.11 = (bf16[24,1792]{1,0:T(8,128)(2,1)}, bf16[24,1792]{1,0:T(8,128)(2,1)S(1)}, u32[]{:S(2)}, u32[]{:S(2)}) collective-permute-start(bf16[24,1792]{1,0:T(8,128)(2,1)} %get-tuple-element.43), channel_id=1, source_target_pairs={{0,5},{1,4},{2,7},{3,6},{4,1},{5,0},{6,3},{7,2},{8,13},{9,12},{10,... | collective-permute-start | bytes 258056 | tf_op jit(solution)/shard_map/ppermute | solution.py:270
  35.3 14.1 %collective-permute-start.12 = (bf16[24,1792]{1,0:T(8,128)(2,1)}, bf16[24,1792]{1,0:T(8,128)(2,1)S(1)}, u32[]{:S(2)}, u32[]{:S(2)}) collective-permute-start(bf16[24,1792]{1,0:T(8,128)(2,1)} %get-tuple-element.44), channel_id=1, source_target_pairs={{0,6},{1,7},{2,4},{3,5},{4,2},{5,3},{6,0},{7,1},{8,14},{9,15},{10,... | collective-permute-start | bytes 258056 | tf_op jit(solution)/shard_map/ppermute | solution.py:270
  38.9 8.7 %copy-start.3 = (bf16[24,1792]{1,0:T(8,128)(2,1)S(1)}, bf16[24,1792]{1,0:T(8,128)(2,1)}, u32[]{:S(2)}) copy-start(bf16[24,1792]{1,0:T(8,128)(2,1)} %get-tuple-element.45) | copy-start | bytes 258052
  38.9 24.8 %copy-start = (bf16[192,3,720]{2,0,1:T(8,128)(2,1)S(1)}, bf16[192,3,720]{2,0,1:T(8,128)(2,1)}, u32[]{:S(2)}) copy-start(bf16[192,3,720]{2,0,1:T(8,128)(2,1)} %param.6) | copy-start | bytes 2488324
  47.7 8.2 %collective-permute-start.13 = (bf16[24,1792]{1,0:T(8,128)(2,1)S(1)}, bf16[24,1792]{1,0:T(8,128)(2,1)S(1)}, u32[]{:S(2)}, u32[]{:S(2)}) collective-permute-start(bf16[24,1792]{1,0:T(8,128)(2,1)S(1)} %copy-done.3), channel_id=1, source_target_pairs={{0,7},{1,6},{2,5},{3,4},{4,3},{5,2},{6,1},{7,0},{8,15},{9,14},{10,... | collective-permute-start | bytes 258056 | tf_op jit(solution)/shard_map/ppermute | solution.py:270
  47.7 8.1 %collective-permute-start = (bf16[2,24,1792]{2,1,0:T(8,128)(2,1)}, bf16[2,24,1792]{2,1,0:T(8,128)(2,1)S(1)}, u32[]{:S(2)}, u32[]{:S(2)}) collective-permute-start(bf16[2,24,1792]{2,1,0:T(8,128)(2,1)} %get-tuple-element.30), channel_id=1, source_target_pairs={{0,1},{1,0},{2,3},{3,2},{4,5},{5,4},{6,7},{7,6},{8,9},{9,8},{10,11... | collective-permute-start | bytes 516104 | tf_op jit(solution)/shard_map/ppermute | solution.py:270
  49.4 9.1 %collective-permute-start.1 = (bf16[2,24,1792]{2,1,0:T(8,128)(2,1)}, bf16[2,24,1792]{2,1,0:T(8,128)(2,1)S(1)}, u32[]{:S(2)}, u32[]{:S(2)}) collective-permute-start(bf16[2,24,1792]{2,1,0:T(8,128)(2,1)} %get-tuple-element.31), channel_id=1, source_target_pairs={{0,2},{1,3},{2,0},{3,1},{4,6},{5,7},{6,4},{7,5},{8,10},{9,11},{10,... | collective-permute-start | bytes 516104 | tf_op jit(solution)/shard_map/ppermute | solution.py:270
  55.8 9.2 %collective-permute-start.2 = (bf16[2,24,1792]{2,1,0:T(8,128)(2,1)}, bf16[2,24,1792]{2,1,0:T(8,128)(2,1)S(1)}, u32[]{:S(2)}, u32[]{:S(2)}) collective-permute-start(bf16[2,24,1792]{2,1,0:T(8,128)(2,1)} %get-tuple-element.32), channel_id=1, source_target_pairs={{0,3},{1,2},{2,1},{3,0},{4,7},{5,6},{6,5},{7,4},{8,11},{9,10},{10,... | collective-permute-start | bytes 516104 | tf_op jit(solution)/shard_map/ppermute | solution.py:270
  55.8 12.8 %collective-permute-start.3 = (bf16[24,1792]{1,0:T(8,128)(2,1)}, bf16[24,1792]{1,0:T(8,128)(2,1)S(1)}, u32[]{:S(2)}, u32[]{:S(2)}) collective-permute-start(bf16[24,1792]{1,0:T(8,128)(2,1)} %get-tuple-element.33), channel_id=1, source_target_pairs={{0,4},{1,5},{2,6},{3,7},{4,0},{5,1},{6,2},{7,3},{8,12},{9,13},{10,... | collective-permute-start | bytes 258056 | tf_op jit(solution)/shard_map/ppermute | solution.py:270
  58.5 13.5 %collective-permute-start.4 = (bf16[24,1792]{1,0:T(8,128)(2,1)}, bf16[24,1792]{1,0:T(8,128)(2,1)S(1)}, u32[]{:S(2)}, u32[]{:S(2)}) collective-permute-start(bf16[24,1792]{1,0:T(8,128)(2,1)} %get-tuple-element.34), channel_id=1, source_target_pairs={{0,5},{1,4},{2,7},{3,6},{4,1},{5,0},{6,3},{7,2},{8,13},{9,12},{10,... | collective-permute-start | bytes 258056 | tf_op jit(solution)/shard_map/ppermute | solution.py:270
  60.1 11.9 %collective-permute-start.5 = (bf16[24,1792]{1,0:T(8,128)(2,1)}, bf16[24,1792]{1,0:T(8,128)(2,1)S(1)}, u32[]{:S(2)}, u32[]{:S(2)}) collective-permute-start(bf16[24,1792]{1,0:T(8,128)(2,1)} %get-tuple-element.35), channel_id=1, source_target_pairs={{0,6},{1,7},{2,4},{3,5},{4,2},{5,3},{6,0},{7,1},{8,14},{9,15},{10,... | collective-permute-start | bytes 258056 | tf_op jit(solution)/shard_map/ppermute | solution.py:270
  62.7 2.3 %copy-start.2 = (bf16[24,1792]{1,0:T(8,128)(2,1)S(1)}, bf16[24,1792]{1,0:T(8,128)(2,1)}, u32[]{:S(2)}) copy-start(bf16[24,1792]{1,0:T(8,128)(2,1)} %get-tuple-element.41.rest_0_) | copy-start | bytes 258052
  62.7 9.3 %collective-permute-start.6 = (bf16[24,1792]{1,0:T(8,128)(2,1)}, bf16[24,1792]{1,0:T(8,128)(2,1)S(1)}, u32[]{:S(2)}, u32[]{:S(2)}) collective-permute-start(bf16[24,1792]{1,0:T(8,128)(2,1)} %get-tuple-element.36), channel_id=1, source_target_pairs={{0,7},{1,6},{2,5},{3,4},{4,3},{5,2},{6,1},{7,0},{8,15},{9,14},{10,... | collective-permute-start | bytes 258056 | tf_op jit(solution)/shard_map/ppermute | solution.py:270
  65.0 7.0 %copy-start.1 = (bf16[24,1792]{1,0:T(8,128)(2,1)S(1)}, bf16[24,1792]{1,0:T(8,128)(2,1)}, u32[]{:S(2)}) copy-start(bf16[24,1792]{1,0:T(8,128)(2,1)} %get-tuple-element.29.rest_0_) | copy-start | bytes 258052
  74.1 1.6 %collective-permute-start.14 = (f32[60,8,128]{2,1,0:T(8,128)S(1)}, f32[60,8,128]{2,1,0:T(8,128)S(1)}, u32[]{:S(2)}, u32[]{:S(2)}) collective-permute-start(f32[60,8,128]{2,1,0:T(8,128)S(1)} %get-tuple-element.47), channel_id=1, source_target_pairs={{0,8},{8,0},{16,24},{24,16},{1,9},{9,1},{17,25},{25,17},{2,10},{10... | collective-permute-start | bytes 737288 | tf_op jit(solution)/shard_map/ppermute | solution.py:270
  75.8 5.4 %collective-permute-start.15 = (f32[30,8,128]{2,1,0:T(8,128)S(1)}, f32[30,8,128]{2,1,0:T(8,128)S(1)}, u32[]{:S(2)}, u32[]{:S(2)}) collective-permute-start(f32[30,8,128]{2,1,0:T(8,128)S(1)} %slice_select_fusion), channel_id=1, source_target_pairs={{0,16},{8,24},{16,0},{24,8},{1,17},{9,25},{17,1},{25,9},{2,18},{10... | collective-permute-start | bytes 368648 | tf_op jit(solution)/shard_map/ppermute | solution.py:270
  81.2 4.9 %collective-permute-start.16 = (f32[30,8,128]{2,1,0:T(8,128)S(1)}, f32[30,8,128]{2,1,0:T(8,128)S(1)}, u32[]{:S(2)}, u32[]{:S(2)}) collective-permute-start(f32[30,8,128]{2,1,0:T(8,128)S(1)} %select_add_fusion), channel_id=1, source_target_pairs={{0,1},{1,0},{2,3},{3,2},{4,5},{5,4},{6,7},{7,6},{8,9},{9,8},{10,11... | collective-permute-start | bytes 368648 | tf_op jit(solution)/shard_map/ppermute | solution.py:270
  86.2 8.3 %collective-permute-start.19 = (f32[30,8,128]{2,1,0:T(8,128)S(1)}, f32[30,8,128]{2,1,0:T(8,128)S(1)}, u32[]{:S(2)}, u32[]{:S(2)}) collective-permute-start(f32[30,8,128]{2,1,0:T(8,128)S(1)} %add.30), channel_id=1, source_target_pairs={{0,2},{1,3},{2,0},{3,1},{4,6},{5,7},{6,4},{7,5},{8,10},{9,11},{10,... | collective-permute-start | bytes 368648 | tf_op jit(solution)/shard_map/ppermute | solution.py:270
  89.4 7.5 %collective-permute-start.17 = (f32[30,8,128]{2,1,0:T(8,128)S(1)}, f32[30,8,128]{2,1,0:T(8,128)S(1)}, u32[]{:S(2)}, u32[]{:S(2)}) collective-permute-start(f32[30,8,128]{2,1,0:T(8,128)S(1)} %add.30), channel_id=1, source_target_pairs={{0,6},{1,7},{2,4},{3,5},{4,2},{5,3},{6,0},{7,1},{8,14},{9,15},{10,... | collective-permute-start | bytes 368648 | tf_op jit(solution)/shard_map/ppermute | solution.py:270
  90.3 10.4 %collective-permute-start.18 = (f32[30,8,128]{2,1,0:T(8,128)S(1)}, f32[30,8,128]{2,1,0:T(8,128)S(1)}, u32[]{:S(2)}, u32[]{:S(2)}) collective-permute-start(f32[30,8,128]{2,1,0:T(8,128)S(1)} %add.30), channel_id=1, source_target_pairs={{0,4},{1,5},{2,6},{3,7},{4,0},{5,1},{6,2},{7,3},{8,12},{9,13},{10,... | collective-permute-start | bytes 368648 | tf_op jit(solution)/shard_map/ppermute | solution.py:270
  100.7 4.9 %collective-permute-start.20 = (f32[30,8,128]{2,1,0:T(8,128)S(1)}, f32[30,8,128]{2,1,0:T(8,128)S(1)}, u32[]{:S(2)}, u32[]{:S(2)}) collective-permute-start(f32[30,8,128]{2,1,0:T(8,128)S(1)} %add_add_fusion), channel_id=1, source_target_pairs={{0,16},{8,24},{16,0},{24,8},{1,17},{9,25},{17,1},{25,9},{2,18},{10... | collective-permute-start | bytes 368648 | tf_op jit(solution)/shard_map/ppermute | solution.py:270
  105.7 1.6 %collective-permute-start.21 = (f32[60,8,128]{2,1,0:T(8,128)S(1)}, f32[60,8,128]{2,1,0:T(8,128)S(1)}, u32[]{:S(2)}, u32[]{:S(2)}) collective-permute-start(f32[60,8,128]{2,1,0:T(8,128)S(1)} %maximum_select_fusion.1), channel_id=1, source_target_pairs={{0,8},{8,0},{16,24},{24,16},{1,9},{9,1},{17,25},{25,17},{2,10},{10... | collective-permute-start | bytes 737288 | tf_op jit(solution)/shard_map/ppermute | solution.py:270

commit v4 on v3

--- a/solution.py
+++ b/solution.py
@@ -12,7 +12,8 @@
 
 LANES = 128
 VMEM_LIMIT = 24 * 1024 * 1024
-STAGED_LIMIT = 59 * 1024 * 1024
+STAGED_LIMIT = 53 * 1024 * 1024
+DIRECT_LIMIT = 44 * 1024 * 1024
 
 
 def round_up(value, step):
@@ -49,27 +50,34 @@
     return lax.rem(index + count - step, count)
 
 
-def dft_kernel(bands, per, chans, lats, chunks, joined, field, table_hbm, *rest):
-    near = bands // 2 - 1 if joined else 0
-    before, rest = rest[:near], rest[near:]
+def dft_kernel(bands, per, chans, lats, chunks, field, table_hbm, *rest):
     outs = rest[:bands]
-    dscr, turned, packed, xbuf, table, sems = rest[bands:]
-    load = pltpu.make_async_copy(table_hbm, table, sems.at[len(chunks)])
-    load.start()
+    dscr, turned, packed = rest[bands : bands + 3]
+    staged = len(rest) > bands + 3
+    if staged:
+        xbuf, table, sems = rest[bands + 3 :]
+        load = pltpu.make_async_copy(table_hbm, table, sems.at[len(chunks)])
+        load.start()
+    else:
+        xbuf, table = field, table_hbm
     copies = []
     row = 0
     for i, rows in enumerate(chunks):
-        cp = pltpu.make_async_copy(
-            field.at[pl.ds(row, rows), :], xbuf.at[pl.ds(row, rows), :], sems.at[i]
-        )
-        cp.start()
+        cp = None
+        if staged:
+            cp = pltpu.make_async_copy(
+                field.at[pl.ds(row, rows), :], xbuf.at[pl.ds(row, rows), :], sems.at[i]
+            )
+            cp.start()
         copies.append((row, rows, cp))
         row += rows
     band = lax.axis_index("lat")
     tiles = dscr.shape[0]
-    load.wait()
+    if staged:
+        load.wait()
     for row, rows, cp in copies:
-        cp.wait()
+        if staged:
+            cp.wait()
         res = jnp.dot(xbuf[pl.ds(row, rows), :], table[...], preferred_element_type=jnp.float32)
         for q in range(tiles):
             dscr[q, pl.ds(row, rows), :] = res[:, q * LANES : (q + 1) * LANES]
@@ -94,14 +102,10 @@
 
     lax.fori_loop(0, bands, pack, 0, unroll=min(bands, 8))
     for s in range(bands):
-        if 0 < s <= near:
-            outs[s][0] = before[s - 1][...]
-            outs[s][1] = packed[s].astype(jnp.bfloat16)
-        else:
-            outs[s][...] = packed[s].astype(jnp.bfloat16)
-
-
-def dft_blocks(field, table, before, bands, per, chans, lats):
+        outs[s][...] = packed[s].astype(jnp.bfloat16)
+
+
+def dft_blocks(field, table, staged, bands, per, chans, lats):
     rows_all, lon_count = field.shape
     width = round_up(per * chans, LANES)
     step = -(-chans // 3) * lats
@@ -113,28 +117,28 @@
     columns = table.shape[1]
     anywhere = pl.BlockSpec(memory_space=pl.ANY)
     vmem = pl.BlockSpec(memory_space=pltpu.VMEM)
-    one, two = ((2,) * k + (lats, width) for k in (0, 1))
-    out_shape = [
-        jax.ShapeDtypeStruct(two if 0 < s <= len(before) else one, jnp.bfloat16)
-        for s in range(bands)
+    staging = [
+        pltpu.VMEM((rows_all, lon_count), jnp.bfloat16),
+        pltpu.VMEM(table.shape, jnp.bfloat16),
+        pltpu.SemaphoreType.DMA((len(chunks) + 1,)),
     ]
-    args = [field, table, *before]
+    staging = staging if staged else []
     return pl.pallas_call(
-        functools.partial(dft_kernel, bands, per, chans, lats, tuple(chunks), bool(before)),
-        out_shape=out_shape,
-        in_specs=[anywhere, anywhere] + [vmem] * (len(args) - 2),
-        out_specs=[vmem] * len(out_shape),
+        functools.partial(dft_kernel, bands, per, chans, lats, tuple(chunks)),
+        out_shape=[jax.ShapeDtypeStruct((lats, width), jnp.bfloat16)] * bands,
+        in_specs=[anywhere if staged else vmem] * 2,
+        out_specs=[vmem] * bands,
         scratch_shapes=[
             pltpu.VMEM((columns // LANES, LANES * lats, LANES), jnp.float32),
             pltpu.VMEM((columns // LANES, LANES * lats, LANES), jnp.float32),
             pltpu.VMEM((bands, lats, width), jnp.float32),
-            pltpu.VMEM((rows_all, lon_count), jnp.bfloat16),
-            pltpu.VMEM(table.shape, jnp.bfloat16),
-            pltpu.SemaphoreType.DMA((len(chunks) + 1,)),
-        ],
-        compiler_params=pltpu.CompilerParams(vmem_limit_bytes=STAGED_LIMIT),
+        ]
+        + staging,
+        compiler_params=pltpu.CompilerParams(
+            vmem_limit_bytes=STAGED_LIMIT if staged else DIRECT_LIMIT
+        ),
         name="dft",
-    )(*args)
+    )(field, table)
 
 
 def turn_kernel(count, *refs):
@@ -169,8 +173,7 @@
     width = 2 * chans
     for s in range(bands):
         row = pl.multiple_of(source_of(band, bands, s) * lats, 8)
-        block = blocks[s][...] if len(blocks[s].shape) == 2 else blocks[s][field]
-        fourier[pl.ds(row, lats), :] = block.astype(jnp.float32)
+        fourier[pl.ds(row, lats), :] = blocks[s][...].astype(jnp.float32)
     for i in range(groups * per_dev):
         columns[i] = fourier[:, pl.ds(i * width, width)].astype(jnp.bfloat16)
     for q in range(groups):
@@ -229,17 +232,27 @@
     )(*blocks, *bases, *before)
 
 
-def loss_kernel(chans, degrees, count, blocks, spectra, loss, sums):
+def loss_kernel(chans, degrees, count, mesh_size, *refs):
+    parts = (len(refs) - 4) // 2
+    owned, other = refs[:parts], refs[parts : 2 * parts]
+    spectra, loss, sums, fields = refs[2 * parts :]
     lane_tiles = round_up(degrees, LANES) // LANES
     row_tiles = round_up(chans, 8) // 8
     scale = 1.0 / count
+    mine = quarter_id(mesh_size)
+    high = lax.rem(lax.axis_index("batch"), 2)
+    size = owned[0].shape[0]
+    for m in range(parts):
+        start = jnp.bitwise_xor(mine, m) * size
+        fields[high, pl.ds(start, size)] = owned[m][...] * scale
+        fields[1 - high, pl.ds(start, size)] = other[m][...] * scale
     for r in range(row_tiles):
         rows = min(8, chans - r * 8)
         acc = jnp.zeros((8, LANES), jnp.float32)
         for k in range(lane_tiles):
             lanes = min(LANES, degrees - k * LANES)
-            first = blocks[r * lane_tiles + k] * scale
-            second = blocks[(row_tiles + r) * lane_tiles + k] * scale
+            first = fields[0, r * lane_tiles + k]
+            second = fields[1, r * lane_tiles + k]
             spectra[0, pl.ds(r * 8, rows), pl.ds(k * LANES, lanes)] = first[:rows, :lanes]
             spectra[1, pl.ds(r * 8, rows), pl.ds(k * LANES, lanes)] = second[:rows, :lanes]
             gap = jnp.log(first + 1e-06) - jnp.log(second + 1e-06)
@@ -253,55 +266,72 @@
     loss[...] = (jnp.sum(turned, axis=0, keepdims=True) * (1.0 / degrees))[:, :chans]
 
 
-def loss_call(blocks, chans, degrees, count):
+def loss_call(owned, other, chans, degrees, count):
+    mesh_size = lax.axis_size("batch"), lax.axis_size("lat")
+    tiles = len(owned) * owned[0].shape[0]
     return pl.pallas_call(
-        functools.partial(loss_kernel, chans, degrees, count),
+        functools.partial(loss_kernel, chans, degrees, count, mesh_size),
         out_shape=(
             jax.ShapeDtypeStruct((2, chans, degrees), jnp.float32),
             jax.ShapeDtypeStruct((1, chans), jnp.float32),
         ),
-        scratch_shapes=[pltpu.VMEM((round_up(chans, 8), LANES), jnp.float32)],
+        scratch_shapes=[
+            pltpu.VMEM((round_up(chans, 8), LANES), jnp.float32),
+            pltpu.VMEM((2, tiles, 8, LANES), jnp.float32),
+        ],
         compiler_params=pltpu.CompilerParams(vmem_limit_bytes=VMEM_LIMIT),
         name="loss",
-    )(blocks)
+    )(*owned, *other)
 
 
 def exchange(value, axis, step):
     return lax.ppermute(value, axis, peers(lax.axis_size(axis), step))
 
 
+def square(mesh_size):
+    groups, bands = mesh_size
+    return [bit for bit, there in ((1, bands > 1), (2 * bands, groups > 2)) if there]
+
+
+def quarter_steps(mesh_size):
+    bits = square(mesh_size)
+    return [sum(bit for k, bit in enumerate(bits) if m >> k & 1) for m in range(1 << len(bits))]
+
+
+def quarter_id(mesh_size):
+    _, bands = mesh_size
+    flat = lax.axis_index("batch") * bands + lax.axis_index("lat")
+    return sum(lax.rem(flat // bit, 2) << k for k, bit in enumerate(square(mesh_size)))
+
+
+def flat_exchange(value, mesh_size, step):
+    count = mesh_size[0] * mesh_size[1]
+    return lax.ppermute(value, ("batch", "lat"), [(i, i ^ step) for i in range(count)])
+
+
 def reduce_all(kept, sent):
-    index = lax.axis_index("batch")
-    groups = lax.axis_size("batch")
+    mesh_size = groups, bands = lax.axis_size("batch"), lax.axis_size("lat")
     value = kept + exchange(sent, "batch", 1)
-    halved = [(1, index % 2 == 1)]
+    steps = quarter_steps(mesh_size)
+    mine = quarter_id(mesh_size)
+    pieces = value.reshape((len(steps), value.shape[0] // len(steps)) + value.shape[1:])
+    value = lax.dynamic_index_in_dim(pieces, mine, 0, keepdims=False)
+    for m in range(len(steps) - 1, 0, -1):
+        piece = lax.dynamic_index_in_dim(pieces, jnp.bitwise_xor(mine, m), 0, keepdims=False)
+        value = value + flat_exchange(piece, mesh_size, steps[m])
+    step = 4
+    while step < groups:
+        value = value + exchange(value, "batch", step)
+        step *= 2
     step = 2
-    while step < groups:
-        if value.shape[0] % 2 == 0:
-            half = value.shape[0] // 2
-            high = (index // step) % 2 == 1
-            lower, upper = value[:half], value[half:]
-            kept = jnp.where(high, upper, lower)
-            sent = jnp.where(high, lower, upper)
-            value = kept + exchange(sent, "batch", step)
-            halved.append((step, high))
-        else:
-            value = value + exchange(value, "batch", step)
-        step *= 2
-    bands = lax.axis_size("lat")
-    step = 1
-    radix = 2 if bands.bit_length() % 2 == 0 else 4
+    radix = 2 if bands.bit_length() % 2 == 1 else 4
     while step < bands:
         parts = [exchange(value, "lat", k * step) for k in range(radix - 1, 0, -1)]
         value = value + sum(parts[1:], parts[0])
         step *= radix
         radix = 4
-    for step, high in reversed(halved):
-        other = exchange(value, "batch", step)
-        value = jnp.where(
-            high, jnp.concatenate([other, value]), jnp.concatenate([value, other])
-        )
-    return value
+    owned = [flat_exchange(value, mesh_size, step) if step else value for step in steps]
+    return owned, [exchange(piece, "batch", 1) for piece in owned]
 
 
 def spectrum_loss(predicted, target, legendre_basis):
@@ -321,26 +351,24 @@
         slots = slots + [slot ^ step for slot in slots]
         step //= 2
 
-    def transform(field, before):
+    def transform(field, staged):
         flat = field.reshape(rows, lon_count)
-        return dft_blocks(flat, table, before, bands, groups * per_dev * 2, chans, lats)
-
-    first = transform(predicted, [])
-    second = transform(target, [first[s] for s in sorted(near)])
+        return dft_blocks(flat, table, staged, bands, groups * per_dev * 2, chans, lats)
+
+    first = transform(predicted, True)
+    second = transform(target, False)
     got0, got1 = {0: first[0]}, {0: second[0]}
-    for s in far:
+    for s in far + near:
         got0[s] = exchange(first[s], "lat", s)
         got1[s] = exchange(second[s], "lat", s)
-    for s in near:
-        got0[s] = got1[s] = exchange(second[s], "lat", s)
     bases = turned_bases(bases)
     blocks = [got0[s] for s in range(bands)]
     before = legendre_energy(blocks, bases, slots, chans, lats, [])
     blocks = [got1[s] for s in range(bands)]
     kept, sent = legendre_energy(blocks, bases, slots, chans, lats, before)
-    energy = reduce_all(kept, sent)
+    owned, other = reduce_all(kept, sent)
     spectra, loss = loss_call(
-        energy, chans, degrees, members * groups * groups * bands * per_dev
+        owned, other, chans, degrees, members * groups * groups * bands * per_dev
     )
     return (spectra, loss.reshape(chans))
 

time: 109 us -> 102 us (0.936)
  waiting for transfers between devices: 57.5 us -> 44 us
  starting transfers between devices: 27.1 us -> 39.3 us
  Pallas kernels: 22.4 us -> 17.1 us
    ppermute x22 -> x25, waiting for transfers between devices: 57.5 us -> 36.2 us  [exchange(): return lax.ppermute(value, axis, peers(lax.axis_size(axis), step))]
    ppermute x0 -> x6, waiting for transfers between devices: none -> 7.82 us  [flat_exchange(): lax.ppermute(value, ('batch', 'lat'), [(i, i ^ step) for i in range(count)])]
    ppermute x0 -> x6, starting transfers between devices: none -> 7.11 us  [flat_exchange(): lax.ppermute(value, ('batch', 'lat'), [(i, i ^ step) for i in range(count)])]
    pallas_call x2, Pallas kernels: 16.3 us -> 10.9 us  [dft_blocks(): pl.pallas_call(functools.partial(dft_kernel, bands, per, chans, lats, tup...]
    ppermute x22 -> x25, starting transfers between devices: 27.1 us -> 32.2 us  [exchange(): return lax.ppermute(value, axis, peers(lax.axis_size(axis), step))]
  transfers between devices with their start and end apart: 22 -> 31, of which waited for: 13 -> 17; matrix products, arithmetic and copies ran while one was open for 0% -> 0% of each run, Pallas kernels for 18% -> 14%
where the time goes in v4:
time: 102 us
  waiting for transfers between devices  44 us (43%)
  starting transfers between devices  39.3 us (39%)
  Pallas kernels  17.1 us (17%)
  local copies, waits for them, and re-layouts  1.15 us (1%)
    ppermute x25, waiting for transfers between devices, exchange(): return lax.ppermute(value, axis, peers(lax.axis_size(axis), step))  36.2 us
    ppermute x25, starting transfers between devices, exchange(): return lax.ppermute(value, axis, peers(lax.axis_size(axis), step))  32.2 us
    pallas_call x2, Pallas kernels, dft_blocks(): pl.pallas_call(functools.partial(dft_kernel, bands, per, chans, lats, tup...  10.9 us
    ppermute x6, waiting for transfers between devices, flat_exchange(): lax.ppermute(value, ('batch', 'lat'), [(i, i ^ step) for i in range(count)])  7.82 us
    ppermute x6, starting transfers between devices, flat_exchange(): lax.ppermute(value, ('batch', 'lat'), [(i, i ^ step) for i in range(count)])  7.11 us
    pallas_call x2, Pallas kernels, legendre_energy(): pl.pallas_call(functools.partial(legendre_kernel, bands, groups, per_dev,...  4.13 us
  transfers between devices with their start and end apart: 31, of which 17 were waited for; matrix products, arithmetic and copies ran while one was open for 0% of the time, Pallas kernels for 14%

profile of v4, /device:TPU:0, one launch (start us, length us, event | category | flops | bytes accessed | tf_op | source)
XLA Modules:
  0.0 102.3 jit_solution(16111167159104887924)
XLA Ops:
  0.6 3.0 %collective-permute-start.7 = (bf16[3,192,720]{2,1,0:T(8,128)(2,1)}, bf16[3,192,720]{2,1,0:T(8,128)(2,1)S(1)}, u32[]{:S(2)}, u32[]{:S(2)}) collective-permute-start(bf16[3,192,720]{2,1,0:T(8,128)(2,1)} %bitcast.18), channel_id=1, source_target_pairs={{0,16},{8,24},{16,0},{24,8},{1,17},{9,25},{17,1},{25,9},{2,18},{10... | collective-permute-start | bytes 2488328 | tf_op jit(solution)/shard_map/ppermute | solution.py:288
  3.7 19.9 %collective-permute-done.7.refs_1_ = bf16[3,192,720]{2,1,0:T(8,128)(2,1)S(1)} collective-permute-done((bf16[3,192,720]{2,1,0:T(8,128)(2,1)}, bf16[3,192,720]{2,1,0:T(8,128)(2,1)S(1)}, u32[]{:S(2)}, u32[]{:S(2)}) %collective-permute-start.7) | collective-permute-done | bytes 829472 | tf_op jit(solution)/shard_map/ppermute | solution.py:288
  23.5 7.0 %dft.3 = (bf16[24,1792]{1,0:T(8,128)(2,1)S(1)}, bf16[24,1792]{1,0:T(8,128)(2,1)S(1)}, bf16[24,1792]{1,0:T(8,128)(2,1)S(1)}, bf16[24,1792]{1,0:T(8,128)(2,1)S(1)}...) custom-call(bf16[1752,1440]{1,0:T(8,128)(2,1)} %bitcast.21, ...), custom_call_target="tpu_custom_call" | custom-call | tf_op jit(solution)/shard_map/dft/pallas_call | solution.py:126
  30.5 1.8 %collective-permute-start.10 = (bf16[24,1792]{1,0:T(8,128)(2,1)S(1)}, bf16[24,1792]{1,0:T(8,128)(2,1)S(1)}, u32[]{:S(2)}, u32[]{:S(2)}) collective-permute-start(bf16[24,1792]{1,0:T(8,128)(2,1)S(1)} %get-tuple-element.39), channel_id=1, source_target_pairs={{0,1},{1,0},{2,3},{3,2},{4,5},{5,4},{6,7},{7,6},{8,9},{9,8},{10,11... | collective-permute-start | bytes 258056 | tf_op jit(solution)/shard_map/ppermute | solution.py:288
  32.3 1.6 %collective-permute-start.11 = (bf16[24,1792]{1,0:T(8,128)(2,1)S(1)}, bf16[24,1792]{1,0:T(8,128)(2,1)S(1)}, u32[]{:S(2)}, u32[]{:S(2)}) collective-permute-start(bf16[24,1792]{1,0:T(8,128)(2,1)S(1)} %get-tuple-element.40), channel_id=1, source_target_pairs={{0,2},{1,3},{2,0},{3,1},{4,6},{5,7},{6,4},{7,5},{8,10},{9,11},{10,... | collective-permute-start | bytes 258056 | tf_op jit(solution)/shard_map/ppermute | solution.py:288
  34.1 1.5 %collective-permute-done.10.rest_1_ = bf16[24,1792]{1,0:T(8,128)(2,1)S(1)} collective-permute-done((bf16[24,1792]{1,0:T(8,128)(2,1)S(1)}, bf16[24,1792]{1,0:T(8,128)(2,1)S(1)}, u32[]{:S(2)}, u32[]{:S(2)}) %collective-permute-start.10) | collective-permute-done | bytes 86048 | tf_op jit(solution)/shard_map/ppermute | solution.py:288
  35.5 2.8 %collective-permute-start.13 = (bf16[24,1792]{1,0:T(8,128)(2,1)S(1)}, bf16[24,1792]{1,0:T(8,128)(2,1)S(1)}, u32[]{:S(2)}, u32[]{:S(2)}) collective-permute-start(bf16[24,1792]{1,0:T(8,128)(2,1)S(1)} %get-tuple-element.42), channel_id=1, source_target_pairs={{0,4},{1,5},{2,6},{3,7},{4,0},{5,1},{6,2},{7,3},{8,12},{9,13},{10,... | collective-permute-start | bytes 258056 | tf_op jit(solution)/shard_map/ppermute | solution.py:288
  38.3 1.3 %collective-permute-start.14 = (bf16[24,1792]{1,0:T(8,128)(2,1)S(1)}, bf16[24,1792]{1,0:T(8,128)(2,1)S(1)}, u32[]{:S(2)}, u32[]{:S(2)}) collective-permute-start(bf16[24,1792]{1,0:T(8,128)(2,1)S(1)} %get-tuple-element.43), channel_id=1, source_target_pairs={{0,5},{1,4},{2,7},{3,6},{4,1},{5,0},{6,3},{7,2},{8,13},{9,12},{10,... | collective-permute-start | bytes 258056 | tf_op jit(solution)/shard_map/ppermute | solution.py:288
  39.6 3.6 %collective-permute-start.15 = (bf16[24,1792]{1,0:T(8,128)(2,1)S(1)}, bf16[24,1792]{1,0:T(8,128)(2,1)S(1)}, u32[]{:S(2)}, u32[]{:S(2)}) collective-permute-start(bf16[24,1792]{1,0:T(8,128)(2,1)S(1)} %get-tuple-element.44), channel_id=1, source_target_pairs={{0,6},{1,7},{2,4},{3,5},{4,2},{5,3},{6,0},{7,1},{8,14},{9,15},{10,... | collective-permute-start | bytes 258056 | tf_op jit(solution)/shard_map/ppermute | solution.py:288
  43.3 4.0 %dft.2 = (bf16[24,1792]{1,0:T(8,128)(2,1)S(1)}, bf16[24,1792]{1,0:T(8,128)(2,1)S(1)}, bf16[24,1792]{1,0:T(8,128)(2,1)S(1)}, bf16[24,1792]{1,0:T(8,128)(2,1)S(1)}...) custom-call(bf16[1752,1440]{1,0:T(8,128)(2,1)S(1)} %bitcast.17, ...), custom_call_target="tpu_custom_call" | custom-call | tf_op jit(solution)/shard_map/dft/pallas_call | solution.py:126
  47.2 3.6 %collective-permute-start.16 = (bf16[24,1792]{1,0:T(8,128)(2,1)S(1)}, bf16[24,1792]{1,0:T(8,128)(2,1)S(1)}, u32[]{:S(2)}, u32[]{:S(2)}) collective-permute-start(bf16[24,1792]{1,0:T(8,128)(2,1)S(1)} %get-tuple-element.45), channel_id=1, source_target_pairs={{0,7},{1,6},{2,5},{3,4},{4,3},{5,2},{6,1},{7,0},{8,15},{9,14},{10,... | collective-permute-start | bytes 258056 | tf_op jit(solution)/shard_map/ppermute | solution.py:288
  51.3 3.3 %collective-permute-done.16.rest_7_ = bf16[24,1792]{1,0:T(8,128)(2,1)S(1)} collective-permute-done((bf16[24,1792]{1,0:T(8,128)(2,1)S(1)}, bf16[24,1792]{1,0:T(8,128)(2,1)S(1)}, u32[]{:S(2)}, u32[]{:S(2)}) %collective-permute-start.16) | collective-permute-done | bytes 86048 | tf_op jit(solution)/shard_map/ppermute | solution.py:288
  55.8 3.5 %collective-permute-start.3 = (bf16[24,1792]{1,0:T(8,128)(2,1)S(1)}, bf16[24,1792]{1,0:T(8,128)(2,1)S(1)}, u32[]{:S(2)}, u32[]{:S(2)}) collective-permute-start(bf16[24,1792]{1,0:T(8,128)(2,1)S(1)} %get-tuple-element.30), channel_id=1, source_target_pairs={{0,4},{1,5},{2,6},{3,7},{4,0},{5,1},{6,2},{7,3},{8,12},{9,13},{10,... | collective-permute-start | bytes 258056 | tf_op jit(solution)/shard_map/ppermute | solution.py:288
  59.4 3.1 %collective-permute-start.5 = (bf16[24,1792]{1,0:T(8,128)(2,1)S(1)}, bf16[24,1792]{1,0:T(8,128)(2,1)S(1)}, u32[]{:S(2)}, u32[]{:S(2)}) collective-permute-start(bf16[24,1792]{1,0:T(8,128)(2,1)S(1)} %get-tuple-element.32), channel_id=1, source_target_pairs={{0,6},{1,7},{2,4},{3,5},{4,2},{5,3},{6,0},{7,1},{8,14},{9,15},{10,... | collective-permute-start | bytes 258056 | tf_op jit(solution)/shard_map/ppermute | solution.py:288
  62.5 1.7 %collective-permute-start.6 = (bf16[24,1792]{1,0:T(8,128)(2,1)S(1)}, bf16[24,1792]{1,0:T(8,128)(2,1)S(1)}, u32[]{:S(2)}, u32[]{:S(2)}) collective-permute-start(bf16[24,1792]{1,0:T(8,128)(2,1)S(1)} %get-tuple-element.33), channel_id=1, source_target_pairs={{0,7},{1,6},{2,5},{3,4},{4,3},{5,2},{6,1},{7,0},{8,15},{9,14},{10,... | collective-permute-start | bytes 258056 | tf_op jit(solution)/shard_map/ppermute | solution.py:288
  64.2 1.2 %turn.1 = (bf16[3,720,256]{2,1,0:T(8,128)(2,1)S(1)}, bf16[3,720,256]{2,1,0:T(8,128)(2,1)S(1)}, bf16[3,720,256]{2,1,0:T(8,128)(2,1)S(1)}, bf16[3,720,256]{2,1,0:T(8,128)(2,1)S(1)}) custom-call(bf16[3,192,720]{2,1,0:T(8,128)(2,1)S(1)} %bitcast.20, bf16[3,192,720]{2,1,0:T(8,128)(2,1)S(1)} %collective-permute-done.7.refs_1_, ...), custom_call_target="tpu_custom_call" | custom-call | tf_op jit(solution)/shard_map/turn/pallas_call | solution.py:153
  65.4 2.1 %legendre.2.rest_12_ = f32[60,8,128]{2,1,0:T(8,128)S(1)} custom-call(bf16[24,1792]{1,0:T(8,128)(2,1)S(1)} %get-tuple-element.38.rest_0_, bf16[24,1792]{1,0:T(8,128)(2,1)S(1)} %collective-permute-done.10.rest_1_, bf16[24,1792]{1,0:T(8,128)(2,1)S(1)} %collective-permute-done.11.rest_2_, bf16[24,1792]{1,0:T(8,128)(2,1)S(1)} %collective-permute-done.12.rest_3_, ...), custom_call_target="tpu_custom_call" | custom-call | tf_op jit(solution)/shard_map/legendre/pallas_call | solution.py:221
  67.5 2.1 %collective-permute-done.3.rest_4_ = bf16[24,1792]{1,0:T(8,128)(2,1)S(1)} collective-permute-done((bf16[24,1792]{1,0:T(8,128)(2,1)S(1)}, bf16[24,1792]{1,0:T(8,128)(2,1)S(1)}, u32[]{:S(2)}, u32[]{:S(2)}) %collective-permute-start.3) | collective-permute-done | bytes 86048 | tf_op jit(solution)/shard_map/ppermute | solution.py:288
  69.6 1.9 %collective-permute-done.4.rest_5_ = bf16[24,1792]{1,0:T(8,128)(2,1)S(1)} collective-permute-done((bf16[24,1792]{1,0:T(8,128)(2,1)S(1)}, bf16[24,1792]{1,0:T(8,128)(2,1)S(1)}, u32[]{:S(2)}, u32[]{:S(2)}) %collective-permute-start.4) | collective-permute-done | bytes 86048 | tf_op jit(solution)/shard_map/ppermute | solution.py:288
  71.4 2.1 %legendre.3 = (f32[60,8,128]{2,1,0:T(8,128)S(1)}, f32[60,8,128]{2,1,0:T(8,128)S(1)}) custom-call(bf16[24,1792]{1,0:T(8,128)(2,1)S(1)} %get-tuple-element.26.rest_0_, bf16[24,1792]{1,0:T(8,128)(2,1)S(1)} %collective-permute-done.rest_1_, bf16[24,1792]{1,0:T(8,128)(2,1)S(1)} %collective-permute-done.1.rest_2_, ...), custom_call_target="tpu_custom_call" | custom-call | tf_op jit(solution)/shard_map/legendre/pallas_call | solution.py:221
  73.6 1.5 %collective-permute-done.17 = f32[60,8,128]{2,1,0:T(8,128)S(1)} collective-permute-done((f32[60,8,128]{2,1,0:T(8,128)S(1)}, f32[60,8,128]{2,1,0:T(8,128)S(1)}, u32[]{:S(2)}, u32[]{:S(2)}) %collective-permute-start.17) | collective-permute-done | bytes 245792 | tf_op jit(solution)/shard_map/ppermute | solution.py:288
  75.1 2.4 %collective-permute-start.18 = (f32[15,8,128]{2,1,0:T(8,128)S(1)}, f32[15,8,128]{2,1,0:T(8,128)S(1)}, u32[]{:S(2)}, u32[]{:S(2)}) collective-permute-start(f32[15,8,128]{2,1,0:T(8,128)S(1)} %get-tuple-element.52), channel_id=1, source_target_pairs={{0,17},{1,16},{2,19},{3,18},{4,21},{5,20},{6,23},{7,22},{8,25},{9,... | collective-permute-start | bytes 184328 | tf_op jit(solution)/shard_map/ppermute | solution.py:309
  78.7 1.9 %collective-permute-done.18 = f32[15,8,128]{2,1,0:T(8,128)S(1)} collective-permute-done((f32[15,8,128]{2,1,0:T(8,128)S(1)}, f32[15,8,128]{2,1,0:T(8,128)S(1)}, u32[]{:S(2)}, u32[]{:S(2)}) %collective-permute-start.18) | collective-permute-done | bytes 61472 | tf_op jit(solution)/shard_map/ppermute | solution.py:309
  80.6 1.2 %collective-permute-done.19 = f32[15,8,128]{2,1,0:T(8,128)S(1)} collective-permute-done((f32[15,8,128]{2,1,0:T(8,128)S(1)}, f32[15,8,128]{2,1,0:T(8,128)S(1)}, u32[]{:S(2)}, u32[]{:S(2)}) %collective-permute-start.19) | collective-permute-done | bytes 61472 | tf_op jit(solution)/shard_map/ppermute | solution.py:309
  82.3 1.5 %collective-permute-start.21 = (f32[15,8,128]{2,1,0:T(8,128)S(1)}, f32[15,8,128]{2,1,0:T(8,128)S(1)}, u32[]{:S(2)}, u32[]{:S(2)}) collective-permute-start(f32[15,8,128]{2,1,0:T(8,128)S(1)} %fusion.1), channel_id=1, source_target_pairs={{0,6},{1,7},{2,4},{3,5},{4,2},{5,3},{6,0},{7,1},{8,14},{9,15},{10,... | collective-permute-start | bytes 184328 | tf_op jit(solution)/shard_map/ppermute | solution.py:288
  83.8 3.1 %collective-permute-start.22 = (f32[15,8,128]{2,1,0:T(8,128)S(1)}, f32[15,8,128]{2,1,0:T(8,128)S(1)}, u32[]{:S(2)}, u32[]{:S(2)}) collective-permute-start(f32[15,8,128]{2,1,0:T(8,128)S(1)} %fusion.1), channel_id=1, source_target_pairs={{0,4},{1,5},{2,6},{3,7},{4,0},{5,1},{6,2},{7,3},{8,12},{9,13},{10,... | collective-permute-start | bytes 184328 | tf_op jit(solution)/shard_map/ppermute | solution.py:288
  87.1 1.5 %collective-permute-done.21 = f32[15,8,128]{2,1,0:T(8,128)S(1)} collective-permute-done((f32[15,8,128]{2,1,0:T(8,128)S(1)}, f32[15,8,128]{2,1,0:T(8,128)S(1)}, u32[]{:S(2)}, u32[]{:S(2)}) %collective-permute-start.21) | collective-permute-done | bytes 61472 | tf_op jit(solution)/shard_map/ppermute | solution.py:288
  88.6 2.3 %collective-permute-done.22 = f32[15,8,128]{2,1,0:T(8,128)S(1)} collective-permute-done((f32[15,8,128]{2,1,0:T(8,128)S(1)}, f32[15,8,128]{2,1,0:T(8,128)S(1)}, u32[]{:S(2)}, u32[]{:S(2)}) %collective-permute-start.22) | collective-permute-done | bytes 61472 | tf_op jit(solution)/shard_map/ppermute | solution.py:288
  92.5 1.6 %collective-permute-start.25 = (f32[15,8,128]{2,1,0:T(8,128)S(1)}, f32[15,8,128]{2,1,0:T(8,128)S(1)}, u32[]{:S(2)}, u32[]{:S(2)}) collective-permute-start(f32[15,8,128]{2,1,0:T(8,128)S(1)} %add_add_fusion.refs_0_), channel_id=1, source_target_pairs={{0,16},{1,17},{2,18},{3,19},{4,20},{5,21},{6,22},{7,23},{8,24},{9,... | collective-permute-start | bytes 184328 | tf_op jit(solution)/shard_map/ppermute | solution.py:309
  95.0 1.2 %collective-permute-done.24.refs_1_ = f32[15,8,128]{2,1,0:T(8,128)S(1)} collective-permute-done((f32[15,8,128]{2,1,0:T(8,128)S(1)}, f32[15,8,128]{2,1,0:T(8,128)S(1)}, u32[]{:S(2)}, u32[]{:S(2)}) %collective-permute-start.24) | collective-permute-done | bytes 61472 | tf_op jit(solution)/shard_map/ppermute | solution.py:309
  96.7 2.5 %collective-permute-done.26.refs_3_ = f32[15,8,128]{2,1,0:T(8,128)S(1)} collective-permute-done((f32[15,8,128]{2,1,0:T(8,128)S(1)}, f32[15,8,128]{2,1,0:T(8,128)S(1)}, u32[]{:S(2)}, u32[]{:S(2)}) %collective-permute-start.26) | collective-permute-done | bytes 61472 | tf_op jit(solution)/shard_map/ppermute | solution.py:309
  99.3 1.2 %collective-permute-done.30.refs_7_ = f32[15,8,128]{2,1,0:T(8,128)S(1)} collective-permute-done((f32[15,8,128]{2,1,0:T(8,128)S(1)}, f32[15,8,128]{2,1,0:T(8,128)S(1)}, u32[]{:S(2)}, u32[]{:S(2)}) %collective-permute-start.30) | collective-permute-done | bytes 61472 | tf_op jit(solution)/shard_map/ppermute | solution.py:288
  (47 shorter events, 8.8 us)
Async XLA Ops:
  0.6 22.9 %collective-permute-start.7 = (bf16[3,192,720]{2,1,0:T(8,128)(2,1)}, bf16[3,192,720]{2,1,0:T(8,128)(2,1)S(1)}, u32[]{:S(2)}, u32[]{:S(2)}) collective-permute-start(bf16[3,192,720]{2,1,0:T(8,128)(2,1)} %bitcast.18), channel_id=1, source_target_pairs={{0,16},{8,24},{16,0},{24,8},{1,17},{9,25},{17,1},{25,9},{2,18},{10... | collective-permute-start | bytes 2488328 | tf_op jit(solution)/shard_map/ppermute | solution.py:288
  3.7 55.7 %collective-permute-start.8 = (bf16[3,192,720]{2,1,0:T(8,128)(2,1)}, bf16[3,192,720]{2,1,0:T(8,128)(2,1)S(1)}, u32[]{:S(2)}, u32[]{:S(2)}) collective-permute-start(bf16[3,192,720]{2,1,0:T(8,128)(2,1)} %bitcast.19), channel_id=1, source_target_pairs={{0,8},{8,0},{16,24},{24,16},{1,9},{9,1},{17,25},{25,17},{2,10},{10... | collective-permute-start | bytes 2488328 | tf_op jit(solution)/shard_map/ppermute | solution.py:288
  23.5 39.0 %collective-permute-start.9 = (bf16[3,192,720]{2,1,0:T(8,128)(2,1)S(1)}, bf16[3,192,720]{2,1,0:T(8,128)(2,1)S(1)}, u32[]{:S(2)}, u32[]{:S(2)}) collective-permute-start(bf16[3,192,720]{2,1,0:T(8,128)(2,1)S(1)} %collective-permute-done.7.refs_1_), channel_id=1, source_target_pairs={{0,8},{8,0},{16,24},{24,16},{1,9},{9,1},{17,25},{25,17},{2,10},{10... | collective-permute-start | bytes 2488328 | tf_op jit(solution)/shard_map/ppermute | solution.py:288
  30.5 5.0 %collective-permute-start.10 = (bf16[24,1792]{1,0:T(8,128)(2,1)S(1)}, bf16[24,1792]{1,0:T(8,128)(2,1)S(1)}, u32[]{:S(2)}, u32[]{:S(2)}) collective-permute-start(bf16[24,1792]{1,0:T(8,128)(2,1)S(1)} %get-tuple-element.39), channel_id=1, source_target_pairs={{0,1},{1,0},{2,3},{3,2},{4,5},{5,4},{6,7},{7,6},{8,9},{9,8},{10,11... | collective-permute-start | bytes 258056 | tf_op jit(solution)/shard_map/ppermute | solution.py:288
  32.3 6.0 %collective-permute-start.11 = (bf16[24,1792]{1,0:T(8,128)(2,1)S(1)}, bf16[24,1792]{1,0:T(8,128)(2,1)S(1)}, u32[]{:S(2)}, u32[]{:S(2)}) collective-permute-start(bf16[24,1792]{1,0:T(8,128)(2,1)S(1)} %get-tuple-element.40), channel_id=1, source_target_pairs={{0,2},{1,3},{2,0},{3,1},{4,6},{5,7},{6,4},{7,5},{8,10},{9,11},{10,... | collective-permute-start | bytes 258056 | tf_op jit(solution)/shard_map/ppermute | solution.py:288
  33.9 5.7 %collective-permute-start.12 = (bf16[24,1792]{1,0:T(8,128)(2,1)S(1)}, bf16[24,1792]{1,0:T(8,128)(2,1)S(1)}, u32[]{:S(2)}, u32[]{:S(2)}) collective-permute-start(bf16[24,1792]{1,0:T(8,128)(2,1)S(1)} %get-tuple-element.41), channel_id=1, source_target_pairs={{0,3},{1,2},{2,1},{3,0},{4,7},{5,6},{6,5},{7,4},{8,11},{9,10},{10,... | collective-permute-start | bytes 258056 | tf_op jit(solution)/shard_map/ppermute | solution.py:288
  35.5 11.7 %collective-permute-start.13 = (bf16[24,1792]{1,0:T(8,128)(2,1)S(1)}, bf16[24,1792]{1,0:T(8,128)(2,1)S(1)}, u32[]{:S(2)}, u32[]{:S(2)}) collective-permute-start(bf16[24,1792]{1,0:T(8,128)(2,1)S(1)} %get-tuple-element.42), channel_id=1, source_target_pairs={{0,4},{1,5},{2,6},{3,7},{4,0},{5,1},{6,2},{7,3},{8,12},{9,13},{10,... | collective-permute-start | bytes 258056 | tf_op jit(solution)/shard_map/ppermute | solution.py:288
  38.3 12.5 %collective-permute-start.14 = (bf16[24,1792]{1,0:T(8,128)(2,1)S(1)}, bf16[24,1792]{1,0:T(8,128)(2,1)S(1)}, u32[]{:S(2)}, u32[]{:S(2)}) collective-permute-start(bf16[24,1792]{1,0:T(8,128)(2,1)S(1)} %get-tuple-element.43), channel_id=1, source_target_pairs={{0,5},{1,4},{2,7},{3,6},{4,1},{5,0},{6,3},{7,2},{8,13},{9,12},{10,... | collective-permute-start | bytes 258056 | tf_op jit(solution)/shard_map/ppermute | solution.py:288
  39.6 11.7 %collective-permute-start.15 = (bf16[24,1792]{1,0:T(8,128)(2,1)S(1)}, bf16[24,1792]{1,0:T(8,128)(2,1)S(1)}, u32[]{:S(2)}, u32[]{:S(2)}) collective-permute-start(bf16[24,1792]{1,0:T(8,128)(2,1)S(1)} %get-tuple-element.44), channel_id=1, source_target_pairs={{0,6},{1,7},{2,4},{3,5},{4,2},{5,3},{6,0},{7,1},{8,14},{9,15},{10,... | collective-permute-start | bytes 258056 | tf_op jit(solution)/shard_map/ppermute | solution.py:288
  43.3 20.9 %copy-start.2 = (bf16[192,3,720]{2,0,1:T(8,128)(2,1)S(1)}, bf16[192,3,720]{2,0,1:T(8,128)(2,1)}, u32[]{:S(2)}) copy-start(bf16[192,3,720]{2,0,1:T(8,128)(2,1)} %param.6) | copy-start | bytes 2488324
  47.2 7.4 %collective-permute-start.16 = (bf16[24,1792]{1,0:T(8,128)(2,1)S(1)}, bf16[24,1792]{1,0:T(8,128)(2,1)S(1)}, u32[]{:S(2)}, u32[]{:S(2)}) collective-permute-start(bf16[24,1792]{1,0:T(8,128)(2,1)S(1)} %get-tuple-element.45), channel_id=1, source_target_pairs={{0,7},{1,6},{2,5},{3,4},{4,3},{5,2},{6,1},{7,0},{8,15},{9,14},{10,... | collective-permute-start | bytes 258056 | tf_op jit(solution)/shard_map/ppermute | solution.py:288
  50.8 5.0 %collective-permute-start = (bf16[24,1792]{1,0:T(8,128)(2,1)S(1)}, bf16[24,1792]{1,0:T(8,128)(2,1)S(1)}, u32[]{:S(2)}, u32[]{:S(2)}) collective-permute-start(bf16[24,1792]{1,0:T(8,128)(2,1)S(1)} %get-tuple-element.27), channel_id=1, source_target_pairs={{0,1},{1,0},{2,3},{3,2},{4,5},{5,4},{6,7},{7,6},{8,9},{9,8},{10,11... | collective-permute-start | bytes 258056 | tf_op jit(solution)/shard_map/ppermute | solution.py:288
  51.3 8.0 %collective-permute-start.1 = (bf16[24,1792]{1,0:T(8,128)(2,1)S(1)}, bf16[24,1792]{1,0:T(8,128)(2,1)S(1)}, u32[]{:S(2)}, u32[]{:S(2)}) collective-permute-start(bf16[24,1792]{1,0:T(8,128)(2,1)S(1)} %get-tuple-element.28), channel_id=1, source_target_pairs={{0,2},{1,3},{2,0},{3,1},{4,6},{5,7},{6,4},{7,5},{8,10},{9,11},{10,... | collective-permute-start | bytes 258056 | tf_op jit(solution)/shard_map/ppermute | solution.py:288
  54.6 12.9 %collective-permute-start.2 = (bf16[24,1792]{1,0:T(8,128)(2,1)S(1)}, bf16[24,1792]{1,0:T(8,128)(2,1)S(1)}, u32[]{:S(2)}, u32[]{:S(2)}) collective-permute-start(bf16[24,1792]{1,0:T(8,128)(2,1)S(1)} %get-tuple-element.29), channel_id=1, source_target_pairs={{0,3},{1,2},{2,1},{3,0},{4,7},{5,6},{6,5},{7,4},{8,11},{9,10},{10,... | collective-permute-start | bytes 258056 | tf_op jit(solution)/shard_map/ppermute | solution.py:288
  55.8 13.7 %collective-permute-start.3 = (bf16[24,1792]{1,0:T(8,128)(2,1)S(1)}, bf16[24,1792]{1,0:T(8,128)(2,1)S(1)}, u32[]{:S(2)}, u32[]{:S(2)}) collective-permute-start(bf16[24,1792]{1,0:T(8,128)(2,1)S(1)} %get-tuple-element.30), channel_id=1, source_target_pairs={{0,4},{1,5},{2,6},{3,7},{4,0},{5,1},{6,2},{7,3},{8,12},{9,13},{10,... | collective-permute-start | bytes 258056 | tf_op jit(solution)/shard_map/ppermute | solution.py:288
  59.4 12.0 %collective-permute-start.4 = (bf16[24,1792]{1,0:T(8,128)(2,1)S(1)}, bf16[24,1792]{1,0:T(8,128)(2,1)S(1)}, u32[]{:S(2)}, u32[]{:S(2)}) collective-permute-start(bf16[24,1792]{1,0:T(8,128)(2,1)S(1)} %get-tuple-element.31), channel_id=1, source_target_pairs={{0,5},{1,4},{2,7},{3,6},{4,1},{5,0},{6,3},{7,2},{8,13},{9,12},{10,... | collective-permute-start | bytes 258056 | tf_op jit(solution)/shard_map/ppermute | solution.py:288
  59.4 12.0 %collective-permute-start.5 = (bf16[24,1792]{1,0:T(8,128)(2,1)S(1)}, bf16[24,1792]{1,0:T(8,128)(2,1)S(1)}, u32[]{:S(2)}, u32[]{:S(2)}) collective-permute-start(bf16[24,1792]{1,0:T(8,128)(2,1)S(1)} %get-tuple-element.32), channel_id=1, source_target_pairs={{0,6},{1,7},{2,4},{3,5},{4,2},{5,3},{6,0},{7,1},{8,14},{9,15},{10,... | collective-permute-start | bytes 258056 | tf_op jit(solution)/shard_map/ppermute | solution.py:288
  62.5 8.9 %collective-permute-start.6 = (bf16[24,1792]{1,0:T(8,128)(2,1)S(1)}, bf16[24,1792]{1,0:T(8,128)(2,1)S(1)}, u32[]{:S(2)}, u32[]{:S(2)}) collective-permute-start(bf16[24,1792]{1,0:T(8,128)(2,1)S(1)} %get-tuple-element.33), channel_id=1, source_target_pairs={{0,7},{1,6},{2,5},{3,4},{4,3},{5,2},{6,1},{7,0},{8,15},{9,14},{10,... | collective-permute-start | bytes 258056 | tf_op jit(solution)/shard_map/ppermute | solution.py:288
  73.5 1.6 %collective-permute-start.17 = (f32[60,8,128]{2,1,0:T(8,128)S(1)}, f32[60,8,128]{2,1,0:T(8,128)S(1)}, u32[]{:S(2)}, u32[]{:S(2)}) collective-permute-start(f32[60,8,128]{2,1,0:T(8,128)S(1)} %get-tuple-element.47), channel_id=1, source_target_pairs={{0,8},{8,0},{16,24},{24,16},{1,9},{9,1},{17,25},{25,17},{2,10},{10... | collective-permute-start | bytes 737288 | tf_op jit(solution)/shard_map/ppermute | solution.py:288
  75.1 5.5 %collective-permute-start.18 = (f32[15,8,128]{2,1,0:T(8,128)S(1)}, f32[15,8,128]{2,1,0:T(8,128)S(1)}, u32[]{:S(2)}, u32[]{:S(2)}) collective-permute-start(f32[15,8,128]{2,1,0:T(8,128)S(1)} %get-tuple-element.52), channel_id=1, source_target_pairs={{0,17},{1,16},{2,19},{3,18},{4,21},{5,20},{6,23},{7,22},{8,25},{9,... | collective-permute-start | bytes 184328 | tf_op jit(solution)/shard_map/ppermute | solution.py:309
  77.6 4.2 %collective-permute-start.19 = (f32[15,8,128]{2,1,0:T(8,128)S(1)}, f32[15,8,128]{2,1,0:T(8,128)S(1)}, u32[]{:S(2)}, u32[]{:S(2)}) collective-permute-start(f32[15,8,128]{2,1,0:T(8,128)S(1)} %get-tuple-element.54), channel_id=1, source_target_pairs={{0,16},{1,17},{2,18},{3,19},{4,20},{5,21},{6,22},{7,23},{8,24},{9,... | collective-permute-start | bytes 184328 | tf_op jit(solution)/shard_map/ppermute | solution.py:309
  78.1 4.2 %collective-permute-start.20 = (f32[15,8,128]{2,1,0:T(8,128)S(1)}, f32[15,8,128]{2,1,0:T(8,128)S(1)}, u32[]{:S(2)}, u32[]{:S(2)}) collective-permute-start(f32[15,8,128]{2,1,0:T(8,128)S(1)} %get-tuple-element.53), channel_id=1, source_target_pairs={{0,1},{1,0},{2,3},{3,2},{4,5},{5,4},{6,7},{7,6},{8,9},{9,8},{10,11... | collective-permute-start | bytes 184328 | tf_op jit(solution)/shard_map/ppermute | solution.py:309
  82.3 6.2 %collective-permute-start.21 = (f32[15,8,128]{2,1,0:T(8,128)S(1)}, f32[15,8,128]{2,1,0:T(8,128)S(1)}, u32[]{:S(2)}, u32[]{:S(2)}) collective-permute-start(f32[15,8,128]{2,1,0:T(8,128)S(1)} %fusion.1), channel_id=1, source_target_pairs={{0,6},{1,7},{2,4},{3,5},{4,2},{5,3},{6,0},{7,1},{8,14},{9,15},{10,... | collective-permute-start | bytes 184328 | tf_op jit(solution)/shard_map/ppermute | solution.py:288
  83.8 7.0 %collective-permute-start.22 = (f32[15,8,128]{2,1,0:T(8,128)S(1)}, f32[15,8,128]{2,1,0:T(8,128)S(1)}, u32[]{:S(2)}, u32[]{:S(2)}) collective-permute-start(f32[15,8,128]{2,1,0:T(8,128)S(1)} %fusion.1), channel_id=1, source_target_pairs={{0,4},{1,5},{2,6},{3,7},{4,0},{5,1},{6,2},{7,3},{8,12},{9,13},{10,... | collective-permute-start | bytes 184328 | tf_op jit(solution)/shard_map/ppermute | solution.py:288
  86.9 4.6 %collective-permute-start.23 = (f32[15,8,128]{2,1,0:T(8,128)S(1)}, f32[15,8,128]{2,1,0:T(8,128)S(1)}, u32[]{:S(2)}, u32[]{:S(2)}) collective-permute-start(f32[15,8,128]{2,1,0:T(8,128)S(1)} %fusion.1), channel_id=1, source_target_pairs={{0,2},{1,3},{2,0},{3,1},{4,6},{5,7},{6,4},{7,5},{8,10},{9,11},{10,... | collective-permute-start | bytes 184328 | tf_op jit(solution)/shard_map/ppermute | solution.py:288
  91.5 4.7 %collective-permute-start.24 = (f32[15,8,128]{2,1,0:T(8,128)S(1)}, f32[15,8,128]{2,1,0:T(8,128)S(1)}, u32[]{:S(2)}, u32[]{:S(2)}) collective-permute-start(f32[15,8,128]{2,1,0:T(8,128)S(1)} %add_add_fusion.refs_0_), channel_id=1, source_target_pairs={{0,1},{1,0},{2,3},{3,2},{4,5},{5,4},{6,7},{7,6},{8,9},{9,8},{10,11... | collective-permute-start | bytes 184328 | tf_op jit(solution)/shard_map/ppermute | solution.py:309
  92.5 4.2 %collective-permute-start.25 = (f32[15,8,128]{2,1,0:T(8,128)S(1)}, f32[15,8,128]{2,1,0:T(8,128)S(1)}, u32[]{:S(2)}, u32[]{:S(2)}) collective-permute-start(f32[15,8,128]{2,1,0:T(8,128)S(1)} %add_add_fusion.refs_0_), channel_id=1, source_target_pairs={{0,16},{1,17},{2,18},{3,19},{4,20},{5,21},{6,22},{7,23},{8,24},{9,... | collective-permute-start | bytes 184328 | tf_op jit(solution)/shard_map/ppermute | solution.py:309
  94.1 5.1 %collective-permute-start.26 = (f32[15,8,128]{2,1,0:T(8,128)S(1)}, f32[15,8,128]{2,1,0:T(8,128)S(1)}, u32[]{:S(2)}, u32[]{:S(2)}) collective-permute-start(f32[15,8,128]{2,1,0:T(8,128)S(1)} %add_add_fusion.refs_0_), channel_id=1, source_target_pairs={{0,17},{1,16},{2,19},{3,18},{4,21},{5,20},{6,23},{7,22},{8,25},{9,... | collective-permute-start | bytes 184328 | tf_op jit(solution)/shard_map/ppermute | solution.py:309
  95.0 4.2 %collective-permute-start.27 = (f32[15,8,128]{2,1,0:T(8,128)S(1)}, f32[15,8,128]{2,1,0:T(8,128)S(1)}, u32[]{:S(2)}, u32[]{:S(2)}) collective-permute-start(f32[15,8,128]{2,1,0:T(8,128)S(1)} %add_add_fusion.refs_0_), channel_id=1, source_target_pairs={{0,8},{8,0},{16,24},{24,16},{1,9},{9,1},{17,25},{25,17},{2,10},{10... | collective-permute-start | bytes 184328 | tf_op jit(solution)/shard_map/ppermute | solution.py:288
  96.2 3.0 %collective-permute-start.28 = (f32[15,8,128]{2,1,0:T(8,128)S(1)}, f32[15,8,128]{2,1,0:T(8,128)S(1)}, u32[]{:S(2)}, u32[]{:S(2)}) collective-permute-start(f32[15,8,128]{2,1,0:T(8,128)S(1)} %collective-permute-done.24.refs_1_), channel_id=1, source_target_pairs={{0,8},{8,0},{16,24},{24,16},{1,9},{9,1},{17,25},{25,17},{2,10},{10... | collective-permute-start | bytes 184328 | tf_op jit(solution)/shard_map/ppermute | solution.py:288
  96.7 2.5 %collective-permute-start.29 = (f32[15,8,128]{2,1,0:T(8,128)S(1)}, f32[15,8,128]{2,1,0:T(8,128)S(1)}, u32[]{:S(2)}, u32[]{:S(2)}) collective-permute-start(f32[15,8,128]{2,1,0:T(8,128)S(1)} %collective-permute-done.25.refs_2_), channel_id=1, source_target_pairs={{0,8},{8,0},{16,24},{24,16},{1,9},{9,1},{17,25},{25,17},{2,10},{10... | collective-permute-start | bytes 184328 | tf_op jit(solution)/shard_map/ppermute | solution.py:288
  99.2 1.2 %collective-permute-start.30 = (f32[15,8,128]{2,1,0:T(8,128)S(1)}, f32[15,8,128]{2,1,0:T(8,128)S(1)}, u32[]{:S(2)}, u32[]{:S(2)}) collective-permute-start(f32[15,8,128]{2,1,0:T(8,128)S(1)} %collective-permute-done.26.refs_3_), channel_id=1, source_target_pairs={{0,8},{8,0},{16,24},{24,16},{1,9},{9,1},{17,25},{25,17},{2,10},{10... | collective-permute-start | bytes 184328 | tf_op jit(solution)/shard_map/ppermute | solution.py:288
  (2 other events, 39.4 us)

commit v5 on v4

--- a/solution.py
+++ b/solution.py
@@ -11,6 +11,7 @@
 
 
 LANES = 128
+SPARE_VMEM = 16 * 1024 * 1024
 VMEM_LIMIT = 24 * 1024 * 1024
 STAGED_LIMIT = 53 * 1024 * 1024
 DIRECT_LIMIT = 44 * 1024 * 1024
@@ -105,6 +106,61 @@
         outs[s][...] = packed[s].astype(jnp.bfloat16)
 
 
+def rows_kernel(bands, per, chunks, field, table_hbm, *rest):
+    outs = rest[:bands]
+    dscr, turned, xbuf, table, sems = rest[bands:]
+    load = pltpu.make_async_copy(table_hbm, table, sems.at[len(chunks)])
+    load.start()
+    copies = []
+    row = 0
+    for i, rows in enumerate(chunks):
+        cp = pltpu.make_async_copy(
+            field.at[pl.ds(row, rows), :], xbuf.at[pl.ds(row, rows), :], sems.at[i]
+        )
+        cp.start()
+        copies.append((row, rows, cp))
+        row += rows
+    load.wait()
+    tiles = dscr.shape[0]
+    for row, rows, cp in copies:
+        cp.wait()
+        res = jnp.dot(xbuf[pl.ds(row, rows), :], table[...], preferred_element_type=jnp.float32)
+        for q in range(tiles):
+            dscr[q, pl.ds(row, rows), :] = res[:, q * LANES : (q + 1) * LANES]
+            for start in range(row, row + rows, LANES):
+                block = dscr[q, pl.ds(start, LANES), :]
+                turned[pl.ds(q * LANES, LANES), pl.ds(start, LANES)] = block.T
+    band = lax.axis_index("lat")
+    for s in range(bands):
+        start = pl.multiple_of(target_of(band, bands, s) * per, 8)
+        outs[s][...] = turned[pl.ds(start, per), :].astype(jnp.bfloat16)
+
+
+def row_blocks(field, table, bands, per):
+    rows_all, lon_count = field.shape
+    width = round_up(rows_all, LANES)
+    columns = table.shape[1]
+    step = 4 * LANES
+    chunks = [min(step, rows_all - row) for row in range(0, rows_all, step)]
+    anywhere = pl.BlockSpec(memory_space=pl.ANY)
+    vmem = pl.BlockSpec(memory_space=pltpu.VMEM)
+    return pl.pallas_call(
+        functools.partial(rows_kernel, bands, per, tuple(chunks)),
+        out_shape=[jax.ShapeDtypeStruct((per, width), jnp.bfloat16)] * bands,
+        in_specs=[anywhere] * 2,
+        out_specs=[vmem] * bands,
+        scratch_shapes=[
+            pltpu.VMEM((columns // LANES, width, LANES), jnp.float32),
+            pltpu.VMEM((columns, width), jnp.float32),
+            pltpu.VMEM((rows_all, lon_count), jnp.bfloat16),
+            pltpu.VMEM(table.shape, jnp.bfloat16),
+            pltpu.SemaphoreType.DMA((len(chunks) + 1,)),
+        ],
+        compiler_params=pltpu.CompilerParams(vmem_limit_bytes=STAGED_LIMIT),
+        name="dft_rows",
+    )(field, table)
+
+
 def dft_blocks(field, table, staged, bands, per, chans, lats):
     rows_all, lon_count = field.shape
     width = round_up(per * chans, LANES)
@@ -158,24 +214,74 @@
     )(*bases)
 
 
+def prepare_kernel(bands, lats, chans, *refs):
+    blocks, (columns, rows, flat, planes) = refs[:bands], refs[bands:]
+    band = lax.axis_index("lat")
+    per, width = blocks[0].shape
+    fit = LANES // per
+    depth = bands * lats
+    for s in range(bands):
+        source = source_of(band, bands, s)
+        start = pl.multiple_of(source // fit * LANES + lax.rem(source, fit) * per, 8)
+        rows[pl.ds(start, per), :] = blocks[s][...].astype(jnp.float32)
+    tiles = flat.shape[0]
+    for q in range(tiles):
+        for start in range(0, width, LANES):
+            block = rows[pl.ds(q * LANES, LANES), pl.ds(start, LANES)]
+            flat[q, pl.ds(start, LANES), :] = block.T
+    for q in range(tiles):
+        for n in range(lats):
+            block = flat.at[q][pl.ds(n, round_up(chans, 8), stride=lats), :].T
+            for k in range(min(fit, bands - q * fit)):
+                place = pl.ds((q * fit + k) * lats + n, per, stride=depth)
+                planes[place, :] = jnp.pad(
+                    block[k * per : (k + 1) * per, :], ((0, 0), (0, LANES - block.shape[1]))
+                )
+    for i in range(per // 2):
+        for p in range(2):
+            piece = planes[pl.ds((2 * i + p) * depth, depth), pl.ds(0, chans)]
+            columns[i, :, pl.ds(p * chans, chans)] = piece.astype(jnp.bfloat16)
+
+
+def prepared_columns(blocks, lats, chans):
+    bands = len(blocks)
+    per, width = blocks[0].shape
+    tiles = -(-bands // (LANES // per))
+    shape = (per // 2, bands * lats, 2 * chans)
+    held = 4 * LANES * (tiles * (width + LANES * lats) + per * bands * lats)
+    return pl.pallas_call(
+        functools.partial(prepare_kernel, bands, lats, chans),
+        out_shape=jax.ShapeDtypeStruct(shape, jnp.bfloat16),
+        scratch_shapes=[
+            pltpu.VMEM((tiles * LANES, width), jnp.float32),
+            pltpu.VMEM((tiles, LANES * lats, LANES), jnp.float32),
+            pltpu.VMEM((per * bands * lats, LANES), jnp.float32),
+        ],
+        compiler_params=pltpu.CompilerParams(vmem_limit_bytes=SPARE_VMEM + held),
+        name="prepare",
+    )(*blocks)
+
+
 def legendre_kernel(bands, groups, per_dev, chans, lats, slots, field, *rest):
-    blocks = rest[:bands]
-    bases = rest[bands : bands + groups]
-    rest = rest[bands + groups :]
-    fourier, columns, total = rest[-3:]
+    inputs = bands if field else 1
+    blocks = rest[:inputs]
+    bases = rest[inputs : inputs + groups]
+    rest = rest[inputs + groups :]
+    total = rest[-1]
     if field == 0:
-        out = rest[0]
+        out, columns = rest[0], blocks[0]
     else:
-        energy_before, kept, sent, out = rest[0], rest[1], rest[2], rest[3]
+        energy_before, kept, sent, out, fourier, columns = rest[:6]
     band, group = lax.axis_index("lat"), lax.axis_index("batch")
     degrees = bases[0].shape[1]
     depth = bands * lats
     width = 2 * chans
-    for s in range(bands):
-        row = pl.multiple_of(source_of(band, bands, s) * lats, 8)
-        fourier[pl.ds(row, lats), :] = blocks[s][...].astype(jnp.float32)
-    for i in range(groups * per_dev):
-        columns[i] = fourier[:, pl.ds(i * width, width)].astype(jnp.bfloat16)
+    if field:
+        for s in range(bands):
+            row = pl.multiple_of(source_of(band, bands, s) * lats, 8)
+            fourier[pl.ds(row, lats), :] = blocks[s][...].astype(jnp.float32)
+        for i in range(groups * per_dev):
+            columns[i] = fourier[:, pl.ds(i * width, width)].astype(jnp.bfloat16)
     for q in range(groups):
         owner = jnp.bitwise_xor(group, slots[q])
         first = jnp.where(jnp.logical_and(band == 0, owner == 0), 1.0, 2.0)
@@ -210,23 +316,24 @@
         sent[...] = jnp.where(high, first, second)
 
 
-def legendre_energy(blocks, bases, slots, chans, lats, before):
-    bands, groups = len(blocks), len(bases)
+def legendre_energy(blocks, bases, slots, chans, lats, bands, before):
+    groups = len(bases)
     per_dev, degrees, _ = bases[0].shape
     row_tiles = round_up(chans, 8) // 8
     lane_tiles = round_up(degrees, LANES) // LANES
     tiles = (row_tiles * lane_tiles, 8, LANES)
     field = len(before)
     out = jax.ShapeDtypeStruct(tiles, jnp.float32)
+    staging = [
+        pltpu.VMEM(tiles, jnp.float32),
+        pltpu.VMEM((bands * lats, blocks[0].shape[-1]), jnp.float32),
+        pltpu.VMEM((groups * per_dev, bands * lats, 2 * chans), jnp.bfloat16),
+    ]
     return pl.pallas_call(
         functools.partial(legendre_kernel, bands, groups, per_dev, chans, lats, slots, field),
         out_shape=[out, out] if field else [out],
-        scratch_shapes=([pltpu.VMEM(tiles, jnp.float32)] if field else [])
-        + [
-            pltpu.VMEM((bands * lats, blocks[0].shape[-1]), jnp.float32),
-            pltpu.VMEM((groups * per_dev, bands * lats, 2 * chans), jnp.bfloat16),
-            pltpu.VMEM((degrees, round_up(2 * chans, LANES)), jnp.float32),
-        ],
+        scratch_shapes=(staging if field else [])
+        + [pltpu.VMEM((degrees, round_up(2 * chans, LANES)), jnp.float32)],
         compiler_params=pltpu.CompilerParams(vmem_limit_bytes=VMEM_LIMIT),
         name="legendre",
     )(*blocks, *bases, *before)
@@ -253,8 +360,8 @@
             lanes = min(LANES, degrees - k * LANES)
             first = fields[0, r * lane_tiles + k]
             second = fields[1, r * lane_tiles + k]
-            spectra[0, pl.ds(r * 8, rows), pl.ds(k * LANES, lanes)] = first[:rows, :lanes]
-            spectra[1, pl.ds(r * 8, rows), pl.ds(k * LANES, lanes)] = second[:rows, :lanes]
+            spectra[pl.ds(r * 8, rows), 0, pl.ds(k * LANES, lanes)] = first[:rows, :lanes]
+            spectra[pl.ds(r * 8, rows), 1, pl.ds(k * LANES, lanes)] = second[:rows, :lanes]
             gap = jnp.log(first + 1e-06) - jnp.log(second + 1e-06)
             gap = gap * gap
             if lanes < LANES:
@@ -272,7 +379,7 @@
     return pl.pallas_call(
         functools.partial(loss_kernel, chans, degrees, count, mesh_size),
         out_shape=(
-            jax.ShapeDtypeStruct((2, chans, degrees), jnp.float32),
+            jax.ShapeDtypeStruct((chans, 2, degrees), jnp.float32),
             jax.ShapeDtypeStruct((1, chans), jnp.float32),
         ),
         scratch_shapes=[
@@ -318,7 +425,8 @@
     value = lax.dynamic_index_in_dim(pieces, mine, 0, keepdims=False)
     for m in range(len(steps) - 1, 0, -1):
         piece = lax.dynamic_index_in_dim(pieces, jnp.bitwise_xor(mine, m), 0, keepdims=False)
-        value = value + flat_exchange(piece, mesh_size, steps[m])
+        piece = flat_exchange(piece, mesh_size, steps[m])
+        value = value + piece
     step = 4
     while step < groups:
         value = value + exchange(value, "batch", step)
@@ -330,7 +438,9 @@
         value = value + sum(parts[1:], parts[0])
         step *= radix
         radix = 4
-    owned = [flat_exchange(value, mesh_size, step) if step else value for step in steps]
+    owned = [value]
+    for m in range(1, len(steps)):
+        owned.append(flat_exchange(value, mesh_size, steps[m]))
     return owned, [exchange(piece, "batch", 1) for piece in owned]
 
 
@@ -353,6 +463,8 @@
 
     def transform(field, staged):
         flat = field.reshape(rows, lon_count)
+        if staged:
+            return row_blocks(flat, table, bands, groups * per_dev * 2)
         return dft_blocks(flat, table, staged, bands, groups * per_dev * 2, chans, lats)
 
     first = transform(predicted, True)
@@ -361,16 +473,16 @@
     for s in far + near:
         got0[s] = exchange(first[s], "lat", s)
         got1[s] = exchange(second[s], "lat", s)
+    columns = prepared_columns([got0[s] for s in range(bands)], lats, chans)
     bases = turned_bases(bases)
-    blocks = [got0[s] for s in range(bands)]
-    before = legendre_energy(blocks, bases, slots, chans, lats, [])
+    before = legendre_energy([columns], bases, slots, chans, lats, bands, [])
     blocks = [got1[s] for s in range(bands)]
-    kept, sent = legendre_energy(blocks, bases, slots, chans, lats, before)
+    kept, sent = legendre_energy(blocks, bases, slots, chans, lats, bands, before)
     owned, other = reduce_all(kept, sent)
     spectra, loss = loss_call(
         owned, other, chans, degrees, members * groups * groups * bands * per_dev
     )
-    return (spectra, loss.reshape(chans))
+    return (jnp.transpose(spectra, (1, 0, 2)), loss.reshape(chans))
 
 
 def reach(bands):

time: 102 us -> 106 us (1.039)
  local copies, waits for them, and re-layouts: 1.15 us -> 3.67 us
  waiting for transfers between devices: 44 us -> 45.6 us
  starting transfers between devices: 39.3 us -> 37.9 us
    pallas_call x0 -> x2, Pallas kernels: none -> 8.16 us  [the longest x1 5.32 us: row_blocks(): pl.pallas_call(functools.partial(rows_kernel, bands, per, tuple(chunks)),...]
    pallas_call x2 -> x1, Pallas kernels: 10.9 us -> 3.79 us  [dft_blocks(): pl.pallas_call(functools.partial(dft_kernel, bands, per, chans, lats, tup...]
    unnamed x7 -> x6, local copies, waits for them, and re-layouts: 1.12 us -> 3.65 us
    ppermute x25, waiting for transfers between devices: 36.2 us -> 38.1 us  [exchange(): return lax.ppermute(value, axis, peers(lax.axis_size(axis), step))]
    ppermute x25, starting transfers between devices: 32.2 us -> 30.8 us  [exchange(): return lax.ppermute(value, axis, peers(lax.axis_size(axis), step))]
  transfers between devices with their start and end apart: 31 -> 31, of which waited for: 17 -> 16; matrix products, arithmetic and copies ran while one was open for 0% -> 0% of each run, Pallas kernels for 14% -> 14%
where the time goes in v5:
time: 106 us
  waiting for transfers between devices  45.6 us (43%)
  starting transfers between devices  37.9 us (36%)
  Pallas kernels  18.1 us (17%)
  local copies, waits for them, and re-layouts  3.67 us (3%)
    ppermute x25, waiting for transfers between devices, exchange(): return lax.ppermute(value, axis, peers(lax.axis_size(axis), step))  38.1 us
    ppermute x25, starting transfers between devices, exchange(): return lax.ppermute(value, axis, peers(lax.axis_size(axis), step))  30.8 us
    ppermute x6, waiting for transfers between devices, flat_exchange(): lax.ppermute(value, ('batch', 'lat'), [(i, i ^ step) for i in range(count)])  7.44 us
    ppermute x6, starting transfers between devices, flat_exchange(): lax.ppermute(value, ('batch', 'lat'), [(i, i ^ step) for i in range(count)])  7.11 us
    pallas_call x1, Pallas kernels, row_blocks(): pl.pallas_call(functools.partial(rows_kernel, bands, per, tuple(chunks)),...  5.32 us
    pallas_call x1, Pallas kernels, dft_blocks(): pl.pallas_call(functools.partial(dft_kernel, bands, per, chans, lats, tup...  3.79 us
    pallas_call x2, Pallas kernels, legendre_energy(): pl.pallas_call(functools.partial(legendre_kernel, bands, groups, per_dev,...  3.76 us
    unnamed x6, local copies, waits for them, and re-layouts  3.65 us
  transfers between devices with their start and end apart: 31, of which 16 were waited for; matrix products, arithmetic and copies ran while one was open for 0% of the time, Pallas kernels for 14%

profile of v5, /device:TPU:0, one launch (start us, length us, event | category | flops | bytes accessed | tf_op | source)
XLA Modules:
  0.0 106.1 jit_solution(532867790245403891)
XLA Ops:
  0.6 3.0 %collective-permute-start.7 = (bf16[3,192,720]{2,1,0:T(8,128)(2,1)}, bf16[3,192,720]{2,1,0:T(8,128)(2,1)S(1)}, u32[]{:S(2)}, u32[]{:S(2)}) collective-permute-start(bf16[3,192,720]{2,1,0:T(8,128)(2,1)} %bitcast.19), channel_id=1, source_target_pairs={{0,16},{8,24},{16,0},{24,8},{1,17},{9,25},{17,1},{25,9},{2,18},{10... | collective-permute-start | bytes 2488328 | tf_op jit(solution)/shard_map/ppermute | solution.py:395
  3.7 19.9 %collective-permute-done.7.refs_1_ = bf16[3,192,720]{2,1,0:T(8,128)(2,1)S(1)} collective-permute-done((bf16[3,192,720]{2,1,0:T(8,128)(2,1)}, bf16[3,192,720]{2,1,0:T(8,128)(2,1)S(1)}, u32[]{:S(2)}, u32[]{:S(2)}) %collective-permute-start.7) | collective-permute-done | bytes 829472 | tf_op jit(solution)/shard_map/ppermute | solution.py:395
  23.5 2.5 %copy-done = bf16[1,73,24,1440]{3,2,1,0:T(8,128)(2,1)S(1)} copy-done((bf16[1,73,24,1440]{3,2,1,0:T(8,128)(2,1)S(1)}, bf16[1,73,24,1440]{3,2,1,0:T(8,128)(2,1)}, u32[]{:S(2)}) %copy-start) | copy-done | bytes 5045784
  27.2 3.8 %dft.1 = (bf16[24,1792]{1,0:T(8,128)(2,1)S(1)}, bf16[24,1792]{1,0:T(8,128)(2,1)S(1)}, bf16[24,1792]{1,0:T(8,128)(2,1)S(1)}, bf16[24,1792]{1,0:T(8,128)(2,1)S(1)}...) custom-call(bf16[1752,1440]{1,0:T(8,128)(2,1)S(1)} %bitcast.18, ...), custom_call_target="tpu_custom_call" | custom-call | tf_op jit(solution)/shard_map/dft/pallas_call | solution.py:182
  31.0 1.8 %collective-permute-start = (bf16[24,1792]{1,0:T(8,128)(2,1)S(1)}, bf16[24,1792]{1,0:T(8,128)(2,1)S(1)}, u32[]{:S(2)}, u32[]{:S(2)}) collective-permute-start(bf16[24,1792]{1,0:T(8,128)(2,1)S(1)} %get-tuple-element.27), channel_id=1, source_target_pairs={{0,1},{1,0},{2,3},{3,2},{4,5},{5,4},{6,7},{7,6},{8,9},{9,8},{10,11... | collective-permute-start | bytes 258056 | tf_op jit(solution)/shard_map/ppermute | solution.py:395
  32.8 1.6 %collective-permute-start.1 = (bf16[24,1792]{1,0:T(8,128)(2,1)S(1)}, bf16[24,1792]{1,0:T(8,128)(2,1)S(1)}, u32[]{:S(2)}, u32[]{:S(2)}) collective-permute-start(bf16[24,1792]{1,0:T(8,128)(2,1)S(1)} %get-tuple-element.28), channel_id=1, source_target_pairs={{0,2},{1,3},{2,0},{3,1},{4,6},{5,7},{6,4},{7,5},{8,10},{9,11},{10,... | collective-permute-start | bytes 258056 | tf_op jit(solution)/shard_map/ppermute | solution.py:395
  34.4 5.3 %dft_rows.1 = (bf16[24,1792]{1,0:T(8,128)(2,1)S(1)}, bf16[24,1792]{1,0:T(8,128)(2,1)S(1)}, bf16[24,1792]{1,0:T(8,128)(2,1)S(1)}, bf16[24,1792]{1,0:T(8,128)(2,1)...) custom-call(bf16[1752,1440]{1,0:T(8,128)(2,1)} %bitcast.22, ...), custom_call_target="tpu_custom_call" | custom-call | tf_op jit(solution)/shard_map/dft_rows/pallas_call | solution.py:147
  40.5 2.8 %collective-permute-start.12 = (bf16[24,1792]{1,0:T(8,128)(2,1)S(1)}, bf16[24,1792]{1,0:T(8,128)(2,1)S(1)}, u32[]{:S(2)}, u32[]{:S(2)}) collective-permute-start(bf16[24,1792]{1,0:T(8,128)(2,1)S(1)} %get-tuple-element.41), channel_id=1, source_target_pairs={{0,3},{1,2},{2,1},{3,0},{4,7},{5,6},{6,5},{7,4},{8,11},{9,10},{10,... | collective-permute-start | bytes 258056 | tf_op jit(solution)/shard_map/ppermute | solution.py:395
  44.3 2.6 %collective-permute-start.13 = (bf16[24,1792]{1,0:T(8,128)(2,1)S(1)}, bf16[24,1792]{1,0:T(8,128)(2,1)S(1)}, u32[]{:S(2)}, u32[]{:S(2)}) collective-permute-start(bf16[24,1792]{1,0:T(8,128)(2,1)S(1)} %get-tuple-element.42), channel_id=1, source_target_pairs={{0,4},{1,5},{2,6},{3,7},{4,0},{5,1},{6,2},{7,3},{8,12},{9,13},{10,... | collective-permute-start | bytes 258056 | tf_op jit(solution)/shard_map/ppermute | solution.py:395
  46.9 2.4 %collective-permute-start.14 = (bf16[24,1792]{1,0:T(8,128)(2,1)S(1)}, bf16[24,1792]{1,0:T(8,128)(2,1)S(1)}, u32[]{:S(2)}, u32[]{:S(2)}) collective-permute-start(bf16[24,1792]{1,0:T(8,128)(2,1)S(1)} %get-tuple-element.43), channel_id=1, source_target_pairs={{0,5},{1,4},{2,7},{3,6},{4,1},{5,0},{6,3},{7,2},{8,13},{9,12},{10,... | collective-permute-start | bytes 258056 | tf_op jit(solution)/shard_map/ppermute | solution.py:395
  49.2 1.7 %collective-permute-start.15 = (bf16[24,1792]{1,0:T(8,128)(2,1)S(1)}, bf16[24,1792]{1,0:T(8,128)(2,1)S(1)}, u32[]{:S(2)}, u32[]{:S(2)}) collective-permute-start(bf16[24,1792]{1,0:T(8,128)(2,1)S(1)} %get-tuple-element.44), channel_id=1, source_target_pairs={{0,6},{1,7},{2,4},{3,5},{4,2},{5,3},{6,0},{7,1},{8,14},{9,15},{10,... | collective-permute-start | bytes 258056 | tf_op jit(solution)/shard_map/ppermute | solution.py:395
  51.0 5.3 %collective-permute-done.13.refs_4_ = bf16[24,1792]{1,0:T(8,128)(2,1)S(1)} collective-permute-done((bf16[24,1792]{1,0:T(8,128)(2,1)S(1)}, bf16[24,1792]{1,0:T(8,128)(2,1)S(1)}, u32[]{:S(2)}, u32[]{:S(2)}) %collective-permute-start.13) | collective-permute-done | bytes 86048 | tf_op jit(solution)/shard_map/ppermute | solution.py:395
  56.3 2.2 %collective-permute-start.16 = (bf16[24,1792]{1,0:T(8,128)(2,1)S(1)}, bf16[24,1792]{1,0:T(8,128)(2,1)S(1)}, u32[]{:S(2)}, u32[]{:S(2)}) collective-permute-start(bf16[24,1792]{1,0:T(8,128)(2,1)S(1)} %get-tuple-element.45), channel_id=1, source_target_pairs={{0,7},{1,6},{2,5},{3,4},{4,3},{5,2},{6,1},{7,0},{8,15},{9,14},{10,... | collective-permute-start | bytes 258056 | tf_op jit(solution)/shard_map/ppermute | solution.py:395
  58.5 3.4 %collective-permute-start.3 = (bf16[24,1792]{1,0:T(8,128)(2,1)S(1)}, bf16[24,1792]{1,0:T(8,128)(2,1)S(1)}, u32[]{:S(2)}, u32[]{:S(2)}) collective-permute-start(bf16[24,1792]{1,0:T(8,128)(2,1)S(1)} %get-tuple-element.30), channel_id=1, source_target_pairs={{0,4},{1,5},{2,6},{3,7},{4,0},{5,1},{6,2},{7,3},{8,12},{9,13},{10,... | collective-permute-start | bytes 258056 | tf_op jit(solution)/shard_map/ppermute | solution.py:395
  61.9 2.4 %collective-permute-done.16.refs_7_ = bf16[24,1792]{1,0:T(8,128)(2,1)S(1)} collective-permute-done((bf16[24,1792]{1,0:T(8,128)(2,1)S(1)}, bf16[24,1792]{1,0:T(8,128)(2,1)S(1)}, u32[]{:S(2)}, u32[]{:S(2)}) %collective-permute-start.16) | collective-permute-done | bytes 86048 | tf_op jit(solution)/shard_map/ppermute | solution.py:395
  64.2 1.6 %collective-permute-start.5 = (bf16[24,1792]{1,0:T(8,128)(2,1)S(1)}, bf16[24,1792]{1,0:T(8,128)(2,1)S(1)}, u32[]{:S(2)}, u32[]{:S(2)}) collective-permute-start(bf16[24,1792]{1,0:T(8,128)(2,1)S(1)} %get-tuple-element.32), channel_id=1, source_target_pairs={{0,6},{1,7},{2,4},{3,5},{4,2},{5,3},{6,0},{7,1},{8,14},{9,15},{10,... | collective-permute-start | bytes 258056 | tf_op jit(solution)/shard_map/ppermute | solution.py:395
  65.9 1.5 %collective-permute-start.6 = (bf16[24,1792]{1,0:T(8,128)(2,1)S(1)}, bf16[24,1792]{1,0:T(8,128)(2,1)S(1)}, u32[]{:S(2)}, u32[]{:S(2)}) collective-permute-start(bf16[24,1792]{1,0:T(8,128)(2,1)S(1)} %get-tuple-element.33), channel_id=1, source_target_pairs={{0,7},{1,6},{2,5},{3,4},{4,3},{5,2},{6,1},{7,0},{8,15},{9,14},{10,... | collective-permute-start | bytes 258056 | tf_op jit(solution)/shard_map/ppermute | solution.py:395
  67.4 2.8 %prepare.1.rest_0_ = bf16[12,192,146]{2,1,0:T(8,128)(2,1)S(1)} custom-call(bf16[24,1792]{1,0:T(8,128)(2,1)S(1)} %get-tuple-element.38.refs_0_, bf16[24,1792]{1,0:T(8,128)(2,1)S(1)} %collective-permute-done.10.refs_1_, bf16[24,1792]{1,0:T(8,128)(2,1)S(1)} %collective-permute-done.11.refs_2_, bf16[24,1792]{1,0:T(8,128)(2,1)S(1)} %collective-permute-done.12.refs_3_, ...), custom_call_target="tpu_custom_call" | custom-call | tf_op jit(solution)/shard_map/prepare/pallas_call | solution.py:252
  70.2 1.2 %turn.1 = (bf16[3,720,256]{2,1,0:T(8,128)(2,1)S(1)}, bf16[3,720,256]{2,1,0:T(8,128)(2,1)S(1)}, bf16[3,720,256]{2,1,0:T(8,128)(2,1)S(1)}, bf16[3,720,256]{2,1,0:T(8,128)(2,1)S(1)}) custom-call(bf16[3,192,720]{2,1,0:T(8,128)(2,1)S(1)} %bitcast.21, bf16[3,192,720]{2,1,0:T(8,128)(2,1)S(1)} %collective-permute-done.7.refs_1_, ...), custom_call_target="tpu_custom_call" | custom-call | tf_op jit(solution)/shard_map/turn/pallas_call | solution.py:209
  71.5 1.7 %legendre.2.rest_12_ = f32[60,8,128]{2,1,0:T(8,128)S(1)} custom-call(bf16[12,192,146]{2,1,0:T(8,128)(2,1)S(1)} %prepare.1.rest_0_, bf16[3,720,256]{2,1,0:T(8,128)(2,1)S(1)} %get-tuple-element.34.rest_1_.rest_8_, bf16[3,720,256]{2,1,0:T(8,128)(2,1)S(1)} %get-tuple-element.35.rest_2_.rest_9_, bf16[3,720,256]{2,1,0:T(8,128)(2,1)S(1)} %get-tuple-element.36.rest_3_.rest_10_, ...), custom_call_target="tpu_custom_call" | custom-call | tf_op jit(solution)/shard_map/legendre/pallas_call | solution.py:332
  73.2 1.4 %collective-permute-done.4.rest_5_ = bf16[24,1792]{1,0:T(8,128)(2,1)S(1)} collective-permute-done((bf16[24,1792]{1,0:T(8,128)(2,1)S(1)}, bf16[24,1792]{1,0:T(8,128)(2,1)S(1)}, u32[]{:S(2)}, u32[]{:S(2)}) %collective-permute-start.4) | collective-permute-done | bytes 86048 | tf_op jit(solution)/shard_map/ppermute | solution.py:395
  74.6 2.1 %legendre.3 = (f32[60,8,128]{2,1,0:T(8,128)S(1)}, f32[60,8,128]{2,1,0:T(8,128)S(1)}) custom-call(bf16[24,1792]{1,0:T(8,128)(2,1)S(1)} %get-tuple-element.26.rest_0_, bf16[24,1792]{1,0:T(8,128)(2,1)S(1)} %collective-permute-done.rest_1_, bf16[24,1792]{1,0:T(8,128)(2,1)S(1)} %collective-permute-done.1.rest_2_, ...), custom_call_target="tpu_custom_call" | custom-call | tf_op jit(solution)/shard_map/legendre/pallas_call | solution.py:332
  76.8 1.5 %collective-permute-done.17 = f32[60,8,128]{2,1,0:T(8,128)S(1)} collective-permute-done((f32[60,8,128]{2,1,0:T(8,128)S(1)}, f32[60,8,128]{2,1,0:T(8,128)S(1)}, u32[]{:S(2)}, u32[]{:S(2)}) %collective-permute-start.17) | collective-permute-done | bytes 245792 | tf_op jit(solution)/shard_map/ppermute | solution.py:395
  79.2 1.5 %collective-permute-start.19 = (f32[15,8,128]{2,1,0:T(8,128)S(1)}, f32[15,8,128]{2,1,0:T(8,128)S(1)}, u32[]{:S(2)}, u32[]{:S(2)}) collective-permute-start(f32[15,8,128]{2,1,0:T(8,128)S(1)} %get-tuple-element.52), channel_id=1, source_target_pairs={{0,16},{1,17},{2,18},{3,19},{4,20},{5,21},{6,22},{7,23},{8,24},{9,... | collective-permute-start | bytes 184328 | tf_op jit(solution)/shard_map/ppermute | solution.py:416
  83.4 2.4 %collective-permute-done.18 = f32[15,8,128]{2,1,0:T(8,128)S(1)} collective-permute-done((f32[15,8,128]{2,1,0:T(8,128)S(1)}, f32[15,8,128]{2,1,0:T(8,128)S(1)}, u32[]{:S(2)}, u32[]{:S(2)}) %collective-permute-start.18) | collective-permute-done | bytes 61472 | tf_op jit(solution)/shard_map/ppermute | solution.py:416
  85.8 3.3 %collective-permute-start.23 = (f32[15,8,128]{2,1,0:T(8,128)S(1)}, f32[15,8,128]{2,1,0:T(8,128)S(1)}, u32[]{:S(2)}, u32[]{:S(2)}) collective-permute-start(f32[15,8,128]{2,1,0:T(8,128)S(1)} %fusion.1), channel_id=1, source_target_pairs={{0,2},{1,3},{2,0},{3,1},{4,6},{5,7},{6,4},{7,5},{8,10},{9,11},{10,... | collective-permute-start | bytes 184328 | tf_op jit(solution)/shard_map/ppermute | solution.py:395
  89.1 2.0 %collective-permute-start.21 = (f32[15,8,128]{2,1,0:T(8,128)S(1)}, f32[15,8,128]{2,1,0:T(8,128)S(1)}, u32[]{:S(2)}, u32[]{:S(2)}) collective-permute-start(f32[15,8,128]{2,1,0:T(8,128)S(1)} %fusion.1), channel_id=1, source_target_pairs={{0,6},{1,7},{2,4},{3,5},{4,2},{5,3},{6,0},{7,1},{8,14},{9,15},{10,... | collective-permute-start | bytes 184328 | tf_op jit(solution)/shard_map/ppermute | solution.py:395
  91.4 3.9 %collective-permute-done.21 = f32[15,8,128]{2,1,0:T(8,128)S(1)} collective-permute-done((f32[15,8,128]{2,1,0:T(8,128)S(1)}, f32[15,8,128]{2,1,0:T(8,128)S(1)}, u32[]{:S(2)}, u32[]{:S(2)}) %collective-permute-start.21) | collective-permute-done | bytes 61472 | tf_op jit(solution)/shard_map/ppermute | solution.py:395
  95.3 1.4 %collective-permute-done.22 = f32[15,8,128]{2,1,0:T(8,128)S(1)} collective-permute-done((f32[15,8,128]{2,1,0:T(8,128)S(1)}, f32[15,8,128]{2,1,0:T(8,128)S(1)}, u32[]{:S(2)}, u32[]{:S(2)}) %collective-permute-start.22) | collective-permute-done | bytes 61472 | tf_op jit(solution)/shard_map/ppermute | solution.py:395
  98.6 1.6 %collective-permute-start.26 = (f32[15,8,128]{2,1,0:T(8,128)S(1)}, f32[15,8,128]{2,1,0:T(8,128)S(1)}, u32[]{:S(2)}, u32[]{:S(2)}) collective-permute-start(f32[15,8,128]{2,1,0:T(8,128)S(1)} %add_add_fusion.refs_0_), channel_id=1, source_target_pairs={{0,17},{1,16},{2,19},{3,18},{4,21},{5,20},{6,23},{7,22},{8,25},{9,... | collective-permute-start | bytes 184328 | tf_op jit(solution)/shard_map/ppermute | solution.py:416
  102.0 1.7 %collective-permute-done.26.refs_3_ = f32[15,8,128]{2,1,0:T(8,128)S(1)} collective-permute-done((f32[15,8,128]{2,1,0:T(8,128)S(1)}, f32[15,8,128]{2,1,0:T(8,128)S(1)}, u32[]{:S(2)}, u32[]{:S(2)}) %collective-permute-start.26) | collective-permute-done | bytes 61472 | tf_op jit(solution)/shard_map/ppermute | solution.py:416
  103.8 1.2 %collective-permute-done.30.refs_7_ = f32[15,8,128]{2,1,0:T(8,128)S(1)} collective-permute-done((f32[15,8,128]{2,1,0:T(8,128)S(1)}, f32[15,8,128]{2,1,0:T(8,128)S(1)}, u32[]{:S(2)}, u32[]{:S(2)}) %collective-permute-start.30) | collective-permute-done | bytes 61472 | tf_op jit(solution)/shard_map/ppermute | solution.py:395
  (47 shorter events, 11.9 us)
Async XLA Ops:
  0.6 22.9 %collective-permute-start.7 = (bf16[3,192,720]{2,1,0:T(8,128)(2,1)}, bf16[3,192,720]{2,1,0:T(8,128)(2,1)S(1)}, u32[]{:S(2)}, u32[]{:S(2)}) collective-permute-start(bf16[3,192,720]{2,1,0:T(8,128)(2,1)} %bitcast.19), channel_id=1, source_target_pairs={{0,16},{8,24},{16,0},{24,8},{1,17},{9,25},{17,1},{25,9},{2,18},{10... | collective-permute-start | bytes 2488328 | tf_op jit(solution)/shard_map/ppermute | solution.py:395
  3.7 60.6 %collective-permute-start.8 = (bf16[3,192,720]{2,1,0:T(8,128)(2,1)}, bf16[3,192,720]{2,1,0:T(8,128)(2,1)S(1)}, u32[]{:S(2)}, u32[]{:S(2)}) collective-permute-start(bf16[3,192,720]{2,1,0:T(8,128)(2,1)} %bitcast.20), channel_id=1, source_target_pairs={{0,8},{8,0},{16,24},{24,16},{1,9},{9,1},{17,25},{25,17},{2,10},{10... | collective-permute-start | bytes 2488328 | tf_op jit(solution)/shard_map/ppermute | solution.py:395
  23.5 42.3 %collective-permute-start.9 = (bf16[3,192,720]{2,1,0:T(8,128)(2,1)S(1)}, bf16[3,192,720]{2,1,0:T(8,128)(2,1)S(1)}, u32[]{:S(2)}, u32[]{:S(2)}) collective-permute-start(bf16[3,192,720]{2,1,0:T(8,128)(2,1)S(1)} %collective-permute-done.7.refs_1_), channel_id=1, source_target_pairs={{0,8},{8,0},{16,24},{24,16},{1,9},{9,1},{17,25},{25,17},{2,10},{10... | collective-permute-start | bytes 2488328 | tf_op jit(solution)/shard_map/ppermute | solution.py:395
  31.0 9.3 %collective-permute-start = (bf16[24,1792]{1,0:T(8,128)(2,1)S(1)}, bf16[24,1792]{1,0:T(8,128)(2,1)S(1)}, u32[]{:S(2)}, u32[]{:S(2)}) collective-permute-start(bf16[24,1792]{1,0:T(8,128)(2,1)S(1)} %get-tuple-element.27), channel_id=1, source_target_pairs={{0,1},{1,0},{2,3},{3,2},{4,5},{5,4},{6,7},{7,6},{8,9},{9,8},{10,11... | collective-permute-start | bytes 258056 | tf_op jit(solution)/shard_map/ppermute | solution.py:395
  32.8 7.7 %collective-permute-start.1 = (bf16[24,1792]{1,0:T(8,128)(2,1)S(1)}, bf16[24,1792]{1,0:T(8,128)(2,1)S(1)}, u32[]{:S(2)}, u32[]{:S(2)}) collective-permute-start(bf16[24,1792]{1,0:T(8,128)(2,1)S(1)} %get-tuple-element.28), channel_id=1, source_target_pairs={{0,2},{1,3},{2,0},{3,1},{4,6},{5,7},{6,4},{7,5},{8,10},{9,11},{10,... | collective-permute-start | bytes 258056 | tf_op jit(solution)/shard_map/ppermute | solution.py:395
  39.7 30.5 %copy-start.2 = (bf16[192,3,720]{2,0,1:T(8,128)(2,1)S(1)}, bf16[192,3,720]{2,0,1:T(8,128)(2,1)}, u32[]{:S(2)}) copy-start(bf16[192,3,720]{2,0,1:T(8,128)(2,1)} %param.6) | copy-start | bytes 2488324
  39.7 4.6 %collective-permute-start.10 = (bf16[24,1792]{1,0:T(8,128)(2,1)S(1)}, bf16[24,1792]{1,0:T(8,128)(2,1)S(1)}, u32[]{:S(2)}, u32[]{:S(2)}) collective-permute-start(bf16[24,1792]{1,0:T(8,128)(2,1)S(1)} %get-tuple-element.39), channel_id=1, source_target_pairs={{0,1},{1,0},{2,3},{3,2},{4,5},{5,4},{6,7},{7,6},{8,9},{9,8},{10,11... | collective-permute-start | bytes 258056 | tf_op jit(solution)/shard_map/ppermute | solution.py:395
  40.3 6.6 %collective-permute-start.11 = (bf16[24,1792]{1,0:T(8,128)(2,1)S(1)}, bf16[24,1792]{1,0:T(8,128)(2,1)S(1)}, u32[]{:S(2)}, u32[]{:S(2)}) collective-permute-start(bf16[24,1792]{1,0:T(8,128)(2,1)S(1)} %get-tuple-element.40), channel_id=1, source_target_pairs={{0,2},{1,3},{2,0},{3,1},{4,6},{5,7},{6,4},{7,5},{8,10},{9,11},{10,... | collective-permute-start | bytes 258056 | tf_op jit(solution)/shard_map/ppermute | solution.py:395
  40.5 8.7 %collective-permute-start.12 = (bf16[24,1792]{1,0:T(8,128)(2,1)S(1)}, bf16[24,1792]{1,0:T(8,128)(2,1)S(1)}, u32[]{:S(2)}, u32[]{:S(2)}) collective-permute-start(bf16[24,1792]{1,0:T(8,128)(2,1)S(1)} %get-tuple-element.41), channel_id=1, source_target_pairs={{0,3},{1,2},{2,1},{3,0},{4,7},{5,6},{6,5},{7,4},{8,11},{9,10},{10,... | collective-permute-start | bytes 258056 | tf_op jit(solution)/shard_map/ppermute | solution.py:395
  44.3 12.0 %collective-permute-start.13 = (bf16[24,1792]{1,0:T(8,128)(2,1)S(1)}, bf16[24,1792]{1,0:T(8,128)(2,1)S(1)}, u32[]{:S(2)}, u32[]{:S(2)}) collective-permute-start(bf16[24,1792]{1,0:T(8,128)(2,1)S(1)} %get-tuple-element.42), channel_id=1, source_target_pairs={{0,4},{1,5},{2,6},{3,7},{4,0},{5,1},{6,2},{7,3},{8,12},{9,13},{10,... | collective-permute-start | bytes 258056 | tf_op jit(solution)/shard_map/ppermute | solution.py:395
  46.9 11.7 %collective-permute-start.14 = (bf16[24,1792]{1,0:T(8,128)(2,1)S(1)}, bf16[24,1792]{1,0:T(8,128)(2,1)S(1)}, u32[]{:S(2)}, u32[]{:S(2)}) collective-permute-start(bf16[24,1792]{1,0:T(8,128)(2,1)S(1)} %get-tuple-element.43), channel_id=1, source_target_pairs={{0,5},{1,4},{2,7},{3,6},{4,1},{5,0},{6,3},{7,2},{8,13},{9,12},{10,... | collective-permute-start | bytes 258056 | tf_op jit(solution)/shard_map/ppermute | solution.py:395
  49.2 9.3 %collective-permute-start.15 = (bf16[24,1792]{1,0:T(8,128)(2,1)S(1)}, bf16[24,1792]{1,0:T(8,128)(2,1)S(1)}, u32[]{:S(2)}, u32[]{:S(2)}) collective-permute-start(bf16[24,1792]{1,0:T(8,128)(2,1)S(1)} %get-tuple-element.44), channel_id=1, source_target_pairs={{0,6},{1,7},{2,4},{3,5},{4,2},{5,3},{6,0},{7,1},{8,14},{9,15},{10,... | collective-permute-start | bytes 258056 | tf_op jit(solution)/shard_map/ppermute | solution.py:395
  56.3 7.9 %collective-permute-start.16 = (bf16[24,1792]{1,0:T(8,128)(2,1)S(1)}, bf16[24,1792]{1,0:T(8,128)(2,1)S(1)}, u32[]{:S(2)}, u32[]{:S(2)}) collective-permute-start(bf16[24,1792]{1,0:T(8,128)(2,1)S(1)} %get-tuple-element.45), channel_id=1, source_target_pairs={{0,7},{1,6},{2,5},{3,4},{4,3},{5,2},{6,1},{7,0},{8,15},{9,14},{10,... | collective-permute-start | bytes 258056 | tf_op jit(solution)/shard_map/ppermute | solution.py:395
  58.5 14.7 %collective-permute-start.2 = (bf16[24,1792]{1,0:T(8,128)(2,1)S(1)}, bf16[24,1792]{1,0:T(8,128)(2,1)S(1)}, u32[]{:S(2)}, u32[]{:S(2)}) collective-permute-start(bf16[24,1792]{1,0:T(8,128)(2,1)S(1)} %get-tuple-element.29), channel_id=1, source_target_pairs={{0,3},{1,2},{2,1},{3,0},{4,7},{5,6},{6,5},{7,4},{8,11},{9,10},{10,... | collective-permute-start | bytes 258056 | tf_op jit(solution)/shard_map/ppermute | solution.py:395
  58.5 14.7 %collective-permute-start.3 = (bf16[24,1792]{1,0:T(8,128)(2,1)S(1)}, bf16[24,1792]{1,0:T(8,128)(2,1)S(1)}, u32[]{:S(2)}, u32[]{:S(2)}) collective-permute-start(bf16[24,1792]{1,0:T(8,128)(2,1)S(1)} %get-tuple-element.30), channel_id=1, source_target_pairs={{0,4},{1,5},{2,6},{3,7},{4,0},{5,1},{6,2},{7,3},{8,12},{9,13},{10,... | collective-permute-start | bytes 258056 | tf_op jit(solution)/shard_map/ppermute | solution.py:395
  64.2 10.4 %collective-permute-start.4 = (bf16[24,1792]{1,0:T(8,128)(2,1)S(1)}, bf16[24,1792]{1,0:T(8,128)(2,1)S(1)}, u32[]{:S(2)}, u32[]{:S(2)}) collective-permute-start(bf16[24,1792]{1,0:T(8,128)(2,1)S(1)} %get-tuple-element.31), channel_id=1, source_target_pairs={{0,5},{1,4},{2,7},{3,6},{4,1},{5,0},{6,3},{7,2},{8,13},{9,12},{10,... | collective-permute-start | bytes 258056 | tf_op jit(solution)/shard_map/ppermute | solution.py:395
  64.2 10.4 %collective-permute-start.5 = (bf16[24,1792]{1,0:T(8,128)(2,1)S(1)}, bf16[24,1792]{1,0:T(8,128)(2,1)S(1)}, u32[]{:S(2)}, u32[]{:S(2)}) collective-permute-start(bf16[24,1792]{1,0:T(8,128)(2,1)S(1)} %get-tuple-element.32), channel_id=1, source_target_pairs={{0,6},{1,7},{2,4},{3,5},{4,2},{5,3},{6,0},{7,1},{8,14},{9,15},{10,... | collective-permute-start | bytes 258056 | tf_op jit(solution)/shard_map/ppermute | solution.py:395
  65.9 8.8 %collective-permute-start.6 = (bf16[24,1792]{1,0:T(8,128)(2,1)S(1)}, bf16[24,1792]{1,0:T(8,128)(2,1)S(1)}, u32[]{:S(2)}, u32[]{:S(2)}) collective-permute-start(bf16[24,1792]{1,0:T(8,128)(2,1)S(1)} %get-tuple-element.33), channel_id=1, source_target_pairs={{0,7},{1,6},{2,5},{3,4},{4,3},{5,2},{6,1},{7,0},{8,15},{9,14},{10,... | collective-permute-start | bytes 258056 | tf_op jit(solution)/shard_map/ppermute | solution.py:395
  76.7 1.6 %collective-permute-start.17 = (f32[60,8,128]{2,1,0:T(8,128)S(1)}, f32[60,8,128]{2,1,0:T(8,128)S(1)}, u32[]{:S(2)}, u32[]{:S(2)}) collective-permute-start(f32[60,8,128]{2,1,0:T(8,128)S(1)} %get-tuple-element.47), channel_id=1, source_target_pairs={{0,8},{8,0},{16,24},{24,16},{1,9},{9,1},{17,25},{25,17},{2,10},{10... | collective-permute-start | bytes 737288 | tf_op jit(solution)/shard_map/ppermute | solution.py:395
  78.3 4.3 %collective-permute-start.20 = (f32[15,8,128]{2,1,0:T(8,128)S(1)}, f32[15,8,128]{2,1,0:T(8,128)S(1)}, u32[]{:S(2)}, u32[]{:S(2)}) collective-permute-start(f32[15,8,128]{2,1,0:T(8,128)S(1)} %get-tuple-element.51), channel_id=1, source_target_pairs={{0,1},{1,0},{2,3},{3,2},{4,5},{5,4},{6,7},{7,6},{8,9},{9,8},{10,11... | collective-permute-start | bytes 184328 | tf_op jit(solution)/shard_map/ppermute | solution.py:416
  79.2 4.2 %collective-permute-start.19 = (f32[15,8,128]{2,1,0:T(8,128)S(1)}, f32[15,8,128]{2,1,0:T(8,128)S(1)}, u32[]{:S(2)}, u32[]{:S(2)}) collective-permute-start(f32[15,8,128]{2,1,0:T(8,128)S(1)} %get-tuple-element.52), channel_id=1, source_target_pairs={{0,16},{1,17},{2,18},{3,19},{4,20},{5,21},{6,22},{7,23},{8,24},{9,... | collective-permute-start | bytes 184328 | tf_op jit(solution)/shard_map/ppermute | solution.py:416
  80.7 5.1 %collective-permute-start.18 = (f32[15,8,128]{2,1,0:T(8,128)S(1)}, f32[15,8,128]{2,1,0:T(8,128)S(1)}, u32[]{:S(2)}, u32[]{:S(2)}) collective-permute-start(f32[15,8,128]{2,1,0:T(8,128)S(1)} %get-tuple-element.50), channel_id=1, source_target_pairs={{0,17},{1,16},{2,19},{3,18},{4,21},{5,20},{6,23},{7,22},{8,25},{9,... | collective-permute-start | bytes 184328 | tf_op jit(solution)/shard_map/ppermute | solution.py:416
  85.8 5.6 %collective-permute-start.23 = (f32[15,8,128]{2,1,0:T(8,128)S(1)}, f32[15,8,128]{2,1,0:T(8,128)S(1)}, u32[]{:S(2)}, u32[]{:S(2)}) collective-permute-start(f32[15,8,128]{2,1,0:T(8,128)S(1)} %fusion.1), channel_id=1, source_target_pairs={{0,2},{1,3},{2,0},{3,1},{4,6},{5,7},{6,4},{7,5},{8,10},{9,11},{10,... | collective-permute-start | bytes 184328 | tf_op jit(solution)/shard_map/ppermute | solution.py:395
  89.1 6.1 %collective-permute-start.21 = (f32[15,8,128]{2,1,0:T(8,128)S(1)}, f32[15,8,128]{2,1,0:T(8,128)S(1)}, u32[]{:S(2)}, u32[]{:S(2)}) collective-permute-start(f32[15,8,128]{2,1,0:T(8,128)S(1)} %fusion.1), channel_id=1, source_target_pairs={{0,6},{1,7},{2,4},{3,5},{4,2},{5,3},{6,0},{7,1},{8,14},{9,15},{10,... | collective-permute-start | bytes 184328 | tf_op jit(solution)/shard_map/ppermute | solution.py:395
  91.2 5.5 %collective-permute-start.22 = (f32[15,8,128]{2,1,0:T(8,128)S(1)}, f32[15,8,128]{2,1,0:T(8,128)S(1)}, u32[]{:S(2)}, u32[]{:S(2)}) collective-permute-start(f32[15,8,128]{2,1,0:T(8,128)S(1)} %fusion.1), channel_id=1, source_target_pairs={{0,4},{1,5},{2,6},{3,7},{4,0},{5,1},{6,2},{7,3},{8,12},{9,13},{10,... | collective-permute-start | bytes 184328 | tf_op jit(solution)/shard_map/ppermute | solution.py:395
  96.6 4.3 %collective-permute-start.24 = (f32[15,8,128]{2,1,0:T(8,128)S(1)}, f32[15,8,128]{2,1,0:T(8,128)S(1)}, u32[]{:S(2)}, u32[]{:S(2)}) collective-permute-start(f32[15,8,128]{2,1,0:T(8,128)S(1)} %add_add_fusion.refs_0_), channel_id=1, source_target_pairs={{0,1},{1,0},{2,3},{3,2},{4,5},{5,4},{6,7},{7,6},{8,9},{9,8},{10,11... | collective-permute-start | bytes 184328 | tf_op jit(solution)/shard_map/ppermute | solution.py:416
  97.8 4.2 %collective-permute-start.25 = (f32[15,8,128]{2,1,0:T(8,128)S(1)}, f32[15,8,128]{2,1,0:T(8,128)S(1)}, u32[]{:S(2)}, u32[]{:S(2)}) collective-permute-start(f32[15,8,128]{2,1,0:T(8,128)S(1)} %add_add_fusion.refs_0_), channel_id=1, source_target_pairs={{0,16},{1,17},{2,18},{3,19},{4,20},{5,21},{6,22},{7,23},{8,24},{9,... | collective-permute-start | bytes 184328 | tf_op jit(solution)/shard_map/ppermute | solution.py:416
  98.6 5.1 %collective-permute-start.26 = (f32[15,8,128]{2,1,0:T(8,128)S(1)}, f32[15,8,128]{2,1,0:T(8,128)S(1)}, u32[]{:S(2)}, u32[]{:S(2)}) collective-permute-start(f32[15,8,128]{2,1,0:T(8,128)S(1)} %add_add_fusion.refs_0_), channel_id=1, source_target_pairs={{0,17},{1,16},{2,19},{3,18},{4,21},{5,20},{6,23},{7,22},{8,25},{9,... | collective-permute-start | bytes 184328 | tf_op jit(solution)/shard_map/ppermute | solution.py:416
  100.2 3.6 %collective-permute-start.27 = (f32[15,8,128]{2,1,0:T(8,128)S(1)}, f32[15,8,128]{2,1,0:T(8,128)S(1)}, u32[]{:S(2)}, u32[]{:S(2)}) collective-permute-start(f32[15,8,128]{2,1,0:T(8,128)S(1)} %add_add_fusion.refs_0_), channel_id=1, source_target_pairs={{0,8},{8,0},{16,24},{24,16},{1,9},{9,1},{17,25},{25,17},{2,10},{10... | collective-permute-start | bytes 184328 | tf_op jit(solution)/shard_map/ppermute | solution.py:395
  100.9 2.8 %collective-permute-start.28 = (f32[15,8,128]{2,1,0:T(8,128)S(1)}, f32[15,8,128]{2,1,0:T(8,128)S(1)}, u32[]{:S(2)}, u32[]{:S(2)}) collective-permute-start(f32[15,8,128]{2,1,0:T(8,128)S(1)} %collective-permute-done.24.refs_1_), channel_id=1, source_target_pairs={{0,8},{8,0},{16,24},{24,16},{1,9},{9,1},{17,25},{25,17},{2,10},{10... | collective-permute-start | bytes 184328 | tf_op jit(solution)/shard_map/ppermute | solution.py:395
  102.0 1.7 %collective-permute-start.29 = (f32[15,8,128]{2,1,0:T(8,128)S(1)}, f32[15,8,128]{2,1,0:T(8,128)S(1)}, u32[]{:S(2)}, u32[]{:S(2)}) collective-permute-start(f32[15,8,128]{2,1,0:T(8,128)S(1)} %collective-permute-done.25.refs_2_), channel_id=1, source_target_pairs={{0,8},{8,0},{16,24},{24,16},{1,9},{9,1},{17,25},{25,17},{2,10},{10... | collective-permute-start | bytes 184328 | tf_op jit(solution)/shard_map/ppermute | solution.py:395
  103.7 1.2 %collective-permute-start.30 = (f32[15,8,128]{2,1,0:T(8,128)S(1)}, f32[15,8,128]{2,1,0:T(8,128)S(1)}, u32[]{:S(2)}, u32[]{:S(2)}) collective-permute-start(f32[15,8,128]{2,1,0:T(8,128)S(1)} %collective-permute-done.26.refs_3_), channel_id=1, source_target_pairs={{0,8},{8,0},{16,24},{24,16},{1,9},{9,1},{17,25},{25,17},{2,10},{10... | collective-permute-start | bytes 184328 | tf_op jit(solution)/shard_map/ppermute | solution.py:395
  (2 other events, 3.6 us)

commit v6 on v5

--- a/solution.py
+++ b/solution.py
@@ -140,7 +140,7 @@
     rows_all, lon_count = field.shape
     width = round_up(rows_all, LANES)
     columns = table.shape[1]
-    step = 4 * LANES
+    step = 5 * LANES
     chunks = [min(step, rows_all - row) for row in range(0, rows_all, step)]
     anywhere = pl.BlockSpec(memory_space=pl.ANY)
     vmem = pl.BlockSpec(memory_space=pltpu.VMEM)
@@ -260,6 +260,15 @@
         compiler_params=pltpu.CompilerParams(vmem_limit_bytes=SPARE_VMEM + held),
         name="prepare",
     )(*blocks)
+
+
+def energy_tiles(chans, degrees):
+    lane_tiles = round_up(degrees, LANES) // LANES
+    row_tiles, tail = chans // 8, chans % 8
+    if tail * lane_tiles > 8:
+        row_tiles, tail = row_tiles + 1, 0
+    count = row_tiles * lane_tiles + (1 if tail else 0)
+    return lane_tiles, row_tiles, tail, round_up(count, 4)
 
 
 def legendre_kernel(bands, groups, per_dev, chans, lats, slots, field, *rest):
@@ -303,12 +312,16 @@
     flat = jnp.pad(
         energy, ((0, round_up(degrees, LANES) - degrees), (0, round_up(chans, 8) - chans))
     )
-    lane_tiles = round_up(degrees, LANES) // LANES
-    row_tiles = round_up(chans, 8) // 8
+    lane_tiles, row_tiles, tail, count = energy_tiles(chans, degrees)
+    end = row_tiles * lane_tiles
+    for b in range(end, count):
+        out[b] = jnp.zeros((8, LANES), jnp.float32)
     for k in range(lane_tiles):
         piece = flat[k * LANES : (k + 1) * LANES, :].T
         for r in range(row_tiles):
             out[r * lane_tiles + k] = piece[r * 8 : (r + 1) * 8, :]
+        if tail:
+            out[end, pl.ds(k * tail, tail), :] = piece[row_tiles * 8 : row_tiles * 8 + tail, :]
     if field == 1:
         high = lax.rem(group, 2) == 1
         first, second = energy_before[...], out[...]
@@ -319,9 +332,7 @@
 def legendre_energy(blocks, bases, slots, chans, lats, bands, before):
     groups = len(bases)
     per_dev, degrees, _ = bases[0].shape
-    row_tiles = round_up(chans, 8) // 8
-    lane_tiles = round_up(degrees, LANES) // LANES
-    tiles = (row_tiles * lane_tiles, 8, LANES)
+    tiles = (energy_tiles(chans, degrees)[3], 8, LANES)
     field = len(before)
     out = jax.ShapeDtypeStruct(tiles, jnp.float32)
     staging = [
@@ -343,8 +354,7 @@
     parts = (len(refs) - 4) // 2
     owned, other = refs[:parts], refs[parts : 2 * parts]
     spectra, loss, sums, fields = refs[2 * parts :]
-    lane_tiles = round_up(degrees, LANES) // LANES
-    row_tiles = round_up(chans, 8) // 8
+    lane_tiles, row_tiles, tail, _ = energy_tiles(chans, degrees)
     scale = 1.0 / count
     mine = quarter_id(mesh_size)
     high = lax.rem(lax.axis_index("batch"), 2)
@@ -353,13 +363,17 @@
         start = jnp.bitwise_xor(mine, m) * size
         fields[high, pl.ds(start, size)] = owned[m][...] * scale
         fields[1 - high, pl.ds(start, size)] = other[m][...] * scale
-    for r in range(row_tiles):
+    for r in range(row_tiles + (1 if tail else 0)):
         rows = min(8, chans - r * 8)
-        acc = jnp.zeros((8, LANES), jnp.float32)
+        held = 8 if r < row_tiles else tail
+        acc = jnp.zeros((held, LANES), jnp.float32)
         for k in range(lane_tiles):
             lanes = min(LANES, degrees - k * LANES)
-            first = fields[0, r * lane_tiles + k]
-            second = fields[1, r * lane_tiles + k]
+            block, line = r * lane_tiles + k, 0
+            if r == row_tiles:
+                block, line = r * lane_tiles, k * tail
+            first = fields[0, block, pl.ds(line, held), :]
+            second = fields[1, block, pl.ds(line, held), :]
             spectra[pl.ds(r * 8, rows), 0, pl.ds(k * LANES, lanes)] = first[:rows, :lanes]
             spectra[pl.ds(r * 8, rows), 1, pl.ds(k * LANES, lanes)] = second[:rows, :lanes]
             gap = jnp.log(first + 1e-06) - jnp.log(second + 1e-06)
@@ -368,7 +382,7 @@
                 lane_ids = lax.broadcasted_iota(jnp.int32, gap.shape, 1)
                 gap = jnp.where(lane_ids < lanes, gap, 0.0)
             acc = acc + gap
-        sums[pl.ds(r * 8, 8), :] = acc
+        sums[pl.ds(r * 8, held), :] = acc
     turned = sums[...].T
     loss[...] = (jnp.sum(turned, axis=0, keepdims=True) * (1.0 / degrees))[:, :chans]
 

time: 106 us -> 106 us (level)
  no operation moved by 1% of the time
where the time goes in v6:
time: 106 us; the launch traced here: 105 us
  waiting for transfers between devices  45.1 us (43%)
  starting transfers between devices  38 us (36%)
  Pallas kernels  17.9 us (17%)
  local copies, waits for them, and re-layouts  3.67 us (3%)
    ppermute x25, waiting for transfers between devices, exchange(): return lax.ppermute(value, axis, peers(lax.axis_size(axis), step))  37.8 us
    ppermute x25, starting transfers between devices, exchange(): return lax.ppermute(value, axis, peers(lax.axis_size(axis), step))  30.8 us
    ppermute x6, waiting for transfers between devices, flat_exchange(): lax.ppermute(value, ('batch', 'lat'), [(i, i ^ step) for i in range(count)])  7.29 us
    ppermute x6, starting transfers between devices, flat_exchange(): lax.ppermute(value, ('batch', 'lat'), [(i, i ^ step) for i in range(count)])  7.1 us
    pallas_call x1, Pallas kernels, row_blocks(): pl.pallas_call(functools.partial(rows_kernel, bands, per, tuple(chunks)),...  5.07 us
    pallas_call x1, Pallas kernels, dft_blocks(): pl.pallas_call(functools.partial(dft_kernel, bands, per, chans, lats, tup...  3.79 us
    pallas_call x2, Pallas kernels, legendre_energy(): pl.pallas_call(functools.partial(legendre_kernel, bands, groups, per_dev,...  3.76 us
    unnamed x6, local copies, waits for them, and re-layouts  3.65 us
  transfers between devices with their start and end apart: 31, of which 16 were waited for; matrix products, arithmetic and copies ran while one was open for 0% of the time, Pallas kernels for 14%

profile of v6, /device:TPU:0, one launch (start us, length us, event | category | flops | bytes accessed | tf_op | source)
XLA Modules:
  0.0 105.4 jit_solution(2048461517297081017)
XLA Ops:
  0.6 3.0 %collective-permute-start.7 = (bf16[3,192,720]{2,1,0:T(8,128)(2,1)}, bf16[3,192,720]{2,1,0:T(8,128)(2,1)S(1)}, u32[]{:S(2)}, u32[]{:S(2)}) collective-permute-start(bf16[3,192,720]{2,1,0:T(8,128)(2,1)} %bitcast.19), channel_id=1, source_target_pairs={{0,16},{8,24},{16,0},{24,8},{1,17},{9,25},{17,1},{25,9},{2,18},{10... | collective-permute-start | bytes 2488328 | tf_op jit(solution)/shard_map/ppermute | solution.py:409
  3.7 19.9 %collective-permute-done.7.refs_1_ = bf16[3,192,720]{2,1,0:T(8,128)(2,1)S(1)} collective-permute-done((bf16[3,192,720]{2,1,0:T(8,128)(2,1)}, bf16[3,192,720]{2,1,0:T(8,128)(2,1)S(1)}, u32[]{:S(2)}, u32[]{:S(2)}) %collective-permute-start.7) | collective-permute-done | bytes 829472 | tf_op jit(solution)/shard_map/ppermute | solution.py:409
  23.5 2.5 %copy-done = bf16[1,73,24,1440]{3,2,1,0:T(8,128)(2,1)S(1)} copy-done((bf16[1,73,24,1440]{3,2,1,0:T(8,128)(2,1)S(1)}, bf16[1,73,24,1440]{3,2,1,0:T(8,128)(2,1)}, u32[]{:S(2)}) %copy-start) | copy-done | bytes 5045784
  27.2 3.8 %dft.1 = (bf16[24,1792]{1,0:T(8,128)(2,1)S(1)}, bf16[24,1792]{1,0:T(8,128)(2,1)S(1)}, bf16[24,1792]{1,0:T(8,128)(2,1)S(1)}, bf16[24,1792]{1,0:T(8,128)(2,1)S(1)}...) custom-call(bf16[1752,1440]{1,0:T(8,128)(2,1)S(1)} %bitcast.18, ...), custom_call_target="tpu_custom_call" | custom-call | tf_op jit(solution)/shard_map/dft/pallas_call | solution.py:182
  31.0 1.8 %collective-permute-start = (bf16[24,1792]{1,0:T(8,128)(2,1)S(1)}, bf16[24,1792]{1,0:T(8,128)(2,1)S(1)}, u32[]{:S(2)}, u32[]{:S(2)}) collective-permute-start(bf16[24,1792]{1,0:T(8,128)(2,1)S(1)} %get-tuple-element.27), channel_id=1, source_target_pairs={{0,1},{1,0},{2,3},{3,2},{4,5},{5,4},{6,7},{7,6},{8,9},{9,8},{10,11... | collective-permute-start | bytes 258056 | tf_op jit(solution)/shard_map/ppermute | solution.py:409
  32.8 1.6 %collective-permute-start.1 = (bf16[24,1792]{1,0:T(8,128)(2,1)S(1)}, bf16[24,1792]{1,0:T(8,128)(2,1)S(1)}, u32[]{:S(2)}, u32[]{:S(2)}) collective-permute-start(bf16[24,1792]{1,0:T(8,128)(2,1)S(1)} %get-tuple-element.28), channel_id=1, source_target_pairs={{0,2},{1,3},{2,0},{3,1},{4,6},{5,7},{6,4},{7,5},{8,10},{9,11},{10,... | collective-permute-start | bytes 258056 | tf_op jit(solution)/shard_map/ppermute | solution.py:409
  34.4 5.1 %dft_rows.1 = (bf16[24,1792]{1,0:T(8,128)(2,1)S(1)}, bf16[24,1792]{1,0:T(8,128)(2,1)S(1)}, bf16[24,1792]{1,0:T(8,128)(2,1)S(1)}, bf16[24,1792]{1,0:T(8,128)(2,1)...) custom-call(bf16[1752,1440]{1,0:T(8,128)(2,1)} %bitcast.22, ...), custom_call_target="tpu_custom_call" | custom-call | tf_op jit(solution)/shard_map/dft_rows/pallas_call | solution.py:147
  40.2 2.8 %collective-permute-start.12 = (bf16[24,1792]{1,0:T(8,128)(2,1)S(1)}, bf16[24,1792]{1,0:T(8,128)(2,1)S(1)}, u32[]{:S(2)}, u32[]{:S(2)}) collective-permute-start(bf16[24,1792]{1,0:T(8,128)(2,1)S(1)} %get-tuple-element.41), channel_id=1, source_target_pairs={{0,3},{1,2},{2,1},{3,0},{4,7},{5,6},{6,5},{7,4},{8,11},{9,10},{10,... | collective-permute-start | bytes 258056 | tf_op jit(solution)/shard_map/ppermute | solution.py:409
  44.0 2.6 %collective-permute-start.13 = (bf16[24,1792]{1,0:T(8,128)(2,1)S(1)}, bf16[24,1792]{1,0:T(8,128)(2,1)S(1)}, u32[]{:S(2)}, u32[]{:S(2)}) collective-permute-start(bf16[24,1792]{1,0:T(8,128)(2,1)S(1)} %get-tuple-element.42), channel_id=1, source_target_pairs={{0,4},{1,5},{2,6},{3,7},{4,0},{5,1},{6,2},{7,3},{8,12},{9,13},{10,... | collective-permute-start | bytes 258056 | tf_op jit(solution)/shard_map/ppermute | solution.py:409
  46.6 2.4 %collective-permute-start.14 = (bf16[24,1792]{1,0:T(8,128)(2,1)S(1)}, bf16[24,1792]{1,0:T(8,128)(2,1)S(1)}, u32[]{:S(2)}, u32[]{:S(2)}) collective-permute-start(bf16[24,1792]{1,0:T(8,128)(2,1)S(1)} %get-tuple-element.43), channel_id=1, source_target_pairs={{0,5},{1,4},{2,7},{3,6},{4,1},{5,0},{6,3},{7,2},{8,13},{9,12},{10,... | collective-permute-start | bytes 258056 | tf_op jit(solution)/shard_map/ppermute | solution.py:409
  49.0 1.7 %collective-permute-start.15 = (bf16[24,1792]{1,0:T(8,128)(2,1)S(1)}, bf16[24,1792]{1,0:T(8,128)(2,1)S(1)}, u32[]{:S(2)}, u32[]{:S(2)}) collective-permute-start(bf16[24,1792]{1,0:T(8,128)(2,1)S(1)} %get-tuple-element.44), channel_id=1, source_target_pairs={{0,6},{1,7},{2,4},{3,5},{4,2},{5,3},{6,0},{7,1},{8,14},{9,15},{10,... | collective-permute-start | bytes 258056 | tf_op jit(solution)/shard_map/ppermute | solution.py:409
  50.7 5.3 %collective-permute-done.13.refs_4_ = bf16[24,1792]{1,0:T(8,128)(2,1)S(1)} collective-permute-done((bf16[24,1792]{1,0:T(8,128)(2,1)S(1)}, bf16[24,1792]{1,0:T(8,128)(2,1)S(1)}, u32[]{:S(2)}, u32[]{:S(2)}) %collective-permute-start.13) | collective-permute-done | bytes 86048 | tf_op jit(solution)/shard_map/ppermute | solution.py:409
  56.0 2.2 %collective-permute-start.16 = (bf16[24,1792]{1,0:T(8,128)(2,1)S(1)}, bf16[24,1792]{1,0:T(8,128)(2,1)S(1)}, u32[]{:S(2)}, u32[]{:S(2)}) collective-permute-start(bf16[24,1792]{1,0:T(8,128)(2,1)S(1)} %get-tuple-element.45), channel_id=1, source_target_pairs={{0,7},{1,6},{2,5},{3,4},{4,3},{5,2},{6,1},{7,0},{8,15},{9,14},{10,... | collective-permute-start | bytes 258056 | tf_op jit(solution)/shard_map/ppermute | solution.py:409
  58.3 3.4 %collective-permute-start.3 = (bf16[24,1792]{1,0:T(8,128)(2,1)S(1)}, bf16[24,1792]{1,0:T(8,128)(2,1)S(1)}, u32[]{:S(2)}, u32[]{:S(2)}) collective-permute-start(bf16[24,1792]{1,0:T(8,128)(2,1)S(1)} %get-tuple-element.30), channel_id=1, source_target_pairs={{0,4},{1,5},{2,6},{3,7},{4,0},{5,1},{6,2},{7,3},{8,12},{9,13},{10,... | collective-permute-start | bytes 258056 | tf_op jit(solution)/shard_map/ppermute | solution.py:409
  61.6 2.4 %collective-permute-done.16.refs_7_ = bf16[24,1792]{1,0:T(8,128)(2,1)S(1)} collective-permute-done((bf16[24,1792]{1,0:T(8,128)(2,1)S(1)}, bf16[24,1792]{1,0:T(8,128)(2,1)S(1)}, u32[]{:S(2)}, u32[]{:S(2)}) %collective-permute-start.16) | collective-permute-done | bytes 86048 | tf_op jit(solution)/shard_map/ppermute | solution.py:409
  64.0 1.6 %collective-permute-start.5 = (bf16[24,1792]{1,0:T(8,128)(2,1)S(1)}, bf16[24,1792]{1,0:T(8,128)(2,1)S(1)}, u32[]{:S(2)}, u32[]{:S(2)}) collective-permute-start(bf16[24,1792]{1,0:T(8,128)(2,1)S(1)} %get-tuple-element.32), channel_id=1, source_target_pairs={{0,6},{1,7},{2,4},{3,5},{4,2},{5,3},{6,0},{7,1},{8,14},{9,15},{10,... | collective-permute-start | bytes 258056 | tf_op jit(solution)/shard_map/ppermute | solution.py:409
  65.6 1.5 %collective-permute-start.6 = (bf16[24,1792]{1,0:T(8,128)(2,1)S(1)}, bf16[24,1792]{1,0:T(8,128)(2,1)S(1)}, u32[]{:S(2)}, u32[]{:S(2)}) collective-permute-start(bf16[24,1792]{1,0:T(8,128)(2,1)S(1)} %get-tuple-element.33), channel_id=1, source_target_pairs={{0,7},{1,6},{2,5},{3,4},{4,3},{5,2},{6,1},{7,0},{8,15},{9,14},{10,... | collective-permute-start | bytes 258056 | tf_op jit(solution)/shard_map/ppermute | solution.py:409
  67.2 2.8 %prepare.1.rest_0_ = bf16[12,192,146]{2,1,0:T(8,128)(2,1)S(1)} custom-call(bf16[24,1792]{1,0:T(8,128)(2,1)S(1)} %get-tuple-element.38.refs_0_, bf16[24,1792]{1,0:T(8,128)(2,1)S(1)} %collective-permute-done.10.refs_1_, bf16[24,1792]{1,0:T(8,128)(2,1)S(1)} %collective-permute-done.11.refs_2_, bf16[24,1792]{1,0:T(8,128)(2,1)S(1)} %collective-permute-done.12.refs_3_, ...), custom_call_target="tpu_custom_call" | custom-call | tf_op jit(solution)/shard_map/prepare/pallas_call | solution.py:252
  70.0 1.2 %turn.1 = (bf16[3,720,256]{2,1,0:T(8,128)(2,1)S(1)}, bf16[3,720,256]{2,1,0:T(8,128)(2,1)S(1)}, bf16[3,720,256]{2,1,0:T(8,128)(2,1)S(1)}, bf16[3,720,256]{2,1,0:T(8,128)(2,1)S(1)}) custom-call(bf16[3,192,720]{2,1,0:T(8,128)(2,1)S(1)} %bitcast.21, bf16[3,192,720]{2,1,0:T(8,128)(2,1)S(1)} %collective-permute-done.7.refs_1_, ...), custom_call_target="tpu_custom_call" | custom-call | tf_op jit(solution)/shard_map/turn/pallas_call | solution.py:209
  71.3 1.7 %legendre.2.rest_12_ = f32[56,8,128]{2,1,0:T(8,128)S(1)} custom-call(bf16[12,192,146]{2,1,0:T(8,128)(2,1)S(1)} %prepare.1.rest_0_, bf16[3,720,256]{2,1,0:T(8,128)(2,1)S(1)} %get-tuple-element.34.rest_1_.rest_8_, bf16[3,720,256]{2,1,0:T(8,128)(2,1)S(1)} %get-tuple-element.35.rest_2_.rest_9_, bf16[3,720,256]{2,1,0:T(8,128)(2,1)S(1)} %get-tuple-element.36.rest_3_.rest_10_, ...), custom_call_target="tpu_custom_call" | custom-call | tf_op jit(solution)/shard_map/legendre/pallas_call | solution.py:343
  73.0 1.4 %collective-permute-done.4.rest_5_ = bf16[24,1792]{1,0:T(8,128)(2,1)S(1)} collective-permute-done((bf16[24,1792]{1,0:T(8,128)(2,1)S(1)}, bf16[24,1792]{1,0:T(8,128)(2,1)S(1)}, u32[]{:S(2)}, u32[]{:S(2)}) %collective-permute-start.4) | collective-permute-done | bytes 86048 | tf_op jit(solution)/shard_map/ppermute | solution.py:409
  74.4 2.1 %legendre.3 = (f32[56,8,128]{2,1,0:T(8,128)S(1)}, f32[56,8,128]{2,1,0:T(8,128)S(1)}) custom-call(bf16[24,1792]{1,0:T(8,128)(2,1)S(1)} %get-tuple-element.26.rest_0_, bf16[24,1792]{1,0:T(8,128)(2,1)S(1)} %collective-permute-done.rest_1_, bf16[24,1792]{1,0:T(8,128)(2,1)S(1)} %collective-permute-done.1.rest_2_, ...), custom_call_target="tpu_custom_call" | custom-call | tf_op jit(solution)/shard_map/legendre/pallas_call | solution.py:343
  76.6 1.4 %collective-permute-done.17 = f32[56,8,128]{2,1,0:T(8,128)S(1)} collective-permute-done((f32[56,8,128]{2,1,0:T(8,128)S(1)}, f32[56,8,128]{2,1,0:T(8,128)S(1)}, u32[]{:S(2)}, u32[]{:S(2)}) %collective-permute-start.17) | collective-permute-done | bytes 229408 | tf_op jit(solution)/shard_map/ppermute | solution.py:409
  78.9 1.5 %collective-permute-start.19 = (f32[14,8,128]{2,1,0:T(8,128)S(1)}, f32[14,8,128]{2,1,0:T(8,128)S(1)}, u32[]{:S(2)}, u32[]{:S(2)}) collective-permute-start(f32[14,8,128]{2,1,0:T(8,128)S(1)} %get-tuple-element.52), channel_id=1, source_target_pairs={{0,16},{1,17},{2,18},{3,19},{4,20},{5,21},{6,22},{7,23},{8,24},{9,... | collective-permute-start | bytes 172040 | tf_op jit(solution)/shard_map/ppermute | solution.py:430
  83.1 2.4 %collective-permute-done.18 = f32[14,8,128]{2,1,0:T(8,128)S(1)} collective-permute-done((f32[14,8,128]{2,1,0:T(8,128)S(1)}, f32[14,8,128]{2,1,0:T(8,128)S(1)}, u32[]{:S(2)}, u32[]{:S(2)}) %collective-permute-start.18) | collective-permute-done | bytes 57376 | tf_op jit(solution)/shard_map/ppermute | solution.py:430
  85.5 3.3 %collective-permute-start.23 = (f32[14,8,128]{2,1,0:T(8,128)S(1)}, f32[14,8,128]{2,1,0:T(8,128)S(1)}, u32[]{:S(2)}, u32[]{:S(2)}) collective-permute-start(f32[14,8,128]{2,1,0:T(8,128)S(1)} %fusion.1), channel_id=1, source_target_pairs={{0,2},{1,3},{2,0},{3,1},{4,6},{5,7},{6,4},{7,5},{8,10},{9,11},{10,... | collective-permute-start | bytes 172040 | tf_op jit(solution)/shard_map/ppermute | solution.py:409
  88.8 2.0 %collective-permute-start.21 = (f32[14,8,128]{2,1,0:T(8,128)S(1)}, f32[14,8,128]{2,1,0:T(8,128)S(1)}, u32[]{:S(2)}, u32[]{:S(2)}) collective-permute-start(f32[14,8,128]{2,1,0:T(8,128)S(1)} %fusion.1), channel_id=1, source_target_pairs={{0,6},{1,7},{2,4},{3,5},{4,2},{5,3},{6,0},{7,1},{8,14},{9,15},{10,... | collective-permute-start | bytes 172040 | tf_op jit(solution)/shard_map/ppermute | solution.py:409
  91.0 3.8 %collective-permute-done.21 = f32[14,8,128]{2,1,0:T(8,128)S(1)} collective-permute-done((f32[14,8,128]{2,1,0:T(8,128)S(1)}, f32[14,8,128]{2,1,0:T(8,128)S(1)}, u32[]{:S(2)}, u32[]{:S(2)}) %collective-permute-start.21) | collective-permute-done | bytes 57376 | tf_op jit(solution)/shard_map/ppermute | solution.py:409
  94.8 1.2 %collective-permute-done.22 = f32[14,8,128]{2,1,0:T(8,128)S(1)} collective-permute-done((f32[14,8,128]{2,1,0:T(8,128)S(1)}, f32[14,8,128]{2,1,0:T(8,128)S(1)}, u32[]{:S(2)}, u32[]{:S(2)}) %collective-permute-start.22) | collective-permute-done | bytes 57376 | tf_op jit(solution)/shard_map/ppermute | solution.py:409
  96.0 1.3 %collective-permute-start.24 = (f32[14,8,128]{2,1,0:T(8,128)S(1)}, f32[14,8,128]{2,1,0:T(8,128)S(1)}, u32[]{:S(2)}, u32[]{:S(2)}) collective-permute-start(f32[14,8,128]{2,1,0:T(8,128)S(1)} %add_add_fusion.refs_0_), channel_id=1, source_target_pairs={{0,1},{1,0},{2,3},{3,2},{4,5},{5,4},{6,7},{7,6},{8,9},{9,8},{10,11... | collective-permute-start | bytes 172040 | tf_op jit(solution)/shard_map/ppermute | solution.py:430
  97.9 1.7 %collective-permute-start.26 = (f32[14,8,128]{2,1,0:T(8,128)S(1)}, f32[14,8,128]{2,1,0:T(8,128)S(1)}, u32[]{:S(2)}, u32[]{:S(2)}) collective-permute-start(f32[14,8,128]{2,1,0:T(8,128)S(1)} %add_add_fusion.refs_0_), channel_id=1, source_target_pairs={{0,17},{1,16},{2,19},{3,18},{4,21},{5,20},{6,23},{7,22},{8,25},{9,... | collective-permute-start | bytes 172040 | tf_op jit(solution)/shard_map/ppermute | solution.py:430
  101.5 1.5 %collective-permute-done.26.refs_3_ = f32[14,8,128]{2,1,0:T(8,128)S(1)} collective-permute-done((f32[14,8,128]{2,1,0:T(8,128)S(1)}, f32[14,8,128]{2,1,0:T(8,128)S(1)}, u32[]{:S(2)}, u32[]{:S(2)}) %collective-permute-start.26) | collective-permute-done | bytes 57376 | tf_op jit(solution)/shard_map/ppermute | solution.py:430
  (47 shorter events, 11.6 us)
Async XLA Ops:
  0.6 22.9 %collective-permute-start.7 = (bf16[3,192,720]{2,1,0:T(8,128)(2,1)}, bf16[3,192,720]{2,1,0:T(8,128)(2,1)S(1)}, u32[]{:S(2)}, u32[]{:S(2)}) collective-permute-start(bf16[3,192,720]{2,1,0:T(8,128)(2,1)} %bitcast.19), channel_id=1, source_target_pairs={{0,16},{8,24},{16,0},{24,8},{1,17},{9,25},{17,1},{25,9},{2,18},{10... | collective-permute-start | bytes 2488328 | tf_op jit(solution)/shard_map/ppermute | solution.py:409
  3.7 60.3 %collective-permute-start.8 = (bf16[3,192,720]{2,1,0:T(8,128)(2,1)}, bf16[3,192,720]{2,1,0:T(8,128)(2,1)S(1)}, u32[]{:S(2)}, u32[]{:S(2)}) collective-permute-start(bf16[3,192,720]{2,1,0:T(8,128)(2,1)} %bitcast.20), channel_id=1, source_target_pairs={{0,8},{8,0},{16,24},{24,16},{1,9},{9,1},{17,25},{25,17},{2,10},{10... | collective-permute-start | bytes 2488328 | tf_op jit(solution)/shard_map/ppermute | solution.py:409
  23.5 42.1 %collective-permute-start.9 = (bf16[3,192,720]{2,1,0:T(8,128)(2,1)S(1)}, bf16[3,192,720]{2,1,0:T(8,128)(2,1)S(1)}, u32[]{:S(2)}, u32[]{:S(2)}) collective-permute-start(bf16[3,192,720]{2,1,0:T(8,128)(2,1)S(1)} %collective-permute-done.7.refs_1_), channel_id=1, source_target_pairs={{0,8},{8,0},{16,24},{24,16},{1,9},{9,1},{17,25},{25,17},{2,10},{10... | collective-permute-start | bytes 2488328 | tf_op jit(solution)/shard_map/ppermute | solution.py:409
  31.0 9.1 %collective-permute-start = (bf16[24,1792]{1,0:T(8,128)(2,1)S(1)}, bf16[24,1792]{1,0:T(8,128)(2,1)S(1)}, u32[]{:S(2)}, u32[]{:S(2)}) collective-permute-start(bf16[24,1792]{1,0:T(8,128)(2,1)S(1)} %get-tuple-element.27), channel_id=1, source_target_pairs={{0,1},{1,0},{2,3},{3,2},{4,5},{5,4},{6,7},{7,6},{8,9},{9,8},{10,11... | collective-permute-start | bytes 258056 | tf_op jit(solution)/shard_map/ppermute | solution.py:409
  32.8 7.4 %collective-permute-start.1 = (bf16[24,1792]{1,0:T(8,128)(2,1)S(1)}, bf16[24,1792]{1,0:T(8,128)(2,1)S(1)}, u32[]{:S(2)}, u32[]{:S(2)}) collective-permute-start(bf16[24,1792]{1,0:T(8,128)(2,1)S(1)} %get-tuple-element.28), channel_id=1, source_target_pairs={{0,2},{1,3},{2,0},{3,1},{4,6},{5,7},{6,4},{7,5},{8,10},{9,11},{10,... | collective-permute-start | bytes 258056 | tf_op jit(solution)/shard_map/ppermute | solution.py:409
  39.4 30.6 %copy-start.2 = (bf16[192,3,720]{2,0,1:T(8,128)(2,1)S(1)}, bf16[192,3,720]{2,0,1:T(8,128)(2,1)}, u32[]{:S(2)}) copy-start(bf16[192,3,720]{2,0,1:T(8,128)(2,1)} %param.6) | copy-start | bytes 2488324
  39.5 4.6 %collective-permute-start.10 = (bf16[24,1792]{1,0:T(8,128)(2,1)S(1)}, bf16[24,1792]{1,0:T(8,128)(2,1)S(1)}, u32[]{:S(2)}, u32[]{:S(2)}) collective-permute-start(bf16[24,1792]{1,0:T(8,128)(2,1)S(1)} %get-tuple-element.39), channel_id=1, source_target_pairs={{0,1},{1,0},{2,3},{3,2},{4,5},{5,4},{6,7},{7,6},{8,9},{9,8},{10,11... | collective-permute-start | bytes 258056 | tf_op jit(solution)/shard_map/ppermute | solution.py:409
  40.0 6.6 %collective-permute-start.11 = (bf16[24,1792]{1,0:T(8,128)(2,1)S(1)}, bf16[24,1792]{1,0:T(8,128)(2,1)S(1)}, u32[]{:S(2)}, u32[]{:S(2)}) collective-permute-start(bf16[24,1792]{1,0:T(8,128)(2,1)S(1)} %get-tuple-element.40), channel_id=1, source_target_pairs={{0,2},{1,3},{2,0},{3,1},{4,6},{5,7},{6,4},{7,5},{8,10},{9,11},{10,... | collective-permute-start | bytes 258056 | tf_op jit(solution)/shard_map/ppermute | solution.py:409
  40.2 8.7 %collective-permute-start.12 = (bf16[24,1792]{1,0:T(8,128)(2,1)S(1)}, bf16[24,1792]{1,0:T(8,128)(2,1)S(1)}, u32[]{:S(2)}, u32[]{:S(2)}) collective-permute-start(bf16[24,1792]{1,0:T(8,128)(2,1)S(1)} %get-tuple-element.41), channel_id=1, source_target_pairs={{0,3},{1,2},{2,1},{3,0},{4,7},{5,6},{6,5},{7,4},{8,11},{9,10},{10,... | collective-permute-start | bytes 258056 | tf_op jit(solution)/shard_map/ppermute | solution.py:409
  44.0 12.0 %collective-permute-start.13 = (bf16[24,1792]{1,0:T(8,128)(2,1)S(1)}, bf16[24,1792]{1,0:T(8,128)(2,1)S(1)}, u32[]{:S(2)}, u32[]{:S(2)}) collective-permute-start(bf16[24,1792]{1,0:T(8,128)(2,1)S(1)} %get-tuple-element.42), channel_id=1, source_target_pairs={{0,4},{1,5},{2,6},{3,7},{4,0},{5,1},{6,2},{7,3},{8,12},{9,13},{10,... | collective-permute-start | bytes 258056 | tf_op jit(solution)/shard_map/ppermute | solution.py:409
  46.6 11.7 %collective-permute-start.14 = (bf16[24,1792]{1,0:T(8,128)(2,1)S(1)}, bf16[24,1792]{1,0:T(8,128)(2,1)S(1)}, u32[]{:S(2)}, u32[]{:S(2)}) collective-permute-start(bf16[24,1792]{1,0:T(8,128)(2,1)S(1)} %get-tuple-element.43), channel_id=1, source_target_pairs={{0,5},{1,4},{2,7},{3,6},{4,1},{5,0},{6,3},{7,2},{8,13},{9,12},{10,... | collective-permute-start | bytes 258056 | tf_op jit(solution)/shard_map/ppermute | solution.py:409
  49.0 9.3 %collective-permute-start.15 = (bf16[24,1792]{1,0:T(8,128)(2,1)S(1)}, bf16[24,1792]{1,0:T(8,128)(2,1)S(1)}, u32[]{:S(2)}, u32[]{:S(2)}) collective-permute-start(bf16[24,1792]{1,0:T(8,128)(2,1)S(1)} %get-tuple-element.44), channel_id=1, source_target_pairs={{0,6},{1,7},{2,4},{3,5},{4,2},{5,3},{6,0},{7,1},{8,14},{9,15},{10,... | collective-permute-start | bytes 258056 | tf_op jit(solution)/shard_map/ppermute | solution.py:409
  56.0 7.9 %collective-permute-start.16 = (bf16[24,1792]{1,0:T(8,128)(2,1)S(1)}, bf16[24,1792]{1,0:T(8,128)(2,1)S(1)}, u32[]{:S(2)}, u32[]{:S(2)}) collective-permute-start(bf16[24,1792]{1,0:T(8,128)(2,1)S(1)} %get-tuple-element.45), channel_id=1, source_target_pairs={{0,7},{1,6},{2,5},{3,4},{4,3},{5,2},{6,1},{7,0},{8,15},{9,14},{10,... | collective-permute-start | bytes 258056 | tf_op jit(solution)/shard_map/ppermute | solution.py:409
  58.3 14.7 %collective-permute-start.2 = (bf16[24,1792]{1,0:T(8,128)(2,1)S(1)}, bf16[24,1792]{1,0:T(8,128)(2,1)S(1)}, u32[]{:S(2)}, u32[]{:S(2)}) collective-permute-start(bf16[24,1792]{1,0:T(8,128)(2,1)S(1)} %get-tuple-element.29), channel_id=1, source_target_pairs={{0,3},{1,2},{2,1},{3,0},{4,7},{5,6},{6,5},{7,4},{8,11},{9,10},{10,... | collective-permute-start | bytes 258056 | tf_op jit(solution)/shard_map/ppermute | solution.py:409
  58.3 14.7 %collective-permute-start.3 = (bf16[24,1792]{1,0:T(8,128)(2,1)S(1)}, bf16[24,1792]{1,0:T(8,128)(2,1)S(1)}, u32[]{:S(2)}, u32[]{:S(2)}) collective-permute-start(bf16[24,1792]{1,0:T(8,128)(2,1)S(1)} %get-tuple-element.30), channel_id=1, source_target_pairs={{0,4},{1,5},{2,6},{3,7},{4,0},{5,1},{6,2},{7,3},{8,12},{9,13},{10,... | collective-permute-start | bytes 258056 | tf_op jit(solution)/shard_map/ppermute | solution.py:409
  64.0 10.4 %collective-permute-start.4 = (bf16[24,1792]{1,0:T(8,128)(2,1)S(1)}, bf16[24,1792]{1,0:T(8,128)(2,1)S(1)}, u32[]{:S(2)}, u32[]{:S(2)}) collective-permute-start(bf16[24,1792]{1,0:T(8,128)(2,1)S(1)} %get-tuple-element.31), channel_id=1, source_target_pairs={{0,5},{1,4},{2,7},{3,6},{4,1},{5,0},{6,3},{7,2},{8,13},{9,12},{10,... | collective-permute-start | bytes 258056 | tf_op jit(solution)/shard_map/ppermute | solution.py:409
  64.0 10.4 %collective-permute-start.5 = (bf16[24,1792]{1,0:T(8,128)(2,1)S(1)}, bf16[24,1792]{1,0:T(8,128)(2,1)S(1)}, u32[]{:S(2)}, u32[]{:S(2)}) collective-permute-start(bf16[24,1792]{1,0:T(8,128)(2,1)S(1)} %get-tuple-element.32), channel_id=1, source_target_pairs={{0,6},{1,7},{2,4},{3,5},{4,2},{5,3},{6,0},{7,1},{8,14},{9,15},{10,... | collective-permute-start | bytes 258056 | tf_op jit(solution)/shard_map/ppermute | solution.py:409
  65.6 8.7 %collective-permute-start.6 = (bf16[24,1792]{1,0:T(8,128)(2,1)S(1)}, bf16[24,1792]{1,0:T(8,128)(2,1)S(1)}, u32[]{:S(2)}, u32[]{:S(2)}) collective-permute-start(bf16[24,1792]{1,0:T(8,128)(2,1)S(1)} %get-tuple-element.33), channel_id=1, source_target_pairs={{0,7},{1,6},{2,5},{3,4},{4,3},{5,2},{6,1},{7,0},{8,15},{9,14},{10,... | collective-permute-start | bytes 258056 | tf_op jit(solution)/shard_map/ppermute | solution.py:409
  76.4 1.6 %collective-permute-start.17 = (f32[56,8,128]{2,1,0:T(8,128)S(1)}, f32[56,8,128]{2,1,0:T(8,128)S(1)}, u32[]{:S(2)}, u32[]{:S(2)}) collective-permute-start(f32[56,8,128]{2,1,0:T(8,128)S(1)} %get-tuple-element.47), channel_id=1, source_target_pairs={{0,8},{8,0},{16,24},{24,16},{1,9},{9,1},{17,25},{25,17},{2,10},{10... | collective-permute-start | bytes 688136 | tf_op jit(solution)/shard_map/ppermute | solution.py:409
  78.1 4.2 %collective-permute-start.20 = (f32[14,8,128]{2,1,0:T(8,128)S(1)}, f32[14,8,128]{2,1,0:T(8,128)S(1)}, u32[]{:S(2)}, u32[]{:S(2)}) collective-permute-start(f32[14,8,128]{2,1,0:T(8,128)S(1)} %get-tuple-element.51), channel_id=1, source_target_pairs={{0,1},{1,0},{2,3},{3,2},{4,5},{5,4},{6,7},{7,6},{8,9},{9,8},{10,11... | collective-permute-start | bytes 172040 | tf_op jit(solution)/shard_map/ppermute | solution.py:430
  78.9 4.2 %collective-permute-start.19 = (f32[14,8,128]{2,1,0:T(8,128)S(1)}, f32[14,8,128]{2,1,0:T(8,128)S(1)}, u32[]{:S(2)}, u32[]{:S(2)}) collective-permute-start(f32[14,8,128]{2,1,0:T(8,128)S(1)} %get-tuple-element.52), channel_id=1, source_target_pairs={{0,16},{1,17},{2,18},{3,19},{4,20},{5,21},{6,22},{7,23},{8,24},{9,... | collective-permute-start | bytes 172040 | tf_op jit(solution)/shard_map/ppermute | solution.py:430
  80.4 5.1 %collective-permute-start.18 = (f32[14,8,128]{2,1,0:T(8,128)S(1)}, f32[14,8,128]{2,1,0:T(8,128)S(1)}, u32[]{:S(2)}, u32[]{:S(2)}) collective-permute-start(f32[14,8,128]{2,1,0:T(8,128)S(1)} %get-tuple-element.50), channel_id=1, source_target_pairs={{0,17},{1,16},{2,19},{3,18},{4,21},{5,20},{6,23},{7,22},{8,25},{9,... | collective-permute-start | bytes 172040 | tf_op jit(solution)/shard_map/ppermute | solution.py:430
  85.5 5.5 %collective-permute-start.23 = (f32[14,8,128]{2,1,0:T(8,128)S(1)}, f32[14,8,128]{2,1,0:T(8,128)S(1)}, u32[]{:S(2)}, u32[]{:S(2)}) collective-permute-start(f32[14,8,128]{2,1,0:T(8,128)S(1)} %fusion.1), channel_id=1, source_target_pairs={{0,2},{1,3},{2,0},{3,1},{4,6},{5,7},{6,4},{7,5},{8,10},{9,11},{10,... | collective-permute-start | bytes 172040 | tf_op jit(solution)/shard_map/ppermute | solution.py:409
  88.8 6.0 %collective-permute-start.21 = (f32[14,8,128]{2,1,0:T(8,128)S(1)}, f32[14,8,128]{2,1,0:T(8,128)S(1)}, u32[]{:S(2)}, u32[]{:S(2)}) collective-permute-start(f32[14,8,128]{2,1,0:T(8,128)S(1)} %fusion.1), channel_id=1, source_target_pairs={{0,6},{1,7},{2,4},{3,5},{4,2},{5,3},{6,0},{7,1},{8,14},{9,15},{10,... | collective-permute-start | bytes 172040 | tf_op jit(solution)/shard_map/ppermute | solution.py:409
  90.8 5.2 %collective-permute-start.22 = (f32[14,8,128]{2,1,0:T(8,128)S(1)}, f32[14,8,128]{2,1,0:T(8,128)S(1)}, u32[]{:S(2)}, u32[]{:S(2)}) collective-permute-start(f32[14,8,128]{2,1,0:T(8,128)S(1)} %fusion.1), channel_id=1, source_target_pairs={{0,4},{1,5},{2,6},{3,7},{4,0},{5,1},{6,2},{7,3},{8,12},{9,13},{10,... | collective-permute-start | bytes 172040 | tf_op jit(solution)/shard_map/ppermute | solution.py:409
  96.0 4.3 %collective-permute-start.24 = (f32[14,8,128]{2,1,0:T(8,128)S(1)}, f32[14,8,128]{2,1,0:T(8,128)S(1)}, u32[]{:S(2)}, u32[]{:S(2)}) collective-permute-start(f32[14,8,128]{2,1,0:T(8,128)S(1)} %add_add_fusion.refs_0_), channel_id=1, source_target_pairs={{0,1},{1,0},{2,3},{3,2},{4,5},{5,4},{6,7},{7,6},{8,9},{9,8},{10,11... | collective-permute-start | bytes 172040 | tf_op jit(solution)/shard_map/ppermute | solution.py:430
  97.4 4.2 %collective-permute-start.25 = (f32[14,8,128]{2,1,0:T(8,128)S(1)}, f32[14,8,128]{2,1,0:T(8,128)S(1)}, u32[]{:S(2)}, u32[]{:S(2)}) collective-permute-start(f32[14,8,128]{2,1,0:T(8,128)S(1)} %add_add_fusion.refs_0_), channel_id=1, source_target_pairs={{0,16},{1,17},{2,18},{3,19},{4,20},{5,21},{6,22},{7,23},{8,24},{9,... | collective-permute-start | bytes 172040 | tf_op jit(solution)/shard_map/ppermute | solution.py:430
  97.9 5.1 %collective-permute-start.26 = (f32[14,8,128]{2,1,0:T(8,128)S(1)}, f32[14,8,128]{2,1,0:T(8,128)S(1)}, u32[]{:S(2)}, u32[]{:S(2)}) collective-permute-start(f32[14,8,128]{2,1,0:T(8,128)S(1)} %add_add_fusion.refs_0_), channel_id=1, source_target_pairs={{0,17},{1,16},{2,19},{3,18},{4,21},{5,20},{6,23},{7,22},{8,25},{9,... | collective-permute-start | bytes 172040 | tf_op jit(solution)/shard_map/ppermute | solution.py:430
  99.6 3.4 %collective-permute-start.27 = (f32[14,8,128]{2,1,0:T(8,128)S(1)}, f32[14,8,128]{2,1,0:T(8,128)S(1)}, u32[]{:S(2)}, u32[]{:S(2)}) collective-permute-start(f32[14,8,128]{2,1,0:T(8,128)S(1)} %add_add_fusion.refs_0_), channel_id=1, source_target_pairs={{0,8},{8,0},{16,24},{24,16},{1,9},{9,1},{17,25},{25,17},{2,10},{10... | collective-permute-start | bytes 172040 | tf_op jit(solution)/shard_map/ppermute | solution.py:409
  100.4 2.6 %collective-permute-start.28 = (f32[14,8,128]{2,1,0:T(8,128)S(1)}, f32[14,8,128]{2,1,0:T(8,128)S(1)}, u32[]{:S(2)}, u32[]{:S(2)}) collective-permute-start(f32[14,8,128]{2,1,0:T(8,128)S(1)} %collective-permute-done.24.refs_1_), channel_id=1, source_target_pairs={{0,8},{8,0},{16,24},{24,16},{1,9},{9,1},{17,25},{25,17},{2,10},{10... | collective-permute-start | bytes 172040 | tf_op jit(solution)/shard_map/ppermute | solution.py:409
  101.5 1.5 %collective-permute-start.29 = (f32[14,8,128]{2,1,0:T(8,128)S(1)}, f32[14,8,128]{2,1,0:T(8,128)S(1)}, u32[]{:S(2)}, u32[]{:S(2)}) collective-permute-start(f32[14,8,128]{2,1,0:T(8,128)S(1)} %collective-permute-done.25.refs_2_), channel_id=1, source_target_pairs={{0,8},{8,0},{16,24},{24,16},{1,9},{9,1},{17,25},{25,17},{2,10},{10... | collective-permute-start | bytes 172040 | tf_op jit(solution)/shard_map/ppermute | solution.py:409
  103.0 1.2 %collective-permute-start.30 = (f32[14,8,128]{2,1,0:T(8,128)S(1)}, f32[14,8,128]{2,1,0:T(8,128)S(1)}, u32[]{:S(2)}, u32[]{:S(2)}) collective-permute-start(f32[14,8,128]{2,1,0:T(8,128)S(1)} %collective-permute-done.26.refs_3_), channel_id=1, source_target_pairs={{0,8},{8,0},{16,24},{24,16},{1,9},{9,1},{17,25},{25,17},{2,10},{10... | collective-permute-start | bytes 172040 | tf_op jit(solution)/shard_map/ppermute | solution.py:409
  (2 other events, 3.6 us)

commit v7 on v6

--- a/solution.py
+++ b/solution.py
@@ -140,7 +140,7 @@
     rows_all, lon_count = field.shape
     width = round_up(rows_all, LANES)
     columns = table.shape[1]
-    step = 5 * LANES
+    step = 6 * LANES
     chunks = [min(step, rows_all - row) for row in range(0, rows_all, step)]
     anywhere = pl.BlockSpec(memory_space=pl.ANY)
     vmem = pl.BlockSpec(memory_space=pltpu.VMEM)
@@ -430,6 +430,16 @@
     return lax.ppermute(value, ("batch", "lat"), [(i, i ^ step) for i in range(count)])
 
 
+def band_stages(bands):
+    stages, step = [], 2
+    radix = 2 if bands.bit_length() % 2 == 1 else 4
+    while step < bands:
+        stages.append([k * step for k in sorted(range(1, radix), key=lambda k: (k == 1, k))])
+        step *= radix
+        radix = 4
+    return stages
+
+
 def reduce_all(kept, sent):
     mesh_size = groups, bands = lax.axis_size("batch"), lax.axis_size("lat")
     value = kept + exchange(sent, "batch", 1)
@@ -445,13 +455,11 @@
     while step < groups:
         value = value + exchange(value, "batch", step)
         step *= 2
-    step = 2
-    radix = 2 if bands.bit_length() % 2 == 1 else 4
-    while step < bands:
-        parts = [exchange(value, "lat", k * step) for k in range(radix - 1, 0, -1)]
+    for distances in band_stages(bands):
+        parts = []
+        for distance in distances:
+            parts.append(exchange(value, "lat", distance))
         value = value + sum(parts[1:], parts[0])
-        step *= radix
-        radix = 4
     owned = [value]
     for m in range(1, len(steps)):
         owned.append(flat_exchange(value, mesh_size, steps[m]))

time: 106 us -> 105 us (level)
  waiting for transfers between devices: 45.1 us -> 43.7 us
  transfers between devices with their start and end apart: 31 -> 31, of which waited for: 16 -> 15; matrix products, arithmetic and copies ran while one was open for 0% -> 0% of each run, Pallas kernels for 14% -> 14%
where the time goes in v7:
time: 105 us
  waiting for transfers between devices  43.7 us (42%)
  starting transfers between devices  38.3 us (36%)
  Pallas kernels  18.2 us (17%)
  local copies, waits for them, and re-layouts  3.67 us (3%)
    ppermute x25, waiting for transfers between devices, exchange(): return lax.ppermute(value, axis, peers(lax.axis_size(axis), step))  36.9 us
    ppermute x25, starting transfers between devices, exchange(): return lax.ppermute(value, axis, peers(lax.axis_size(axis), step))  31.2 us
    ppermute x6, starting transfers between devices, flat_exchange(): lax.ppermute(value, ('batch', 'lat'), [(i, i ^ step) for i in range(count)])  7.1 us
    ppermute x6, waiting for transfers between devices, flat_exchange(): lax.ppermute(value, ('batch', 'lat'), [(i, i ^ step) for i in range(count)])  6.75 us
    pallas_call x1, Pallas kernels, row_blocks(): pl.pallas_call(functools.partial(rows_kernel, bands, per, tuple(chunks)),...  5.38 us
    pallas_call x1, Pallas kernels, dft_blocks(): pl.pallas_call(functools.partial(dft_kernel, bands, per, chans, lats, tup...  3.79 us
    pallas_call x2, Pallas kernels, legendre_energy(): pl.pallas_call(functools.partial(legendre_kernel, bands, groups, per_dev,...  3.76 us
    unnamed x6, local copies, waits for them, and re-layouts  3.65 us
  transfers between devices with their start and end apart: 31, of which 15 were waited for; matrix products, arithmetic and copies ran while one was open for 0% of the time, Pallas kernels for 14%

profile of v7, /device:TPU:0, one launch (start us, length us, event | category | flops | bytes accessed | tf_op | source)
XLA Modules:
  0.0 104.7 jit_solution(1702303425728115592)
XLA Ops:
  0.6 3.0 %collective-permute-start.7 = (bf16[3,192,720]{2,1,0:T(8,128)(2,1)}, bf16[3,192,720]{2,1,0:T(8,128)(2,1)S(1)}, u32[]{:S(2)}, u32[]{:S(2)}) collective-permute-start(bf16[3,192,720]{2,1,0:T(8,128)(2,1)} %bitcast.19), channel_id=1, source_target_pairs={{0,16},{8,24},{16,0},{24,8},{1,17},{9,25},{17,1},{25,9},{2,18},{10... | collective-permute-start | bytes 2488328 | tf_op jit(solution)/shard_map/ppermute | solution.py:409
  3.7 19.9 %collective-permute-done.7.refs_1_ = bf16[3,192,720]{2,1,0:T(8,128)(2,1)S(1)} collective-permute-done((bf16[3,192,720]{2,1,0:T(8,128)(2,1)}, bf16[3,192,720]{2,1,0:T(8,128)(2,1)S(1)}, u32[]{:S(2)}, u32[]{:S(2)}) %collective-permute-start.7) | collective-permute-done | bytes 829472 | tf_op jit(solution)/shard_map/ppermute | solution.py:409
  23.5 2.5 %copy-done = bf16[1,73,24,1440]{3,2,1,0:T(8,128)(2,1)S(1)} copy-done((bf16[1,73,24,1440]{3,2,1,0:T(8,128)(2,1)S(1)}, bf16[1,73,24,1440]{3,2,1,0:T(8,128)(2,1)}, u32[]{:S(2)}) %copy-start) | copy-done | bytes 5045784
  27.2 3.8 %dft.1 = (bf16[24,1792]{1,0:T(8,128)(2,1)S(1)}, bf16[24,1792]{1,0:T(8,128)(2,1)S(1)}, bf16[24,1792]{1,0:T(8,128)(2,1)S(1)}, bf16[24,1792]{1,0:T(8,128)(2,1)S(1)}...) custom-call(bf16[1752,1440]{1,0:T(8,128)(2,1)S(1)} %bitcast.18, ...), custom_call_target="tpu_custom_call" | custom-call | tf_op jit(solution)/shard_map/dft/pallas_call | solution.py:182
  31.0 1.8 %collective-permute-start = (bf16[24,1792]{1,0:T(8,128)(2,1)S(1)}, bf16[24,1792]{1,0:T(8,128)(2,1)S(1)}, u32[]{:S(2)}, u32[]{:S(2)}) collective-permute-start(bf16[24,1792]{1,0:T(8,128)(2,1)S(1)} %get-tuple-element.27), channel_id=1, source_target_pairs={{0,1},{1,0},{2,3},{3,2},{4,5},{5,4},{6,7},{7,6},{8,9},{9,8},{10,11... | collective-permute-start | bytes 258056 | tf_op jit(solution)/shard_map/ppermute | solution.py:409
  32.8 1.6 %collective-permute-start.1 = (bf16[24,1792]{1,0:T(8,128)(2,1)S(1)}, bf16[24,1792]{1,0:T(8,128)(2,1)S(1)}, u32[]{:S(2)}, u32[]{:S(2)}) collective-permute-start(bf16[24,1792]{1,0:T(8,128)(2,1)S(1)} %get-tuple-element.28), channel_id=1, source_target_pairs={{0,2},{1,3},{2,0},{3,1},{4,6},{5,7},{6,4},{7,5},{8,10},{9,11},{10,... | collective-permute-start | bytes 258056 | tf_op jit(solution)/shard_map/ppermute | solution.py:409
  34.4 5.4 %dft_rows.1 = (bf16[24,1792]{1,0:T(8,128)(2,1)S(1)}, bf16[24,1792]{1,0:T(8,128)(2,1)S(1)}, bf16[24,1792]{1,0:T(8,128)(2,1)S(1)}, bf16[24,1792]{1,0:T(8,128)(2,1)...) custom-call(bf16[1752,1440]{1,0:T(8,128)(2,1)} %bitcast.22, ...), custom_call_target="tpu_custom_call" | custom-call | tf_op jit(solution)/shard_map/dft_rows/pallas_call | solution.py:147
  40.6 2.8 %collective-permute-start.12 = (bf16[24,1792]{1,0:T(8,128)(2,1)S(1)}, bf16[24,1792]{1,0:T(8,128)(2,1)S(1)}, u32[]{:S(2)}, u32[]{:S(2)}) collective-permute-start(bf16[24,1792]{1,0:T(8,128)(2,1)S(1)} %get-tuple-element.41), channel_id=1, source_target_pairs={{0,3},{1,2},{2,1},{3,0},{4,7},{5,6},{6,5},{7,4},{8,11},{9,10},{10,... | collective-permute-start | bytes 258056 | tf_op jit(solution)/shard_map/ppermute | solution.py:409
  44.3 2.6 %collective-permute-start.13 = (bf16[24,1792]{1,0:T(8,128)(2,1)S(1)}, bf16[24,1792]{1,0:T(8,128)(2,1)S(1)}, u32[]{:S(2)}, u32[]{:S(2)}) collective-permute-start(bf16[24,1792]{1,0:T(8,128)(2,1)S(1)} %get-tuple-element.42), channel_id=1, source_target_pairs={{0,4},{1,5},{2,6},{3,7},{4,0},{5,1},{6,2},{7,3},{8,12},{9,13},{10,... | collective-permute-start | bytes 258056 | tf_op jit(solution)/shard_map/ppermute | solution.py:409
  46.9 2.4 %collective-permute-start.14 = (bf16[24,1792]{1,0:T(8,128)(2,1)S(1)}, bf16[24,1792]{1,0:T(8,128)(2,1)S(1)}, u32[]{:S(2)}, u32[]{:S(2)}) collective-permute-start(bf16[24,1792]{1,0:T(8,128)(2,1)S(1)} %get-tuple-element.43), channel_id=1, source_target_pairs={{0,5},{1,4},{2,7},{3,6},{4,1},{5,0},{6,3},{7,2},{8,13},{9,12},{10,... | collective-permute-start | bytes 258056 | tf_op jit(solution)/shard_map/ppermute | solution.py:409
  49.3 1.7 %collective-permute-start.15 = (bf16[24,1792]{1,0:T(8,128)(2,1)S(1)}, bf16[24,1792]{1,0:T(8,128)(2,1)S(1)}, u32[]{:S(2)}, u32[]{:S(2)}) collective-permute-start(bf16[24,1792]{1,0:T(8,128)(2,1)S(1)} %get-tuple-element.44), channel_id=1, source_target_pairs={{0,6},{1,7},{2,4},{3,5},{4,2},{5,3},{6,0},{7,1},{8,14},{9,15},{10,... | collective-permute-start | bytes 258056 | tf_op jit(solution)/shard_map/ppermute | solution.py:409
  51.0 5.3 %collective-permute-done.13.refs_4_ = bf16[24,1792]{1,0:T(8,128)(2,1)S(1)} collective-permute-done((bf16[24,1792]{1,0:T(8,128)(2,1)S(1)}, bf16[24,1792]{1,0:T(8,128)(2,1)S(1)}, u32[]{:S(2)}, u32[]{:S(2)}) %collective-permute-start.13) | collective-permute-done | bytes 86048 | tf_op jit(solution)/shard_map/ppermute | solution.py:409
  56.4 2.2 %collective-permute-start.16 = (bf16[24,1792]{1,0:T(8,128)(2,1)S(1)}, bf16[24,1792]{1,0:T(8,128)(2,1)S(1)}, u32[]{:S(2)}, u32[]{:S(2)}) collective-permute-start(bf16[24,1792]{1,0:T(8,128)(2,1)S(1)} %get-tuple-element.45), channel_id=1, source_target_pairs={{0,7},{1,6},{2,5},{3,4},{4,3},{5,2},{6,1},{7,0},{8,15},{9,14},{10,... | collective-permute-start | bytes 258056 | tf_op jit(solution)/shard_map/ppermute | solution.py:409
  58.6 3.4 %collective-permute-start.3 = (bf16[24,1792]{1,0:T(8,128)(2,1)S(1)}, bf16[24,1792]{1,0:T(8,128)(2,1)S(1)}, u32[]{:S(2)}, u32[]{:S(2)}) collective-permute-start(bf16[24,1792]{1,0:T(8,128)(2,1)S(1)} %get-tuple-element.30), channel_id=1, source_target_pairs={{0,4},{1,5},{2,6},{3,7},{4,0},{5,1},{6,2},{7,3},{8,12},{9,13},{10,... | collective-permute-start | bytes 258056 | tf_op jit(solution)/shard_map/ppermute | solution.py:409
  61.9 2.4 %collective-permute-done.16.refs_7_ = bf16[24,1792]{1,0:T(8,128)(2,1)S(1)} collective-permute-done((bf16[24,1792]{1,0:T(8,128)(2,1)S(1)}, bf16[24,1792]{1,0:T(8,128)(2,1)S(1)}, u32[]{:S(2)}, u32[]{:S(2)}) %collective-permute-start.16) | collective-permute-done | bytes 86048 | tf_op jit(solution)/shard_map/ppermute | solution.py:409
  64.3 1.6 %collective-permute-start.5 = (bf16[24,1792]{1,0:T(8,128)(2,1)S(1)}, bf16[24,1792]{1,0:T(8,128)(2,1)S(1)}, u32[]{:S(2)}, u32[]{:S(2)}) collective-permute-start(bf16[24,1792]{1,0:T(8,128)(2,1)S(1)} %get-tuple-element.32), channel_id=1, source_target_pairs={{0,6},{1,7},{2,4},{3,5},{4,2},{5,3},{6,0},{7,1},{8,14},{9,15},{10,... | collective-permute-start | bytes 258056 | tf_op jit(solution)/shard_map/ppermute | solution.py:409
  65.9 1.5 %collective-permute-start.6 = (bf16[24,1792]{1,0:T(8,128)(2,1)S(1)}, bf16[24,1792]{1,0:T(8,128)(2,1)S(1)}, u32[]{:S(2)}, u32[]{:S(2)}) collective-permute-start(bf16[24,1792]{1,0:T(8,128)(2,1)S(1)} %get-tuple-element.33), channel_id=1, source_target_pairs={{0,7},{1,6},{2,5},{3,4},{4,3},{5,2},{6,1},{7,0},{8,15},{9,14},{10,... | collective-permute-start | bytes 258056 | tf_op jit(solution)/shard_map/ppermute | solution.py:409
  67.5 2.8 %prepare.1.rest_0_ = bf16[12,192,146]{2,1,0:T(8,128)(2,1)S(1)} custom-call(bf16[24,1792]{1,0:T(8,128)(2,1)S(1)} %get-tuple-element.38.refs_0_, bf16[24,1792]{1,0:T(8,128)(2,1)S(1)} %collective-permute-done.10.refs_1_, bf16[24,1792]{1,0:T(8,128)(2,1)S(1)} %collective-permute-done.11.refs_2_, bf16[24,1792]{1,0:T(8,128)(2,1)S(1)} %collective-permute-done.12.refs_3_, ...), custom_call_target="tpu_custom_call" | custom-call | tf_op jit(solution)/shard_map/prepare/pallas_call | solution.py:252
  70.3 1.2 %turn.1 = (bf16[3,720,256]{2,1,0:T(8,128)(2,1)S(1)}, bf16[3,720,256]{2,1,0:T(8,128)(2,1)S(1)}, bf16[3,720,256]{2,1,0:T(8,128)(2,1)S(1)}, bf16[3,720,256]{2,1,0:T(8,128)(2,1)S(1)}) custom-call(bf16[3,192,720]{2,1,0:T(8,128)(2,1)S(1)} %bitcast.21, bf16[3,192,720]{2,1,0:T(8,128)(2,1)S(1)} %collective-permute-done.7.refs_1_, ...), custom_call_target="tpu_custom_call" | custom-call | tf_op jit(solution)/shard_map/turn/pallas_call | solution.py:209
  71.6 1.7 %legendre.2.rest_12_ = f32[56,8,128]{2,1,0:T(8,128)S(1)} custom-call(bf16[12,192,146]{2,1,0:T(8,128)(2,1)S(1)} %prepare.1.rest_0_, bf16[3,720,256]{2,1,0:T(8,128)(2,1)S(1)} %get-tuple-element.34.rest_1_.rest_8_, bf16[3,720,256]{2,1,0:T(8,128)(2,1)S(1)} %get-tuple-element.35.rest_2_.rest_9_, bf16[3,720,256]{2,1,0:T(8,128)(2,1)S(1)} %get-tuple-element.36.rest_3_.rest_10_, ...), custom_call_target="tpu_custom_call" | custom-call | tf_op jit(solution)/shard_map/legendre/pallas_call | solution.py:343
  73.3 1.4 %collective-permute-done.4.rest_5_ = bf16[24,1792]{1,0:T(8,128)(2,1)S(1)} collective-permute-done((bf16[24,1792]{1,0:T(8,128)(2,1)S(1)}, bf16[24,1792]{1,0:T(8,128)(2,1)S(1)}, u32[]{:S(2)}, u32[]{:S(2)}) %collective-permute-start.4) | collective-permute-done | bytes 86048 | tf_op jit(solution)/shard_map/ppermute | solution.py:409
  74.7 2.1 %legendre.3 = (f32[56,8,128]{2,1,0:T(8,128)S(1)}, f32[56,8,128]{2,1,0:T(8,128)S(1)}) custom-call(bf16[24,1792]{1,0:T(8,128)(2,1)S(1)} %get-tuple-element.26.rest_0_, bf16[24,1792]{1,0:T(8,128)(2,1)S(1)} %collective-permute-done.rest_1_, bf16[24,1792]{1,0:T(8,128)(2,1)S(1)} %collective-permute-done.1.rest_2_, ...), custom_call_target="tpu_custom_call" | custom-call | tf_op jit(solution)/shard_map/legendre/pallas_call | solution.py:343
  76.9 1.4 %collective-permute-done.17 = f32[56,8,128]{2,1,0:T(8,128)S(1)} collective-permute-done((f32[56,8,128]{2,1,0:T(8,128)S(1)}, f32[56,8,128]{2,1,0:T(8,128)S(1)}, u32[]{:S(2)}, u32[]{:S(2)}) %collective-permute-start.17) | collective-permute-done | bytes 229408 | tf_op jit(solution)/shard_map/ppermute | solution.py:409
  79.2 1.5 %collective-permute-start.19 = (f32[14,8,128]{2,1,0:T(8,128)S(1)}, f32[14,8,128]{2,1,0:T(8,128)S(1)}, u32[]{:S(2)}, u32[]{:S(2)}) collective-permute-start(f32[14,8,128]{2,1,0:T(8,128)S(1)} %get-tuple-element.52), channel_id=1, source_target_pairs={{0,16},{1,17},{2,18},{3,19},{4,20},{5,21},{6,22},{7,23},{8,24},{9,... | collective-permute-start | bytes 172040 | tf_op jit(solution)/shard_map/ppermute | solution.py:430
  80.7 1.2 %collective-permute-start.18 = (f32[14,8,128]{2,1,0:T(8,128)S(1)}, f32[14,8,128]{2,1,0:T(8,128)S(1)}, u32[]{:S(2)}, u32[]{:S(2)}) collective-permute-start(f32[14,8,128]{2,1,0:T(8,128)S(1)} %get-tuple-element.50), channel_id=1, source_target_pairs={{0,17},{1,16},{2,19},{3,18},{4,21},{5,20},{6,23},{7,22},{8,25},{9,... | collective-permute-start | bytes 172040 | tf_op jit(solution)/shard_map/ppermute | solution.py:430
  83.4 2.4 %collective-permute-done.18 = f32[14,8,128]{2,1,0:T(8,128)S(1)} collective-permute-done((f32[14,8,128]{2,1,0:T(8,128)S(1)}, f32[14,8,128]{2,1,0:T(8,128)S(1)}, u32[]{:S(2)}, u32[]{:S(2)}) %collective-permute-start.18) | collective-permute-done | bytes 57376 | tf_op jit(solution)/shard_map/ppermute | solution.py:430
  85.8 3.3 %collective-permute-start.23 = (f32[14,8,128]{2,1,0:T(8,128)S(1)}, f32[14,8,128]{2,1,0:T(8,128)S(1)}, u32[]{:S(2)}, u32[]{:S(2)}) collective-permute-start(f32[14,8,128]{2,1,0:T(8,128)S(1)} %fusion.1), channel_id=1, source_target_pairs={{0,2},{1,3},{2,0},{3,1},{4,6},{5,7},{6,4},{7,5},{8,10},{9,11},{10,... | collective-permute-start | bytes 172040 | tf_op jit(solution)/shard_map/ppermute | solution.py:409
  89.8 1.8 %collective-permute-start.22 = (f32[14,8,128]{2,1,0:T(8,128)S(1)}, f32[14,8,128]{2,1,0:T(8,128)S(1)}, u32[]{:S(2)}, u32[]{:S(2)}) collective-permute-start(f32[14,8,128]{2,1,0:T(8,128)S(1)} %fusion.1), channel_id=1, source_target_pairs={{0,6},{1,7},{2,4},{3,5},{4,2},{5,3},{6,0},{7,1},{8,14},{9,15},{10,... | collective-permute-start | bytes 172040 | tf_op jit(solution)/shard_map/ppermute | solution.py:409
  91.6 3.2 %collective-permute-done.21 = f32[14,8,128]{2,1,0:T(8,128)S(1)} collective-permute-done((f32[14,8,128]{2,1,0:T(8,128)S(1)}, f32[14,8,128]{2,1,0:T(8,128)S(1)}, u32[]{:S(2)}, u32[]{:S(2)}) %collective-permute-start.21) | collective-permute-done | bytes 57376 | tf_op jit(solution)/shard_map/ppermute | solution.py:409
  97.2 2.2 %collective-permute-start.26 = (f32[14,8,128]{2,1,0:T(8,128)S(1)}, f32[14,8,128]{2,1,0:T(8,128)S(1)}, u32[]{:S(2)}, u32[]{:S(2)}) collective-permute-start(f32[14,8,128]{2,1,0:T(8,128)S(1)} %add_add_fusion.refs_0_), channel_id=1, source_target_pairs={{0,17},{1,16},{2,19},{3,18},{4,21},{5,20},{6,23},{7,22},{8,25},{9,... | collective-permute-start | bytes 172040 | tf_op jit(solution)/shard_map/ppermute | solution.py:430
  100.8 1.5 %collective-permute-done.26.refs_3_ = f32[14,8,128]{2,1,0:T(8,128)S(1)} collective-permute-done((f32[14,8,128]{2,1,0:T(8,128)S(1)}, f32[14,8,128]{2,1,0:T(8,128)S(1)}, u32[]{:S(2)}, u32[]{:S(2)}) %collective-permute-start.26) | collective-permute-done | bytes 57376 | tf_op jit(solution)/shard_map/ppermute | solution.py:430
  102.3 1.2 %collective-permute-done.30.refs_7_ = f32[14,8,128]{2,1,0:T(8,128)S(1)} collective-permute-done((f32[14,8,128]{2,1,0:T(8,128)S(1)}, f32[14,8,128]{2,1,0:T(8,128)S(1)}, u32[]{:S(2)}, u32[]{:S(2)}) %collective-permute-start.30) | collective-permute-done | bytes 57376 | tf_op jit(solution)/shard_map/ppermute | solution.py:409
  (47 shorter events, 11.0 us)
Async XLA Ops:
  0.6 22.9 %collective-permute-start.7 = (bf16[3,192,720]{2,1,0:T(8,128)(2,1)}, bf16[3,192,720]{2,1,0:T(8,128)(2,1)S(1)}, u32[]{:S(2)}, u32[]{:S(2)}) collective-permute-start(bf16[3,192,720]{2,1,0:T(8,128)(2,1)} %bitcast.19), channel_id=1, source_target_pairs={{0,16},{8,24},{16,0},{24,8},{1,17},{9,25},{17,1},{25,9},{2,18},{10... | collective-permute-start | bytes 2488328 | tf_op jit(solution)/shard_map/ppermute | solution.py:409
  3.7 60.6 %collective-permute-start.8 = (bf16[3,192,720]{2,1,0:T(8,128)(2,1)}, bf16[3,192,720]{2,1,0:T(8,128)(2,1)S(1)}, u32[]{:S(2)}, u32[]{:S(2)}) collective-permute-start(bf16[3,192,720]{2,1,0:T(8,128)(2,1)} %bitcast.20), channel_id=1, source_target_pairs={{0,8},{8,0},{16,24},{24,16},{1,9},{9,1},{17,25},{25,17},{2,10},{10... | collective-permute-start | bytes 2488328 | tf_op jit(solution)/shard_map/ppermute | solution.py:409
  23.5 42.4 %collective-permute-start.9 = (bf16[3,192,720]{2,1,0:T(8,128)(2,1)S(1)}, bf16[3,192,720]{2,1,0:T(8,128)(2,1)S(1)}, u32[]{:S(2)}, u32[]{:S(2)}) collective-permute-start(bf16[3,192,720]{2,1,0:T(8,128)(2,1)S(1)} %collective-permute-done.7.refs_1_), channel_id=1, source_target_pairs={{0,8},{8,0},{16,24},{24,16},{1,9},{9,1},{17,25},{25,17},{2,10},{10... | collective-permute-start | bytes 2488328 | tf_op jit(solution)/shard_map/ppermute | solution.py:409
  31.0 9.4 %collective-permute-start = (bf16[24,1792]{1,0:T(8,128)(2,1)S(1)}, bf16[24,1792]{1,0:T(8,128)(2,1)S(1)}, u32[]{:S(2)}, u32[]{:S(2)}) collective-permute-start(bf16[24,1792]{1,0:T(8,128)(2,1)S(1)} %get-tuple-element.27), channel_id=1, source_target_pairs={{0,1},{1,0},{2,3},{3,2},{4,5},{5,4},{6,7},{7,6},{8,9},{9,8},{10,11... | collective-permute-start | bytes 258056 | tf_op jit(solution)/shard_map/ppermute | solution.py:409
  32.8 7.8 %collective-permute-start.1 = (bf16[24,1792]{1,0:T(8,128)(2,1)S(1)}, bf16[24,1792]{1,0:T(8,128)(2,1)S(1)}, u32[]{:S(2)}, u32[]{:S(2)}) collective-permute-start(bf16[24,1792]{1,0:T(8,128)(2,1)S(1)} %get-tuple-element.28), channel_id=1, source_target_pairs={{0,2},{1,3},{2,0},{3,1},{4,6},{5,7},{6,4},{7,5},{8,10},{9,11},{10,... | collective-permute-start | bytes 258056 | tf_op jit(solution)/shard_map/ppermute | solution.py:409
  39.8 30.5 %copy-start.2 = (bf16[192,3,720]{2,0,1:T(8,128)(2,1)S(1)}, bf16[192,3,720]{2,0,1:T(8,128)(2,1)}, u32[]{:S(2)}) copy-start(bf16[192,3,720]{2,0,1:T(8,128)(2,1)} %param.6) | copy-start | bytes 2488324
  39.8 4.6 %collective-permute-start.10 = (bf16[24,1792]{1,0:T(8,128)(2,1)S(1)}, bf16[24,1792]{1,0:T(8,128)(2,1)S(1)}, u32[]{:S(2)}, u32[]{:S(2)}) collective-permute-start(bf16[24,1792]{1,0:T(8,128)(2,1)S(1)} %get-tuple-element.39), channel_id=1, source_target_pairs={{0,1},{1,0},{2,3},{3,2},{4,5},{5,4},{6,7},{7,6},{8,9},{9,8},{10,11... | collective-permute-start | bytes 258056 | tf_op jit(solution)/shard_map/ppermute | solution.py:409
  40.3 6.6 %collective-permute-start.11 = (bf16[24,1792]{1,0:T(8,128)(2,1)S(1)}, bf16[24,1792]{1,0:T(8,128)(2,1)S(1)}, u32[]{:S(2)}, u32[]{:S(2)}) collective-permute-start(bf16[24,1792]{1,0:T(8,128)(2,1)S(1)} %get-tuple-element.40), channel_id=1, source_target_pairs={{0,2},{1,3},{2,0},{3,1},{4,6},{5,7},{6,4},{7,5},{8,10},{9,11},{10,... | collective-permute-start | bytes 258056 | tf_op jit(solution)/shard_map/ppermute | solution.py:409
  40.6 8.7 %collective-permute-start.12 = (bf16[24,1792]{1,0:T(8,128)(2,1)S(1)}, bf16[24,1792]{1,0:T(8,128)(2,1)S(1)}, u32[]{:S(2)}, u32[]{:S(2)}) collective-permute-start(bf16[24,1792]{1,0:T(8,128)(2,1)S(1)} %get-tuple-element.41), channel_id=1, source_target_pairs={{0,3},{1,2},{2,1},{3,0},{4,7},{5,6},{6,5},{7,4},{8,11},{9,10},{10,... | collective-permute-start | bytes 258056 | tf_op jit(solution)/shard_map/ppermute | solution.py:409
  44.3 12.0 %collective-permute-start.13 = (bf16[24,1792]{1,0:T(8,128)(2,1)S(1)}, bf16[24,1792]{1,0:T(8,128)(2,1)S(1)}, u32[]{:S(2)}, u32[]{:S(2)}) collective-permute-start(bf16[24,1792]{1,0:T(8,128)(2,1)S(1)} %get-tuple-element.42), channel_id=1, source_target_pairs={{0,4},{1,5},{2,6},{3,7},{4,0},{5,1},{6,2},{7,3},{8,12},{9,13},{10,... | collective-permute-start | bytes 258056 | tf_op jit(solution)/shard_map/ppermute | solution.py:409
  46.9 11.7 %collective-permute-start.14 = (bf16[24,1792]{1,0:T(8,128)(2,1)S(1)}, bf16[24,1792]{1,0:T(8,128)(2,1)S(1)}, u32[]{:S(2)}, u32[]{:S(2)}) collective-permute-start(bf16[24,1792]{1,0:T(8,128)(2,1)S(1)} %get-tuple-element.43), channel_id=1, source_target_pairs={{0,5},{1,4},{2,7},{3,6},{4,1},{5,0},{6,3},{7,2},{8,13},{9,12},{10,... | collective-permute-start | bytes 258056 | tf_op jit(solution)/shard_map/ppermute | solution.py:409
  49.3 9.3 %collective-permute-start.15 = (bf16[24,1792]{1,0:T(8,128)(2,1)S(1)}, bf16[24,1792]{1,0:T(8,128)(2,1)S(1)}, u32[]{:S(2)}, u32[]{:S(2)}) collective-permute-start(bf16[24,1792]{1,0:T(8,128)(2,1)S(1)} %get-tuple-element.44), channel_id=1, source_target_pairs={{0,6},{1,7},{2,4},{3,5},{4,2},{5,3},{6,0},{7,1},{8,14},{9,15},{10,... | collective-permute-start | bytes 258056 | tf_op jit(solution)/shard_map/ppermute | solution.py:409
  56.4 7.9 %collective-permute-start.16 = (bf16[24,1792]{1,0:T(8,128)(2,1)S(1)}, bf16[24,1792]{1,0:T(8,128)(2,1)S(1)}, u32[]{:S(2)}, u32[]{:S(2)}) collective-permute-start(bf16[24,1792]{1,0:T(8,128)(2,1)S(1)} %get-tuple-element.45), channel_id=1, source_target_pairs={{0,7},{1,6},{2,5},{3,4},{4,3},{5,2},{6,1},{7,0},{8,15},{9,14},{10,... | collective-permute-start | bytes 258056 | tf_op jit(solution)/shard_map/ppermute | solution.py:409
  58.6 14.7 %collective-permute-start.2 = (bf16[24,1792]{1,0:T(8,128)(2,1)S(1)}, bf16[24,1792]{1,0:T(8,128)(2,1)S(1)}, u32[]{:S(2)}, u32[]{:S(2)}) collective-permute-start(bf16[24,1792]{1,0:T(8,128)(2,1)S(1)} %get-tuple-element.29), channel_id=1, source_target_pairs={{0,3},{1,2},{2,1},{3,0},{4,7},{5,6},{6,5},{7,4},{8,11},{9,10},{10,... | collective-permute-start | bytes 258056 | tf_op jit(solution)/shard_map/ppermute | solution.py:409
  58.6 14.7 %collective-permute-start.3 = (bf16[24,1792]{1,0:T(8,128)(2,1)S(1)}, bf16[24,1792]{1,0:T(8,128)(2,1)S(1)}, u32[]{:S(2)}, u32[]{:S(2)}) collective-permute-start(bf16[24,1792]{1,0:T(8,128)(2,1)S(1)} %get-tuple-element.30), channel_id=1, source_target_pairs={{0,4},{1,5},{2,6},{3,7},{4,0},{5,1},{6,2},{7,3},{8,12},{9,13},{10,... | collective-permute-start | bytes 258056 | tf_op jit(solution)/shard_map/ppermute | solution.py:409
  64.3 10.4 %collective-permute-start.4 = (bf16[24,1792]{1,0:T(8,128)(2,1)S(1)}, bf16[24,1792]{1,0:T(8,128)(2,1)S(1)}, u32[]{:S(2)}, u32[]{:S(2)}) collective-permute-start(bf16[24,1792]{1,0:T(8,128)(2,1)S(1)} %get-tuple-element.31), channel_id=1, source_target_pairs={{0,5},{1,4},{2,7},{3,6},{4,1},{5,0},{6,3},{7,2},{8,13},{9,12},{10,... | collective-permute-start | bytes 258056 | tf_op jit(solution)/shard_map/ppermute | solution.py:409
  64.3 10.4 %collective-permute-start.5 = (bf16[24,1792]{1,0:T(8,128)(2,1)S(1)}, bf16[24,1792]{1,0:T(8,128)(2,1)S(1)}, u32[]{:S(2)}, u32[]{:S(2)}) collective-permute-start(bf16[24,1792]{1,0:T(8,128)(2,1)S(1)} %get-tuple-element.32), channel_id=1, source_target_pairs={{0,6},{1,7},{2,4},{3,5},{4,2},{5,3},{6,0},{7,1},{8,14},{9,15},{10,... | collective-permute-start | bytes 258056 | tf_op jit(solution)/shard_map/ppermute | solution.py:409
  65.9 8.8 %collective-permute-start.6 = (bf16[24,1792]{1,0:T(8,128)(2,1)S(1)}, bf16[24,1792]{1,0:T(8,128)(2,1)S(1)}, u32[]{:S(2)}, u32[]{:S(2)}) collective-permute-start(bf16[24,1792]{1,0:T(8,128)(2,1)S(1)} %get-tuple-element.33), channel_id=1, source_target_pairs={{0,7},{1,6},{2,5},{3,4},{4,3},{5,2},{6,1},{7,0},{8,15},{9,14},{10,... | collective-permute-start | bytes 258056 | tf_op jit(solution)/shard_map/ppermute | solution.py:409
  76.8 1.6 %collective-permute-start.17 = (f32[56,8,128]{2,1,0:T(8,128)S(1)}, f32[56,8,128]{2,1,0:T(8,128)S(1)}, u32[]{:S(2)}, u32[]{:S(2)}) collective-permute-start(f32[56,8,128]{2,1,0:T(8,128)S(1)} %get-tuple-element.47), channel_id=1, source_target_pairs={{0,8},{8,0},{16,24},{24,16},{1,9},{9,1},{17,25},{25,17},{2,10},{10... | collective-permute-start | bytes 688136 | tf_op jit(solution)/shard_map/ppermute | solution.py:409
  78.4 4.2 %collective-permute-start.20 = (f32[14,8,128]{2,1,0:T(8,128)S(1)}, f32[14,8,128]{2,1,0:T(8,128)S(1)}, u32[]{:S(2)}, u32[]{:S(2)}) collective-permute-start(f32[14,8,128]{2,1,0:T(8,128)S(1)} %get-tuple-element.51), channel_id=1, source_target_pairs={{0,1},{1,0},{2,3},{3,2},{4,5},{5,4},{6,7},{7,6},{8,9},{9,8},{10,11... | collective-permute-start | bytes 172040 | tf_op jit(solution)/shard_map/ppermute | solution.py:430
  79.2 4.2 %collective-permute-start.19 = (f32[14,8,128]{2,1,0:T(8,128)S(1)}, f32[14,8,128]{2,1,0:T(8,128)S(1)}, u32[]{:S(2)}, u32[]{:S(2)}) collective-permute-start(f32[14,8,128]{2,1,0:T(8,128)S(1)} %get-tuple-element.52), channel_id=1, source_target_pairs={{0,16},{1,17},{2,18},{3,19},{4,20},{5,21},{6,22},{7,23},{8,24},{9,... | collective-permute-start | bytes 172040 | tf_op jit(solution)/shard_map/ppermute | solution.py:430
  80.7 5.1 %collective-permute-start.18 = (f32[14,8,128]{2,1,0:T(8,128)S(1)}, f32[14,8,128]{2,1,0:T(8,128)S(1)}, u32[]{:S(2)}, u32[]{:S(2)}) collective-permute-start(f32[14,8,128]{2,1,0:T(8,128)S(1)} %get-tuple-element.50), channel_id=1, source_target_pairs={{0,17},{1,16},{2,19},{3,18},{4,21},{5,20},{6,23},{7,22},{8,25},{9,... | collective-permute-start | bytes 172040 | tf_op jit(solution)/shard_map/ppermute | solution.py:430
  85.8 5.7 %collective-permute-start.23 = (f32[14,8,128]{2,1,0:T(8,128)S(1)}, f32[14,8,128]{2,1,0:T(8,128)S(1)}, u32[]{:S(2)}, u32[]{:S(2)}) collective-permute-start(f32[14,8,128]{2,1,0:T(8,128)S(1)} %fusion.1), channel_id=1, source_target_pairs={{0,2},{1,3},{2,0},{3,1},{4,6},{5,7},{6,4},{7,5},{8,10},{9,11},{10,... | collective-permute-start | bytes 172040 | tf_op jit(solution)/shard_map/ppermute | solution.py:409
  89.1 5.6 %collective-permute-start.21 = (f32[14,8,128]{2,1,0:T(8,128)S(1)}, f32[14,8,128]{2,1,0:T(8,128)S(1)}, u32[]{:S(2)}, u32[]{:S(2)}) collective-permute-start(f32[14,8,128]{2,1,0:T(8,128)S(1)} %fusion.1), channel_id=1, source_target_pairs={{0,4},{1,5},{2,6},{3,7},{4,0},{5,1},{6,2},{7,3},{8,12},{9,13},{10,... | collective-permute-start | bytes 172040 | tf_op jit(solution)/shard_map/ppermute | solution.py:409
  89.8 6.1 %collective-permute-start.22 = (f32[14,8,128]{2,1,0:T(8,128)S(1)}, f32[14,8,128]{2,1,0:T(8,128)S(1)}, u32[]{:S(2)}, u32[]{:S(2)}) collective-permute-start(f32[14,8,128]{2,1,0:T(8,128)S(1)} %fusion.1), channel_id=1, source_target_pairs={{0,6},{1,7},{2,4},{3,5},{4,2},{5,3},{6,0},{7,1},{8,14},{9,15},{10,... | collective-permute-start | bytes 172040 | tf_op jit(solution)/shard_map/ppermute | solution.py:409
  95.9 4.2 %collective-permute-start.24 = (f32[14,8,128]{2,1,0:T(8,128)S(1)}, f32[14,8,128]{2,1,0:T(8,128)S(1)}, u32[]{:S(2)}, u32[]{:S(2)}) collective-permute-start(f32[14,8,128]{2,1,0:T(8,128)S(1)} %add_add_fusion.refs_0_), channel_id=1, source_target_pairs={{0,1},{1,0},{2,3},{3,2},{4,5},{5,4},{6,7},{7,6},{8,9},{9,8},{10,11... | collective-permute-start | bytes 172040 | tf_op jit(solution)/shard_map/ppermute | solution.py:430
  96.6 4.2 %collective-permute-start.25 = (f32[14,8,128]{2,1,0:T(8,128)S(1)}, f32[14,8,128]{2,1,0:T(8,128)S(1)}, u32[]{:S(2)}, u32[]{:S(2)}) collective-permute-start(f32[14,8,128]{2,1,0:T(8,128)S(1)} %add_add_fusion.refs_0_), channel_id=1, source_target_pairs={{0,16},{1,17},{2,18},{3,19},{4,20},{5,21},{6,22},{7,23},{8,24},{9,... | collective-permute-start | bytes 172040 | tf_op jit(solution)/shard_map/ppermute | solution.py:430
  97.2 5.1 %collective-permute-start.26 = (f32[14,8,128]{2,1,0:T(8,128)S(1)}, f32[14,8,128]{2,1,0:T(8,128)S(1)}, u32[]{:S(2)}, u32[]{:S(2)}) collective-permute-start(f32[14,8,128]{2,1,0:T(8,128)S(1)} %add_add_fusion.refs_0_), channel_id=1, source_target_pairs={{0,17},{1,16},{2,19},{3,18},{4,21},{5,20},{6,23},{7,22},{8,25},{9,... | collective-permute-start | bytes 172040 | tf_op jit(solution)/shard_map/ppermute | solution.py:430
  99.4 2.9 %collective-permute-start.27 = (f32[14,8,128]{2,1,0:T(8,128)S(1)}, f32[14,8,128]{2,1,0:T(8,128)S(1)}, u32[]{:S(2)}, u32[]{:S(2)}) collective-permute-start(f32[14,8,128]{2,1,0:T(8,128)S(1)} %add_add_fusion.refs_0_), channel_id=1, source_target_pairs={{0,8},{8,0},{16,24},{24,16},{1,9},{9,1},{17,25},{25,17},{2,10},{10... | collective-permute-start | bytes 172040 | tf_op jit(solution)/shard_map/ppermute | solution.py:409
  100.1 2.2 %collective-permute-start.28 = (f32[14,8,128]{2,1,0:T(8,128)S(1)}, f32[14,8,128]{2,1,0:T(8,128)S(1)}, u32[]{:S(2)}, u32[]{:S(2)}) collective-permute-start(f32[14,8,128]{2,1,0:T(8,128)S(1)} %collective-permute-done.24.refs_1_), channel_id=1, source_target_pairs={{0,8},{8,0},{16,24},{24,16},{1,9},{9,1},{17,25},{25,17},{2,10},{10... | collective-permute-start | bytes 172040 | tf_op jit(solution)/shard_map/ppermute | solution.py:409
  100.8 1.5 %collective-permute-start.29 = (f32[14,8,128]{2,1,0:T(8,128)S(1)}, f32[14,8,128]{2,1,0:T(8,128)S(1)}, u32[]{:S(2)}, u32[]{:S(2)}) collective-permute-start(f32[14,8,128]{2,1,0:T(8,128)S(1)} %collective-permute-done.25.refs_2_), channel_id=1, source_target_pairs={{0,8},{8,0},{16,24},{24,16},{1,9},{9,1},{17,25},{25,17},{2,10},{10... | collective-permute-start | bytes 172040 | tf_op jit(solution)/shard_map/ppermute | solution.py:409
  102.3 1.2 %collective-permute-start.30 = (f32[14,8,128]{2,1,0:T(8,128)S(1)}, f32[14,8,128]{2,1,0:T(8,128)S(1)}, u32[]{:S(2)}, u32[]{:S(2)}) collective-permute-start(f32[14,8,128]{2,1,0:T(8,128)S(1)} %collective-permute-done.26.refs_3_), channel_id=1, source_target_pairs={{0,8},{8,0},{16,24},{24,16},{1,9},{9,1},{17,25},{25,17},{2,10},{10... | collective-permute-start | bytes 172040 | tf_op jit(solution)/shard_map/ppermute | solution.py:409
  (2 other events, 3.6 us)
